TPU v7x, 256 devices: a whole 4x4x8 slice. The times are simulated.
256 devices in a mesh: south: 4 (over x), east: 4 (over y), down: 16 (over z, core).
Axes of the slice: x: 4, y: 4, z: 8, core: 2. Of those that a mesh axis runs over, the one named last changes fastest.
Arguments:
- field_values: float32 [32, 384, 128, 128], P('south', 'east', 'down'), may hold values from 0.2 to 1.8
- flow_y: float32 [32, 384, 128, 128], P('south', 'east', 'down'), may hold values from -0.3 to 0.3
- flow_x: float32 [32, 384, 128, 128], P('south', 'east', 'down'), may hold values from -0.3 to 0.3
- flow_z: float32 [32, 384, 128, 128], P('south', 'east', 'down'), may hold values from -0.3 to 0.3
Outputs:
- potential: float32 [32, 384, 128, 128], P('south', 'east', 'down')
- field_values_end: float32 [32, 384, 128, 128], P('south', 'east', 'down')
All inputs are finite; a program needn't handle non-finite values.
Results may differ from a plain program's by a relative error of at most 0.00002.
Values sent between devices are 32-bit elements; how exact they have to be, the bound alone decides.
No kernel may reach another device: no remote copies, remote signals or barrier semaphores. Data moves between devices by JAX's collectives and lax.ppermute only.
A program may use at most 128 MiB of HBM per device.

v0:
```python
import jax
import jax.numpy as jnp
from jax import lax
from jax.sharding import Mesh
from jax.sharding import PartitionSpec as P

STEPS = 4
DOWN = ("down_0", "down_1")


def with_halo(array, sides, width):
    edges = {}
    for axis, dim in sides:
        size, length = (lax.axis_size(axis), array.shape[dim])
        up = [(i, (i + 1) % size) for i in range(size)]
        last = lax.slice_in_dim(array, length - width, length, axis=dim)
        initial = lax.slice_in_dim(array, 0, width, axis=dim)
        edges[dim] = (
            lax.ppermute(last, axis, up),
            lax.ppermute(initial, axis, [(b, a) for a, b in up]),
        )
    done = []
    for _, dim in sides:
        low, high = edges[dim]
        around = [(width, width) if d in done else (0, 0) for d in range(array.ndim)]
        array = jnp.concatenate([jnp.pad(low, around), array, jnp.pad(high, around)], axis=dim)
        done.append(dim)
    return array


def filled_with(array, identity):
    return jnp.zeros_like(array) + jnp.asarray(identity, array.dtype)


def prefix_by_axis(array, axes, combine, identity):
    before = start = filled_with(array, identity)
    so_far = array
    for axis in reversed(axes):
        length, here = (lax.axis_size(axis), lax.axis_index(axis))
        pieces = lax.all_gather(so_far, axis)
        inside, so_far = (start, start)
        for k in range(length):
            passed = k < here
            so_far = combine(so_far, pieces[k])
            inside = jnp.where(passed, so_far, inside)
        before = combine(inside, before)
    return before


def without_rim(values, dims):
    for dim in dims:
        values = lax.slice_in_dim(values, 1, values.shape[dim] - 1, axis=dim)
    return values


def shifted_cells(values, dim, start, dims):
    others = [other for other in dims if other != dim]
    values = without_rim(values, others)
    return lax.slice_in_dim(values, start, start + values.shape[dim] - 2, axis=dim)


def march_step(padded, flow_y, flow_x, flow_z):
    middle = without_rim(padded, (0, 1, 2))
    lower = [shifted_cells(padded, dim, 0, (0, 1, 2)) for dim in (0, 1, 2)]
    upper = [shifted_cells(padded, dim, 2, (0, 1, 2)) for dim in (0, 1, 2)]
    slopes = [above - below for above, below in zip(upper, lower)]
    smooth_rate = 0.05
    spread = lower[0] + upper[0] + lower[1] + upper[1] + lower[2] + upper[2] - 6.0 * middle
    return (
        middle - flow_y * slopes[0] - flow_x * slopes[1] - flow_z * slopes[2] + smooth_rate * spread
    )


def local(field_values, flow_y, flow_x, flow_z):
    for step in range(STEPS):
        padded = with_halo(field_values, (("south", 0), ("east", 1), (DOWN, 2)), 1)
        field_values = march_step(padded, flow_y, flow_x, flow_z)
    here = jnp.cumsum(field_values, axis=2)
    total = lax.slice_in_dim(here, here.shape[2] - 1, here.shape[2], axis=2)

    def add_pair(earlier_total, later_total):
        return earlier_total + later_total

    below = prefix_by_axis(total, DOWN, add_pair, jnp.zeros_like(total))
    potential = (here + below) / (field_values.shape[2] * lax.axis_size(DOWN))
    return (potential, field_values)


def solution(mesh):
    finer = Mesh(
        mesh.devices.reshape(mesh.shape["south"], mesh.shape["east"], 8, 2),
        ("south", "east", "down_0", "down_1"),
    )
    in_specs = (
        P("south", "east", DOWN, None),
        P("south", "east", DOWN, None),
        P("south", "east", DOWN, None),
        P("south", "east", DOWN, None),
    )
    out_specs = (P("south", "east", DOWN, None), P("south", "east", DOWN, None))
    return jax.shard_map(local, mesh=finer, in_specs=in_specs, out_specs=out_specs, check_vma=False)
```

profile of v0, /device:TPU:1, one launch (start us, length us, event | category | flops | bytes accessed | tf_op | source)
XLA Modules:
  0.0 166.6 jit_solution(3304423742802304191)
XLA Ops:
  7.2 2.6 %copy.20 = f32[8,96,8,128]{3,1,2,0:T(8,128)S(1)} copy(f32[8,96,8,128]{3,2,1,0:T(8,128)} %param.4) | data formatting | bytes 6291456 | tf_op args[0]
  13.4 2.9 %collective-permute-start.2 = (f32[8,1,8,128]{3,1,2,0:T(1,128)S(1)}, f32[8,1,8,128]{3,1,2,0:T(1,128)S(1)}, u32[]{:S(2)}, u32[]{:S(2)}) collective-permute-start(f32[8,1,8,128]{3,1,2,0:T(1,128)S(1)} %bitcast.44), channel_id=1, source_target_pairs={{16,0},{32,16},{48,32},{0,48},{17,1},{33,17},{49,33},{1,49},{18,2}... | collective-permute-start | bytes 98312 | tf_op jit(solution)/shard_map/ppermute | solution.py:20
  16.3 2.2 %collective-permute-start.4 = (f32[8,96,1,128]{3,1,2,0:T(8,128)S(1)}, f32[8,96,1,128]{3,1,2,0:T(8,128)S(1)}, u32[]{:S(2)}, u32[]{:S(2)}) collective-permute-start(f32[8,96,1,128]{3,1,2,0:T(8,128)S(1)} %get-tuple-element.23), channel_id=1, source_target_pairs={{1,0},{2,1},{3,2},{4,3},{5,4},{6,5},{7,6},{8,7},{9,8},{10,9},{11,1... | collective-permute-start | bytes 1179656 | tf_op jit(solution)/shard_map/ppermute | solution.py:20
  18.6 2.3 %collective-permute-start.5 = (f32[8,96,1,128]{3,1,2,0:T(8,128)S(1)}, f32[8,96,1,128]{3,1,2,0:T(8,128)S(1)}, u32[]{:S(2)}, u32[]{:S(2)}) collective-permute-start(f32[8,96,1,128]{3,1,2,0:T(8,128)S(1)} %get-tuple-element.22), channel_id=1, source_target_pairs={{0,1},{1,2},{2,3},{3,4},{4,5},{5,6},{6,7},{7,8},{8,9},{9,10},{10,1... | collective-permute-start | bytes 1179656 | tf_op jit(solution)/shard_map/ppermute | solution.py:19
  21.7 3.2 %collective-permute-done.4 = f32[8,96,1,128]{3,1,2,0:T(8,128)S(1)} collective-permute-done((f32[8,96,1,128]{3,1,2,0:T(8,128)S(1)}, f32[8,96,1,128]{3,1,2,0:T(8,128)S(1)}, u32[]{:S(2)}, u32[]{:S(2)}) %collective-permute-start.4) | collective-permute-done | bytes 393248 | tf_op jit(solution)/shard_map/ppermute | solution.py:20
  25.6 7.9 %multiply_add_fusion.3 = f32[8,96,8,128]{3,1,2,0:T(8,128)S(1)} fusion(f32[8,96,8,128]{3,1,2,0:T(8,128)S(1)} %copy.20, f32[8,96,1,128]{3,1,2,0:T(8,128)S(1)} %collective-permute-done.4, f32[10,1,8,128]{3,1,2,0:T(1,128)S(1)} %pad.50, f32[10,96,8,128]{3,1,2,0:T(8,128)S(1)} %constant_dynamic-update-slice_fusion, f32[10,1,8,128]{3,1,2,0:T(1,128)S(1)} %pad.51, ...), kind=kLoop, calls=%fused_computation.78 | loop fusion | flops 26738688 | bytes 21315584 | tf_op jit(solution)/shard_map/add | solution.py:70
  33.7 5.2 %collective-permute-start.10 = (f32[8,96,1,128]{3,1,2,0:T(8,128)S(1)}, f32[8,96,1,128]{3,1,2,0:T(8,128)S(1)}, u32[]{:S(2)}, u32[]{:S(2)}) collective-permute-start(f32[8,96,1,128]{3,1,2,0:T(8,128)S(1)} %get-tuple-element.17), channel_id=1, source_target_pairs={{1,0},{2,1},{3,2},{4,3},{5,4},{6,5},{7,6},{8,7},{9,8},{10,9},{11,1... | collective-permute-start | bytes 1179656 | tf_op jit(solution)/shard_map/ppermute | solution.py:20
  40.4 2.8 %collective-permute-start.8 = (f32[8,1,8,128]{3,1,2,0:T(1,128)S(1)}, f32[8,1,8,128]{3,1,2,0:T(1,128)S(1)}, u32[]{:S(2)}, u32[]{:S(2)}) collective-permute-start(f32[8,1,8,128]{3,1,2,0:T(1,128)S(1)} %get-tuple-element.19), channel_id=1, source_target_pairs={{16,0},{32,16},{48,32},{0,48},{17,1},{33,17},{49,33},{1,49},{18,2}... | collective-permute-start | bytes 98312 | tf_op jit(solution)/shard_map/ppermute | solution.py:20
  44.2 4.8 %collective-permute-done.9 = f32[8,1,8,128]{3,1,2,0:T(1,128)S(1)} collective-permute-done((f32[8,1,8,128]{3,1,2,0:T(1,128)S(1)}, f32[8,1,8,128]{3,1,2,0:T(1,128)S(1)}, u32[]{:S(2)}, u32[]{:S(2)}) %collective-permute-start.9) | collective-permute-done | bytes 32800 | tf_op jit(solution)/shard_map/ppermute | solution.py:19
  49.0 2.2 %collective-permute-done.7 = f32[1,96,8,128]{3,1,2,0:T(8,128)S(1)} collective-permute-done((f32[1,96,8,128]{3,1,2,0:T(8,128)S(1)}, f32[1,96,8,128]{3,1,2,0:T(8,128)S(1)}, u32[]{:S(2)}, u32[]{:S(2)}) %collective-permute-start.7) | collective-permute-done | bytes 393248 | tf_op jit(solution)/shard_map/ppermute | solution.py:19
  51.2 7.5 %multiply_add_fusion.2 = f32[8,96,8,128]{3,1,2,0:T(8,128)S(1)} fusion(f32[8,96,8,128]{3,1,2,0:T(8,128)S(1)} %multiply_add_fusion.3, f32[8,96,1,128]{3,1,2,0:T(8,128)S(1)} %collective-permute-done.10, f32[10,1,8,128]{3,1,2,0:T(1,128)S(1)} %pad.54, f32[1,96,8,128]{3,1,2,0:T(8,128)S(1)} %collective-permute-done.6, ...), kind=kLoop, calls=%fused_computation.77 | loop fusion | flops 33030144 | bytes 17383424 | tf_op jit(solution)/shard_map/add | solution.py:70
  60.5 2.2 %collective-permute-start.16 = (f32[8,96,1,128]{3,1,2,0:T(8,128)S(1)}, f32[8,96,1,128]{3,1,2,0:T(8,128)S(1)}, u32[]{:S(2)}, u32[]{:S(2)}) collective-permute-start(f32[8,96,1,128]{3,1,2,0:T(8,128)S(1)} %get-tuple-element.11), channel_id=1, source_target_pairs={{1,0},{2,1},{3,2},{4,3},{5,4},{6,5},{7,6},{8,7},{9,8},{10,9},{11,1... | collective-permute-start | bytes 1179656 | tf_op jit(solution)/shard_map/ppermute | solution.py:20
  62.8 2.8 %collective-permute-start.14 = (f32[8,1,8,128]{3,1,2,0:T(1,128)S(1)}, f32[8,1,8,128]{3,1,2,0:T(1,128)S(1)}, u32[]{:S(2)}, u32[]{:S(2)}) collective-permute-start(f32[8,1,8,128]{3,1,2,0:T(1,128)S(1)} %get-tuple-element.13), channel_id=1, source_target_pairs={{16,0},{32,16},{48,32},{0,48},{17,1},{33,17},{49,33},{1,49},{18,2}... | collective-permute-start | bytes 98312 | tf_op jit(solution)/shard_map/ppermute | solution.py:20
  66.6 4.8 %collective-permute-done.15 = f32[8,1,8,128]{3,1,2,0:T(1,128)S(1)} collective-permute-done((f32[8,1,8,128]{3,1,2,0:T(1,128)S(1)}, f32[8,1,8,128]{3,1,2,0:T(1,128)S(1)}, u32[]{:S(2)}, u32[]{:S(2)}) %collective-permute-start.15) | collective-permute-done | bytes 32800 | tf_op jit(solution)/shard_map/ppermute | solution.py:19
  71.5 7.5 %multiply_add_fusion.1 = f32[8,96,8,128]{3,1,2,0:T(8,128)S(1)} fusion(f32[8,96,8,128]{3,1,2,0:T(8,128)S(1)} %multiply_add_fusion.2, f32[8,96,1,128]{3,1,2,0:T(8,128)S(1)} %collective-permute-done.16, f32[10,1,8,128]{3,1,2,0:T(1,128)S(1)} %pad.58, f32[1,96,8,128]{3,1,2,0:T(8,128)S(1)} %collective-permute-done.12, ...), kind=kLoop, calls=%fused_computation.76 | loop fusion | flops 33030144 | bytes 17383424 | tf_op jit(solution)/shard_map/add | solution.py:70
  80.7 3.4 %collective-permute-start.22 = (f32[8,96,1,128]{3,1,2,0:T(8,128)S(1)}, f32[8,96,1,128]{3,1,2,0:T(8,128)S(1)}, u32[]{:S(2)}, u32[]{:S(2)}) collective-permute-start(f32[8,96,1,128]{3,1,2,0:T(8,128)S(1)} %get-tuple-element.5), channel_id=1, source_target_pairs={{1,0},{2,1},{3,2},{4,3},{5,4},{6,5},{7,6},{8,7},{9,8},{10,9},{11,1... | collective-permute-start | bytes 1179656 | tf_op jit(solution)/shard_map/ppermute | solution.py:20
  87.4 4.5 %collective-permute-done.21 = f32[8,1,8,128]{3,1,2,0:T(1,128)S(1)} collective-permute-done((f32[8,1,8,128]{3,1,2,0:T(1,128)S(1)}, f32[8,1,8,128]{3,1,2,0:T(1,128)S(1)}, u32[]{:S(2)}, u32[]{:S(2)}) %collective-permute-start.21) | collective-permute-done | bytes 32800 | tf_op jit(solution)/shard_map/ppermute | solution.py:19
  92.0 7.5 %multiply_add_fusion = f32[8,96,8,128]{3,1,2,0:T(8,128)S(1)} fusion(f32[8,96,8,128]{3,1,2,0:T(8,128)S(1)} %multiply_add_fusion.1, f32[8,96,1,128]{3,1,2,0:T(8,128)S(1)} %collective-permute-done.22, f32[10,1,8,128]{3,1,2,0:T(1,128)S(1)} %pad.62, f32[1,96,8,128]{3,1,2,0:T(8,128)S(1)} %collective-permute-done.18, ...), kind=kLoop, calls=%fused_computation.75 | loop fusion | flops 33030144 | bytes 17383424 | tf_op jit(solution)/shard_map/add | solution.py:70
  99.5 3.3 %fusion.27 = f32[8,96,8,128]{3,1,2,0:T(8,128)S(1)} fusion(f32[8,96,8,128]{3,1,2,0:T(8,128)S(1)} %multiply_add_fusion), kind=kOutput, calls=%fused_computation.112 | output fusion | flops 5505024 | bytes 6291456 | tf_op jit(solution)/shard_map/jit(cumsum)/reduce_window_sum | solution.py:78
  104.5 4.9 %all-gather = f32[16,96,1,128]{3,1,2,0:T(8,128)} all-gather(f32[8,96,1,128]{3,1,2,0:T(8,128)S(1)} %slice.424), channel_id=2, replica_groups=mesh['south'=4,'east'=4,'down_0'=8,'down_1'=2] {'down_1'}, dimensions={0}, use_global_device_ids=true | all-gather | bytes 1179648 | tf_op jit(solution)/shard_map/all_gather | solution.py:40
  111.4 3.4 %copy.49 = f32[8,96,8,128]{3,2,1,0:T(8,128)} copy(f32[8,96,8,128]{3,1,2,0:T(8,128)S(1)} %multiply_add_fusion) | data formatting | bytes 6291456
  114.9 38.6 %all-gather.4.cloned.1.call-done = f32[64,96,1,128]{3,1,2,0:T(8,128)} async-done(((f32[8,96,1,128]{3,1,2,0:T(8,128)}), f32[64,96,1,128]{3,1,2,0:T(8,128)}) %all-gather.4.cloned.1.call-update) | async-done | bytes 3145744 | tf_op jit(solution)/shard_map/all_gather | solution.py:40
  153.4 2.5 %fusion.11 = f32[8,96,128]{2,1,0:T(8,128)S(1)} fusion(f32[64,96,1,128]{3,1,0,2:T(8,128)} %bitcast.42, f32[16,96,1,128]{3,1,2,0:T(8,128)} %all-gather, pred[]{:T(512)S(6)} %gt.33, pred[]{:T(512)S(6)} %gt.34, pred[]{:T(512)S(6)} %gt.35, pred[]{:T(512)S(6)} %gt.36, pred[]{:T(512)S(6)} %gt.37, pred[]{:T(512)S(6)} %gt.38, pred[]{:T(512)S(6)} %gt.39, pred[]{:T(512)S(6)} %gt.30, ...), kind=kLoop, calls=%fused_computation.83 | loop fusion | flops 1867776 | bytes 4325386 | tf_op jit(solution)/shard_map/add | solution.py:82
  156.3 3.4 %copy.48 = f32[8,96,8,128]{3,2,1,0:T(8,128)} copy(f32[8,96,8,128]{3,1,2,0:T(8,128)S(1)} %add_multiply_fusion) | data formatting | bytes 6291456
  (75 shorter events, 19.8 us)
Async XLA Ops:
  7.2 146.3 %all-gather.4.cloned.1.call-start = ((), (), s32[]{:S(2)}) async-start(), calls=%async_computation | async-start | bytes 3538944 | tf_op jit(solution)/shard_map/all_gather | solution.py:40
  9.9 11.1 %collective-permute-start.1 = (f32[1,96,8,128]{3,1,2,0:T(8,128)S(1)}, f32[1,96,8,128]{3,1,2,0:T(8,128)S(1)}, u32[]{:S(2)}, u32[]{:S(2)}) collective-permute-start(f32[1,96,8,128]{3,1,2,0:T(8,128)S(1)} %get-tuple-element.27), channel_id=1, source_target_pairs={{0,64},{64,128},{128,192},{192,0},{1,65},{65,129},{129,193},{193,1... | collective-permute-start | bytes 1179656 | tf_op jit(solution)/shard_map/ppermute | solution.py:19
  12.0 9.6 %collective-permute-start = (f32[1,96,8,128]{3,1,2,0:T(8,128)S(1)}, f32[1,96,8,128]{3,1,2,0:T(8,128)S(1)}, u32[]{:S(2)}, u32[]{:S(2)}) collective-permute-start(f32[1,96,8,128]{3,1,2,0:T(8,128)S(1)} %get-tuple-element.26), channel_id=1, source_target_pairs={{64,0},{128,64},{192,128},{0,192},{65,1},{129,65},{193,129},{1,193... | collective-permute-start | bytes 1179656 | tf_op jit(solution)/shard_map/ppermute | solution.py:20
  13.4 5.2 %collective-permute-start.2 = (f32[8,1,8,128]{3,1,2,0:T(1,128)S(1)}, f32[8,1,8,128]{3,1,2,0:T(1,128)S(1)}, u32[]{:S(2)}, u32[]{:S(2)}) collective-permute-start(f32[8,1,8,128]{3,1,2,0:T(1,128)S(1)} %bitcast.44), channel_id=1, source_target_pairs={{16,0},{32,16},{48,32},{0,48},{17,1},{33,17},{49,33},{1,49},{18,2}... | collective-permute-start | bytes 98312 | tf_op jit(solution)/shard_map/ppermute | solution.py:20
  16.3 4.7 %collective-permute-start.3 = (f32[8,1,8,128]{3,1,2,0:T(1,128)S(1)}, f32[8,1,8,128]{3,1,2,0:T(1,128)S(1)}, u32[]{:S(2)}, u32[]{:S(2)}) collective-permute-start(f32[8,1,8,128]{3,1,2,0:T(1,128)S(1)} %bitcast.43), channel_id=1, source_target_pairs={{0,16},{16,32},{32,48},{48,0},{1,17},{17,33},{33,49},{49,1},{2,18}... | collective-permute-start | bytes 98312 | tf_op jit(solution)/shard_map/ppermute | solution.py:19
  16.3 8.5 %collective-permute-start.4 = (f32[8,96,1,128]{3,1,2,0:T(8,128)S(1)}, f32[8,96,1,128]{3,1,2,0:T(8,128)S(1)}, u32[]{:S(2)}, u32[]{:S(2)}) collective-permute-start(f32[8,96,1,128]{3,1,2,0:T(8,128)S(1)} %get-tuple-element.23), channel_id=1, source_target_pairs={{1,0},{2,1},{3,2},{4,3},{5,4},{6,5},{7,6},{8,7},{9,8},{10,9},{11,1... | collective-permute-start | bytes 1179656 | tf_op jit(solution)/shard_map/ppermute | solution.py:20
  18.6 7.0 %collective-permute-start.5 = (f32[8,96,1,128]{3,1,2,0:T(8,128)S(1)}, f32[8,96,1,128]{3,1,2,0:T(8,128)S(1)}, u32[]{:S(2)}, u32[]{:S(2)}) collective-permute-start(f32[8,96,1,128]{3,1,2,0:T(8,128)S(1)} %get-tuple-element.22), channel_id=1, source_target_pairs={{0,1},{1,2},{2,3},{3,4},{4,5},{5,6},{6,7},{7,8},{8,9},{9,10},{10,1... | collective-permute-start | bytes 1179656 | tf_op jit(solution)/shard_map/ppermute | solution.py:19
  33.7 15.3 %collective-permute-start.10 = (f32[8,96,1,128]{3,1,2,0:T(8,128)S(1)}, f32[8,96,1,128]{3,1,2,0:T(8,128)S(1)}, u32[]{:S(2)}, u32[]{:S(2)}) collective-permute-start(f32[8,96,1,128]{3,1,2,0:T(8,128)S(1)} %get-tuple-element.17), channel_id=1, source_target_pairs={{1,0},{2,1},{3,2},{4,3},{5,4},{6,5},{7,6},{8,7},{9,8},{10,9},{11,1... | collective-permute-start | bytes 1179656 | tf_op jit(solution)/shard_map/ppermute | solution.py:20
  38.8 10.2 %collective-permute-start.11 = (f32[8,96,1,128]{3,1,2,0:T(8,128)S(1)}, f32[8,96,1,128]{3,1,2,0:T(8,128)S(1)}, u32[]{:S(2)}, u32[]{:S(2)}) collective-permute-start(f32[8,96,1,128]{3,1,2,0:T(8,128)S(1)} %get-tuple-element.16), channel_id=1, source_target_pairs={{0,1},{1,2},{2,3},{3,4},{4,5},{5,6},{6,7},{7,8},{8,9},{9,10},{10,1... | collective-permute-start | bytes 1179656 | tf_op jit(solution)/shard_map/ppermute | solution.py:19
  38.8 10.2 %collective-permute-start.6 = (f32[1,96,8,128]{3,1,2,0:T(8,128)S(1)}, f32[1,96,8,128]{3,1,2,0:T(8,128)S(1)}, u32[]{:S(2)}, u32[]{:S(2)}) collective-permute-start(f32[1,96,8,128]{3,1,2,0:T(8,128)S(1)} %get-tuple-element.21), channel_id=1, source_target_pairs={{64,0},{128,64},{192,128},{0,192},{65,1},{129,65},{193,129},{1,193... | collective-permute-start | bytes 1179656 | tf_op jit(solution)/shard_map/ppermute | solution.py:20
  40.1 11.1 %collective-permute-start.7 = (f32[1,96,8,128]{3,1,2,0:T(8,128)S(1)}, f32[1,96,8,128]{3,1,2,0:T(8,128)S(1)}, u32[]{:S(2)}, u32[]{:S(2)}) collective-permute-start(f32[1,96,8,128]{3,1,2,0:T(8,128)S(1)} %get-tuple-element.20), channel_id=1, source_target_pairs={{0,64},{64,128},{128,192},{192,0},{1,65},{65,129},{129,193},{193,1... | collective-permute-start | bytes 1179656 | tf_op jit(solution)/shard_map/ppermute | solution.py:19
  40.4 3.8 %collective-permute-start.8 = (f32[8,1,8,128]{3,1,2,0:T(1,128)S(1)}, f32[8,1,8,128]{3,1,2,0:T(1,128)S(1)}, u32[]{:S(2)}, u32[]{:S(2)}) collective-permute-start(f32[8,1,8,128]{3,1,2,0:T(1,128)S(1)} %get-tuple-element.19), channel_id=1, source_target_pairs={{16,0},{32,16},{48,32},{0,48},{17,1},{33,17},{49,33},{1,49},{18,2}... | collective-permute-start | bytes 98312 | tf_op jit(solution)/shard_map/ppermute | solution.py:20
  44.1 4.8 %collective-permute-start.9 = (f32[8,1,8,128]{3,1,2,0:T(1,128)S(1)}, f32[8,1,8,128]{3,1,2,0:T(1,128)S(1)}, u32[]{:S(2)}, u32[]{:S(2)}) collective-permute-start(f32[8,1,8,128]{3,1,2,0:T(1,128)S(1)} %get-tuple-element.18), channel_id=1, source_target_pairs={{0,16},{16,32},{32,48},{48,0},{1,17},{17,33},{33,49},{49,1},{2,18}... | collective-permute-start | bytes 98312 | tf_op jit(solution)/shard_map/ppermute | solution.py:19
  58.8 12.6 %collective-permute-start.12 = (f32[1,96,8,128]{3,1,2,0:T(8,128)S(1)}, f32[1,96,8,128]{3,1,2,0:T(8,128)S(1)}, u32[]{:S(2)}, u32[]{:S(2)}) collective-permute-start(f32[1,96,8,128]{3,1,2,0:T(8,128)S(1)} %get-tuple-element.15), channel_id=1, source_target_pairs={{64,0},{128,64},{192,128},{0,192},{65,1},{129,65},{193,129},{1,193... | collective-permute-start | bytes 1179656 | tf_op jit(solution)/shard_map/ppermute | solution.py:20
  59.4 12.0 %collective-permute-start.13 = (f32[1,96,8,128]{3,1,2,0:T(8,128)S(1)}, f32[1,96,8,128]{3,1,2,0:T(8,128)S(1)}, u32[]{:S(2)}, u32[]{:S(2)}) collective-permute-start(f32[1,96,8,128]{3,1,2,0:T(8,128)S(1)} %get-tuple-element.14), channel_id=1, source_target_pairs={{0,64},{64,128},{128,192},{192,0},{1,65},{65,129},{129,193},{193,1... | collective-permute-start | bytes 1179656 | tf_op jit(solution)/shard_map/ppermute | solution.py:19
  60.5 10.9 %collective-permute-start.16 = (f32[8,96,1,128]{3,1,2,0:T(8,128)S(1)}, f32[8,96,1,128]{3,1,2,0:T(8,128)S(1)}, u32[]{:S(2)}, u32[]{:S(2)}) collective-permute-start(f32[8,96,1,128]{3,1,2,0:T(8,128)S(1)} %get-tuple-element.11), channel_id=1, source_target_pairs={{1,0},{2,1},{3,2},{4,3},{5,4},{6,5},{7,6},{8,7},{9,8},{10,9},{11,1... | collective-permute-start | bytes 1179656 | tf_op jit(solution)/shard_map/ppermute | solution.py:20
  62.8 8.7 %collective-permute-start.17 = (f32[8,96,1,128]{3,1,2,0:T(8,128)S(1)}, f32[8,96,1,128]{3,1,2,0:T(8,128)S(1)}, u32[]{:S(2)}, u32[]{:S(2)}) collective-permute-start(f32[8,96,1,128]{3,1,2,0:T(8,128)S(1)} %get-tuple-element.10), channel_id=1, source_target_pairs={{0,1},{1,2},{2,3},{3,4},{4,5},{5,6},{6,7},{7,8},{8,9},{9,10},{10,1... | collective-permute-start | bytes 1179656 | tf_op jit(solution)/shard_map/ppermute | solution.py:19
  62.8 3.8 %collective-permute-start.14 = (f32[8,1,8,128]{3,1,2,0:T(1,128)S(1)}, f32[8,1,8,128]{3,1,2,0:T(1,128)S(1)}, u32[]{:S(2)}, u32[]{:S(2)}) collective-permute-start(f32[8,1,8,128]{3,1,2,0:T(1,128)S(1)} %get-tuple-element.13), channel_id=1, source_target_pairs={{16,0},{32,16},{48,32},{0,48},{17,1},{33,17},{49,33},{1,49},{18,2}... | collective-permute-start | bytes 98312 | tf_op jit(solution)/shard_map/ppermute | solution.py:20
  66.6 4.8 %collective-permute-start.15 = (f32[8,1,8,128]{3,1,2,0:T(1,128)S(1)}, f32[8,1,8,128]{3,1,2,0:T(1,128)S(1)}, u32[]{:S(2)}, u32[]{:S(2)}) collective-permute-start(f32[8,1,8,128]{3,1,2,0:T(1,128)S(1)} %get-tuple-element.12), channel_id=1, source_target_pairs={{0,16},{16,32},{32,48},{48,0},{1,17},{17,33},{33,49},{49,1},{2,18}... | collective-permute-start | bytes 98312 | tf_op jit(solution)/shard_map/ppermute | solution.py:19
  79.2 12.8 %collective-permute-start.18 = (f32[1,96,8,128]{3,1,2,0:T(8,128)S(1)}, f32[1,96,8,128]{3,1,2,0:T(8,128)S(1)}, u32[]{:S(2)}, u32[]{:S(2)}) collective-permute-start(f32[1,96,8,128]{3,1,2,0:T(8,128)S(1)} %get-tuple-element.9), channel_id=1, source_target_pairs={{64,0},{128,64},{192,128},{0,192},{65,1},{129,65},{193,129},{1,193... | collective-permute-start | bytes 1179656 | tf_op jit(solution)/shard_map/ppermute | solution.py:20
  80.7 11.2 %collective-permute-start.19 = (f32[1,96,8,128]{3,1,2,0:T(8,128)S(1)}, f32[1,96,8,128]{3,1,2,0:T(8,128)S(1)}, u32[]{:S(2)}, u32[]{:S(2)}) collective-permute-start(f32[1,96,8,128]{3,1,2,0:T(8,128)S(1)} %get-tuple-element.8), channel_id=1, source_target_pairs={{0,64},{64,128},{128,192},{192,0},{1,65},{65,129},{129,193},{193,1... | collective-permute-start | bytes 1179656 | tf_op jit(solution)/shard_map/ppermute | solution.py:19
  80.7 11.2 %collective-permute-start.22 = (f32[8,96,1,128]{3,1,2,0:T(8,128)S(1)}, f32[8,96,1,128]{3,1,2,0:T(8,128)S(1)}, u32[]{:S(2)}, u32[]{:S(2)}) collective-permute-start(f32[8,96,1,128]{3,1,2,0:T(8,128)S(1)} %get-tuple-element.5), channel_id=1, source_target_pairs={{1,0},{2,1},{3,2},{4,3},{5,4},{6,5},{7,6},{8,7},{9,8},{10,9},{11,1... | collective-permute-start | bytes 1179656 | tf_op jit(solution)/shard_map/ppermute | solution.py:20
  84.2 7.8 %collective-permute-start.23 = (f32[8,96,1,128]{3,1,2,0:T(8,128)S(1)}, f32[8,96,1,128]{3,1,2,0:T(8,128)S(1)}, u32[]{:S(2)}, u32[]{:S(2)}) collective-permute-start(f32[8,96,1,128]{3,1,2,0:T(8,128)S(1)} %get-tuple-element.4), channel_id=1, source_target_pairs={{0,1},{1,2},{2,3},{3,4},{4,5},{5,6},{6,7},{7,8},{8,9},{9,10},{10,1... | collective-permute-start | bytes 1179656 | tf_op jit(solution)/shard_map/ppermute | solution.py:19
  87.4 4.6 %collective-permute-start.21 = (f32[8,1,8,128]{3,1,2,0:T(1,128)S(1)}, f32[8,1,8,128]{3,1,2,0:T(1,128)S(1)}, u32[]{:S(2)}, u32[]{:S(2)}) collective-permute-start(f32[8,1,8,128]{3,1,2,0:T(1,128)S(1)} %get-tuple-element.6), channel_id=1, source_target_pairs={{0,16},{16,32},{32,48},{48,0},{1,17},{17,33},{33,49},{49,1},{2,18}... | collective-permute-start | bytes 98312 | tf_op jit(solution)/shard_map/ppermute | solution.py:19
  (7 other events, 70.6 us)
Sparse Core Ops, SparseCore 0:
  111.5 41.8 all-gather.3
where the time goes:
time: 167 us
  waiting for transfers between devices  62.3 us (37%)
  other arithmetic  38.5 us (23%)
  starting transfers between devices  33.9 us (20%)
  between operations  14.4 us (9%)
  local copies, waits for them, and re-layouts  12.6 us (8%)
  blocking collectives  4.94 us (3%)
    all_gather x1, waiting for transfers between devices, prefix_by_axis(): pieces = lax.all_gather(so_far, axis)  38.6 us
    add x4, other arithmetic, march_step(): middle - flow_y * slopes[0] - flow_x * slopes[1] - flow_z * slopes[2]  30.5 us
    ppermute x12, starting transfers between devices, with_halo(): lax.ppermute(initial, axis, [(b, a) for a, b in up])  28.1 us
    ppermute x12, waiting for transfers between devices, with_halo(): lax.ppermute(last, axis, up)  17.1 us
    unnamed x17, local copies, waits for them, and re-layouts  11.8 us
    ppermute x12, waiting for transfers between devices, with_halo(): lax.ppermute(initial, axis, [(b, a) for a, b in up])  6.56 us
    ppermute x12, starting transfers between devices, with_halo(): lax.ppermute(last, axis, up)  5.75 us
    all_gather x1, blocking collectives, prefix_by_axis(): pieces = lax.all_gather(so_far, axis)  4.94 us
  transfers between devices with their start and end apart: 25, of which 10 were waited for; matrix products, arithmetic and copies ran while one was open for 3% of the time, Pallas kernels for 0%

commit v1 on v0

v1 whole, which is shorter than its diff:
```python
import functools

import jax
import jax.numpy as jnp
from jax import lax
from jax.experimental import pallas as pl
from jax.experimental.pallas import tpu as pltpu
from jax.sharding import Mesh
from jax.sharding import PartitionSpec as P

STEPS = 4
RATE = 0.05
BLOCK = 8
VMEM = 5 << 20


DOWN = ("chip", "core")
IN_VMEM = pl.BlockSpec(memory_space=pltpu.VMEM)
IN_HBM = pl.BlockSpec(memory_space=pltpu.HBM)


def shape(*dims):
    return jax.ShapeDtypeStruct(dims, jnp.float32)


def call(kernel, outs, *args, flops=1 << 21, in_specs=None, out_specs=None, scratch=(), alias=None):
    return pl.pallas_call(
        kernel,
        out_shape=outs,
        in_specs=in_specs or [IN_VMEM] * len(args),
        out_specs=out_specs or [IN_VMEM] * len(outs),
        scratch_shapes=scratch,
        input_output_aliases=alias or {},
        compiler_params=pltpu.CompilerParams(vmem_limit_bytes=VMEM),
        cost_estimate=pl.CostEstimate(flops=flops, bytes_accessed=0, transcendentals=0),
    )(*args)


def march_row(row, cells, here, above, below, put, downs, flows, sides=None):
    zlo, zhi = downs
    fy, fx, fz = flows
    sublane = lax.broadcasted_iota(jnp.int32, (8, 128), 0)

    def cell(x, left, mid, right):
        up, down = above(x), below(x)
        head = jnp.broadcast_to(zhi[row, pl.ds(x, 1), :], (8, 128))
        tail = jnp.broadcast_to(zlo[row, pl.ds(x, 1), :], (8, 128))
        ahead = jnp.where(sublane == 7, head, pltpu.roll(mid, 7, 0))
        behind = jnp.where(sublane == 0, tail, pltpu.roll(mid, 1, 0))
        around = ((up + down) + (left + right)) + (ahead + behind)
        carried = (fy[row, x] * (up - down) + fx[row, x] * (right - left)) + fz[row, x] * (ahead - behind)
        put(x, ((1.0 - 6.0 * RATE) * mid + RATE * around) - carried)

    def run(start, count, left, mid):
        for k in range(count):
            right = here(start + k + 1)
            cell(start + k, left, mid, right)
            left, mid = mid, right
        return left, mid

    def body(i, carry):
        return run(pl.multiple_of(i * BLOCK, BLOCK), BLOCK, *carry)

    if sides is not None:
        cell(0, sides[0][row], here(0), here(1))
        cell(cells - 1, here(cells - 2), here(cells - 1), sides[1][row])
    carry = run(1, BLOCK - 1, here(0), here(1))
    carry = lax.fori_loop(1, cells // BLOCK - 1, body, carry)
    run(cells - BLOCK, BLOCK - 1, *carry)


def march_sides(row, cells, here, above, below, put, downs, flows, sides):
    zlo, zhi = downs
    fy, fx, fz = flows
    sublane = lax.broadcasted_iota(jnp.int32, (8, 128), 0)
    for x, left, right in ((0, sides[0][row], here(1)), (cells - 1, here(cells - 2), sides[1][row])):
        mid, up, down = here(x), above(x), below(x)
        head = jnp.broadcast_to(zhi[row, pl.ds(x, 1), :], (8, 128))
        tail = jnp.broadcast_to(zlo[row, pl.ds(x, 1), :], (8, 128))
        ahead = jnp.where(sublane == 7, head, pltpu.roll(mid, 7, 0))
        behind = jnp.where(sublane == 0, tail, pltpu.roll(mid, 1, 0))
        around = ((up + down) + (left + right)) + (ahead + behind)
        carried = (fy[row, x] * (up - down) + fx[row, x] * (right - left)) + fz[row, x] * (ahead - behind)
        put(x, ((1.0 - 6.0 * RATE) * mid + RATE * around) - carried)


def reader(ref, *at):
    return lambda x: ref[(*at, x)]


def writer(ref, *at):
    def put(x, value):
        ref[(*at, x)] = value

    return put


def planes_of(refs, height):
    if len(refs) == 1:
        return [refs[0].at[y] for y in range(height)]
    low, inner, high = refs
    return [low, *(inner.at[y] for y in range(height - 2)), high]


def inner_kernel(parts, height, *refs):
    field, downs, flows, (out,) = refs[:parts], refs[parts : parts + 2], refs[parts + 2 : parts + 5], refs[parts + 5 :]
    rows = [reader(plane) for plane in planes_of(field, height)]
    for y in range(1, height - 1):
        march_row(y, flows[0].shape[1], rows[y], rows[y + 1], rows[y - 1], writer(out, y - 1), downs, flows)


def rim_kernel(parts, height, *refs):
    field, downs, flows = refs[:parts], refs[parts : parts + 2], refs[parts + 2 : parts + 5]
    sides, (slo, shi) = refs[parts + 5 : parts + 7], refs[parts + 7 : parts + 9]
    mid, low, high = refs[parts + 10 :]
    cells = flows[0].shape[1]
    rows = [reader(plane) for plane in planes_of(field, height)]
    puts = [writer(low), *(writer(mid, y) for y in range(height - 2)), writer(high)]
    for y in range(height):
        above = reader(shi) if y == height - 1 else rows[y + 1]
        below = reader(slo) if y == 0 else rows[y - 1]
        march = march_row if y in (0, height - 1) else march_sides
        march(y, cells, rows[y], above, below, puts[y], downs, flows, sides)


def rows_kernel(field, low, high, done):
    copies = [
        pltpu.make_async_copy(field.at[0], low, done.at[0]),
        pltpu.make_async_copy(field.at[field.shape[0] - 1], high, done.at[1]),
    ]
    for copy in copies:
        copy.start()
    for copy in copies:
        copy.wait()


def faces_kernel(parts, height, *refs):
    field, (first, last, left, right) = refs[:parts], refs[parts:]
    cells = first.shape[1]
    for y, plane in enumerate(planes_of(field, height)):
        flat = plane.reshape(cells * 8, 128)
        first[y] = flat[pl.ds(0, cells, 8), :]
        last[y] = flat[pl.ds(7, cells, 8), :]
        left[y] = plane[0]
        right[y] = plane[cells - 1]


def totals_kernel(core, low, inner, high, own, other, end, done):
    half, cells = own.shape[:2]
    planes = planes_of((low, inner, high), 2 * half)
    copies = [
        pltpu.make_async_copy(low, end.at[0], done.at[0]),
        pltpu.make_async_copy(inner, end.at[pl.ds(1, 2 * half - 2)], done.at[1]),
        pltpu.make_async_copy(high, end.at[2 * half - 1], done.at[2]),
    ]
    for copy in copies:
        copy.start()

    def add_up(out, planes):
        for y, plane in enumerate(planes):
            flat = plane.reshape(cells * 8, 128)
            terms = [flat[pl.ds(k, cells, 8), :] for k in range(8)]
            out[y] = ((terms[0] + terms[1]) + (terms[2] + terms[3])) + ((terms[4] + terms[5]) + (terms[6] + terms[7]))

    @pl.when(core[0] == 0)
    def _():
        add_up(own, planes[:half])
        add_up(other, planes[half:])

    @pl.when(core[0] != 0)
    def _():
        add_up(own, planes[half:])
        add_up(other, planes[:half])

    for copy in copies:
        copy.wait()


def add_kernel(a, b, out):
    out[...] = a[...] + b[...]


def before_kernel(pieces, out):
    so_far = jnp.zeros(pieces.shape[1:], jnp.float32)
    for k in range(pieces.shape[0]):
        out[k] = so_far
        so_far = so_far + pieces[k]


def split_kernel(core, chips, own, got, mine, partners):
    @pl.when(core[0] == 0)
    def _():
        mine[...] = chips[...]
        partners[...] = chips[...] + own[...]

    @pl.when(core[0] != 0)
    def _():
        mine[...] = chips[...] + got[...]
        partners[...] = chips[...]


def potential_kernel(scale, core, low, inner, high, mine, theirs, out, held, done):
    half, cells = mine.shape[:2]
    sublane = lax.broadcasted_iota(jnp.int32, (8, 128), 0)
    planes = planes_of((low, inner, high), 2 * half)

    def fill(y, before, j):
        def body(i, carry):
            start = pl.multiple_of(i * BLOCK, BLOCK)
            for k in range(BLOCK):
                x = start + k
                value = planes[y][x]
                for reach in (1, 2, 4):
                    value = value + jnp.where(sublane >= reach, pltpu.roll(value, reach, 0), 0.0)
                held[y, x] = (value + jnp.broadcast_to(before[j, pl.ds(x, 1), :], (8, 128))) * scale
            return carry

        lax.fori_loop(0, cells // BLOCK, body, 0)
        copy = pltpu.make_async_copy(held.at[y], out.at[y], done.at[y])
        copy.start()

    @pl.when(core[0] == 0)
    def _():
        for y in range(2 * half):
            fill(y, (mine, theirs)[y // half], y % half)

    @pl.when(core[0] != 0)
    def _():
        for y in range(2 * half):
            fill(y, (theirs, mine)[y // half], y % half)

    for y in range(2 * half):
        pltpu.make_async_copy(held.at[y], out.at[y], done.at[y]).wait()


def sent(array, axis, by):
    size = lax.axis_size(axis)
    return lax.ppermute(array, axis, [(i, (i + by) % size) for i in range(size)])


def local(field_values, flow_y, flow_x, flow_z):
    core, field_values = lax.optimization_barrier((lax.axis_index("core").reshape(1), field_values))
    height, cells = field_values.shape[:2]
    flows = (flow_y, flow_x, flow_z)
    row = shape(cells, 8, 128)
    inner = shape(height - 2, cells, 8, 128)
    whole = shape(*field_values.shape)
    edge, side = shape(height, cells, 128), shape(height, 8, 128)
    field = (field_values,)
    low, high = call(rows_kernel, (row, row), field_values, in_specs=[IN_HBM], scratch=[pltpu.SemaphoreType.DMA((2,))])
    for _ in range(STEPS):
        parts = len(field)
        slo, shi = sent(high, "south", 1), sent(low, "south", -1)
        first, last, left, right = call(
            functools.partial(faces_kernel, parts, height), (edge, edge, side, side), *field
        )
        downs = (sent(last, DOWN, 1), sent(first, DOWN, -1))
        sides = (sent(right, "east", 1), sent(left, "east", -1))
        (mid,) = call(
            functools.partial(inner_kernel, parts, height), (inner,), *(*field, *downs, *flows), flops=1 << 23
        )
        mid, low, high = call(
            functools.partial(rim_kernel, parts, height),
            (inner, row, row),
            *(*field, *downs, *flows, *sides, slo, shi, mid),
            alias={parts + 9: 0},
        )
        field = (low, mid, high)
    scalar = pl.BlockSpec(memory_space=pltpu.SMEM)
    quarter = shape(height // 2, cells, 128)
    own, other, end = call(
        totals_kernel,
        (quarter, quarter, whole),
        *(core, *field),
        in_specs=[scalar, *[IN_VMEM] * 3],
        out_specs=[IN_VMEM, IN_VMEM, IN_HBM],
        scratch=[pltpu.SemaphoreType.DMA((3,))],
    )
    got = sent(other, "core", 1)
    (total,) = call(add_kernel, (quarter,), own, got)
    chips = lax.axis_size("chip")
    pieces = lax.all_to_all(total.reshape(chips, -1, 128), "chip", 0, 0, tiled=True)
    (pieces,) = call(before_kernel, (shape(*pieces.shape),), pieces)
    below = lax.all_to_all(pieces, "chip", 0, 0, tiled=True).reshape(total.shape)
    mine, partners = call(split_kernel, (quarter, quarter), core, below, own, got, in_specs=[scalar, *[IN_VMEM] * 3])
    theirs = sent(partners, "core", 1)
    (potential,) = call(
        functools.partial(potential_kernel, 1.0 / (8 * chips * 2)),
        (whole,),
        *(core, *field, mine, theirs),
        in_specs=[scalar, *[IN_VMEM] * 5],
        out_specs=[IN_HBM],
        scratch=[pltpu.VMEM(whole.shape, jnp.float32), pltpu.SemaphoreType.DMA((height,))],
    )
    return potential, end


def solution(mesh):
    finer = Mesh(
        mesh.devices.reshape(mesh.shape["south"], mesh.shape["east"], -1, 2), ("south", "east", "chip", "core")
    )
    spec = P("south", "east", DOWN, None)
    return jax.shard_map(local, mesh=finer, in_specs=(spec,) * 4, out_specs=(spec, spec), check_vma=False)
```

time: 167 us -> 103 us (0.62)
  waiting for transfers between devices: 62.3 us -> 11.8 us
  other arithmetic: 38.5 us -> 0 us
  blocking collectives: 4.94 us -> 24.7 us
  Pallas kernels: 0 us -> 16 us
  between operations: 14.4 us -> 1.02 us
  starting transfers between devices: 33.9 us -> 45.6 us
  local copies, waits for them, and re-layouts: 12.6 us -> 3.79 us
    all_gather x1 -> x0, waiting for transfers between devices: 38.6 us -> none  [prefix_by_axis(): pieces = lax.all_gather(so_far, axis)]
    add x6 -> x0, other arithmetic: 34.8 us -> none  [the longest x4 30.5 us: march_step(): middle - flow_y * slopes[0] - flow_x * slopes[1] - flow_z * slopes[2]]
    all_to_all x0 -> x2, blocking collectives: none -> 24.7 us  [the longest x1 13.4 us: local(): lax.all_to_all(total.reshape(chips, -1, 128), 'chip', 0, 0, tiled=True)]
    pallas_call x0 -> x18, Pallas kernels: none -> 16 us  [call(): pl.pallas_call(kernel, out_shape=outs, in_specs=in_specs or [IN_VMEM] * l...]
    ppermute x24 -> x26, waiting for transfers between devices: 23.7 us -> 11.8 us  [sent(): lax.ppermute(array, axis, [(i, (i + by) % size) for i in range(size)])]
    ppermute x24 -> x26, starting transfers between devices: 33.8 us -> 45.6 us  [sent(): lax.ppermute(array, axis, [(i, (i + by) % size) for i in range(size)])]
    unnamed x17 -> x10, local copies, waits for them, and re-layouts: 11.8 us -> 3.79 us
    all_gather x1 -> x0, blocking collectives: 4.94 us -> none  [prefix_by_axis(): pieces = lax.all_gather(so_far, axis)]
  transfers between devices with their start and end apart: 25 -> 26, of which waited for: 10 -> 9; matrix products, arithmetic and copies ran while one was open for 3% -> 0% of each run, Pallas kernels for 0% -> 8%
where the time goes in v1:
time: 103 us
  starting transfers between devices  45.6 us (44%)
  blocking collectives  24.7 us (24%)
  Pallas kernels  16 us (16%)
  waiting for transfers between devices  11.8 us (11%)
  local copies, waits for them, and re-layouts  3.79 us (4%)
    ppermute x26, starting transfers between devices, sent(): lax.ppermute(array, axis, [(i, (i + by) % size) for i in range(size)])  45.6 us
    pallas_call x18, Pallas kernels, call(): pl.pallas_call(kernel, out_shape=outs, in_specs=in_specs or [IN_VMEM] * l...  16 us
    all_to_all x1, blocking collectives, local(): lax.all_to_all(total.reshape(chips, -1, 128), 'chip', 0, 0, tiled=True)  13.4 us
    ppermute x26, waiting for transfers between devices, sent(): lax.ppermute(array, axis, [(i, (i + by) % size) for i in range(size)])  11.8 us
    all_to_all x1, blocking collectives, local(): lax.all_to_all(pieces, 'chip', 0, 0, tiled=True).reshape(total.shape)  11.3 us
    unnamed x10, local copies, waits for them, and re-layouts  3.79 us
  transfers between devices with their start and end apart: 26, of which 9 were waited for; matrix products, arithmetic and copies ran while one was open for 0% of the time, Pallas kernels for 8%

profile of v1, /device:TPU:1, one launch (start us, length us, event | category | flops | bytes accessed | tf_op | source)
XLA Modules:
  0.0 102.9 jit_solution(727597153066710894)
XLA Ops:
  0.6 1.9 %copy-done.4 = f32[8,96,8,128]{3,2,1,0:T(8,128)S(1)} copy-done((f32[8,96,8,128]{3,2,1,0:T(8,128)S(1)}, f32[8,96,8,128]{3,2,1,0:T(8,128)}, u32[]{:S(2)}) %copy-start.4) | copy-done | bytes 3145752
  2.7 3.0 %collective-permute-start = (f32[8,96,128]{2,1,0:T(8,128)S(1)}, f32[8,96,128]{2,1,0:T(8,128)S(1)}, u32[]{:S(2)}, u32[]{:S(2)}) collective-permute-start(f32[8,96,128]{2,1,0:T(8,128)S(1)} %get-tuple-element.41), channel_id=1, source_target_pairs={{0,1},{1,2},{2,3},{3,4},{4,5},{5,6},{6,7},{7,8},{8,9},{9,10},{10,1... | collective-permute-start | bytes 1179656 | tf_op jit(solution)/shard_map/ppermute | solution.py:238
  10.4 2.7 %collective-permute-start.3 = (f32[8,8,128]{2,1,0:T(8,128)S(1)}, f32[8,8,128]{2,1,0:T(8,128)S(1)}, u32[]{:S(2)}, u32[]{:S(2)}) collective-permute-start(f32[8,8,128]{2,1,0:T(8,128)S(1)} %get-tuple-element.44), channel_id=1, source_target_pairs={{0,48},{16,0},{32,16},{48,32},{1,49},{17,1},{33,17},{49,33},{2,50}... | collective-permute-start | bytes 98312 | tf_op jit(solution)/shard_map/ppermute | solution.py:238
  13.2 1.9 %copy-done.2 = f32[8,96,8,128]{3,2,1,0:T(8,128)S(1)} copy-done((f32[8,96,8,128]{3,2,1,0:T(8,128)S(1)}, f32[8,96,8,128]{3,2,1,0:T(8,128)}, u32[]{:S(2)}) %copy-start.2) | copy-done | bytes 3145752
  15.1 2.0 %shard_map.61.refs_10_ = f32[6,96,8,128]{3,2,1,0:T(8,128)S(1)} custom-call(f32[8,96,8,128]{3,2,1,0:T(8,128)S(1)} %copy-done.4, f32[8,96,128]{2,1,0:T(8,128)S(1)} %collective-permute-done.refs_1_, f32[8,96,128]{2,1,0:T(8,128)S(1)} %collective-permute-done.1.refs_2_, f32[8,96,8,128]{3,2,1,0:T(8,128)S(1)} %copy-done, f32[8,96,8,128]{3,2,1,0:T(8,128)S(1)} %copy-done.1, ...), custom_call_target="tpu_custom_call" | custom-call | flops 8388608 | tf_op jit(solution)/shard_map/pallas_call | solution.py:27
  18.0 3.4 %collective-permute-start.6 = (f32[8,96,128]{2,1,0:T(8,128)S(1)}, f32[8,96,128]{2,1,0:T(8,128)S(1)}, u32[]{:S(2)}, u32[]{:S(2)}) collective-permute-start(f32[8,96,128]{2,1,0:T(8,128)S(1)} %get-tuple-element.50), channel_id=1, source_target_pairs={{0,1},{1,2},{2,3},{3,4},{4,5},{5,6},{6,7},{7,8},{8,9},{9,10},{10,1... | collective-permute-start | bytes 1179656 | tf_op jit(solution)/shard_map/ppermute | solution.py:238
  22.8 2.5 %collective-permute-start.11 = (f32[96,8,128]{2,1,0:T(8,128)S(1)}, f32[96,8,128]{2,1,0:T(8,128)S(1)}, u32[]{:S(2)}, u32[]{:S(2)}) collective-permute-start(f32[96,8,128]{2,1,0:T(8,128)S(1)} %get-tuple-element.47.refs_0_), channel_id=1, source_target_pairs={{0,192},{64,0},{128,64},{192,128},{1,193},{65,1},{129,65},{193,129... | collective-permute-start | bytes 1179656 | tf_op jit(solution)/shard_map/ppermute | solution.py:238
  26.1 2.7 %collective-permute-start.9 = (f32[8,8,128]{2,1,0:T(8,128)S(1)}, f32[8,8,128]{2,1,0:T(8,128)S(1)}, u32[]{:S(2)}, u32[]{:S(2)}) collective-permute-start(f32[8,8,128]{2,1,0:T(8,128)S(1)} %get-tuple-element.53), channel_id=1, source_target_pairs={{0,48},{16,0},{32,16},{48,32},{1,49},{17,1},{33,17},{49,33},{2,50}... | collective-permute-start | bytes 98312 | tf_op jit(solution)/shard_map/ppermute | solution.py:238
  28.8 2.0 %shard_map.64.refs_12_ = f32[6,96,8,128]{3,2,1,0:T(8,128)S(1)} custom-call(f32[96,8,128]{2,1,0:T(8,128)S(1)} %get-tuple-element.47.refs_0_, f32[6,96,8,128]{3,2,1,0:T(8,128)S(1)} %get-tuple-element.48.refs_1_, f32[96,8,128]{2,1,0:T(8,128)S(1)} %get-tuple-element.49.refs_2_, f32[8,96,128]{2,1,0:T(8,128)S(1)} %collective-permute-done.6.refs_3_, ...), custom_call_target="tpu_custom_call" | custom-call | flops 8388608 | tf_op jit(solution)/shard_map/pallas_call | solution.py:27
  30.8 3.1 %collective-permute-done.10.refs_10_ = f32[96,8,128]{2,1,0:T(8,128)S(1)} collective-permute-done((f32[96,8,128]{2,1,0:T(8,128)S(1)}, f32[96,8,128]{2,1,0:T(8,128)S(1)}, u32[]{:S(2)}, u32[]{:S(2)}) %collective-permute-start.10) | collective-permute-done | bytes 393248 | tf_op jit(solution)/shard_map/ppermute | solution.py:238
  34.8 4.4 %collective-permute-start.12 = (f32[8,96,128]{2,1,0:T(8,128)S(1)}, f32[8,96,128]{2,1,0:T(8,128)S(1)}, u32[]{:S(2)}, u32[]{:S(2)}) collective-permute-start(f32[8,96,128]{2,1,0:T(8,128)S(1)} %get-tuple-element.57), channel_id=1, source_target_pairs={{0,1},{1,2},{2,3},{3,4},{4,5},{5,6},{6,7},{7,8},{8,9},{9,10},{10,1... | collective-permute-start | bytes 1179656 | tf_op jit(solution)/shard_map/ppermute | solution.py:238
  41.9 2.0 %collective-permute-done.12.refs_3_ = f32[8,96,128]{2,1,0:T(8,128)S(1)} collective-permute-done((f32[8,96,128]{2,1,0:T(8,128)S(1)}, f32[8,96,128]{2,1,0:T(8,128)S(1)}, u32[]{:S(2)}, u32[]{:S(2)}) %collective-permute-start.12) | collective-permute-done | bytes 393248 | tf_op jit(solution)/shard_map/ppermute | solution.py:238
  43.9 2.7 %collective-permute-start.15 = (f32[8,8,128]{2,1,0:T(8,128)S(1)}, f32[8,8,128]{2,1,0:T(8,128)S(1)}, u32[]{:S(2)}, u32[]{:S(2)}) collective-permute-start(f32[8,8,128]{2,1,0:T(8,128)S(1)} %get-tuple-element.60), channel_id=1, source_target_pairs={{0,48},{16,0},{32,16},{48,32},{1,49},{17,1},{33,17},{49,33},{2,50}... | collective-permute-start | bytes 98312 | tf_op jit(solution)/shard_map/ppermute | solution.py:238
  46.6 2.0 %shard_map.67.refs_12_ = f32[6,96,8,128]{3,2,1,0:T(8,128)S(1)} custom-call(f32[96,8,128]{2,1,0:T(8,128)S(1)} %get-tuple-element.54.refs_0_, f32[6,96,8,128]{3,2,1,0:T(8,128)S(1)} %get-tuple-element.55.refs_1_, f32[96,8,128]{2,1,0:T(8,128)S(1)} %get-tuple-element.56.refs_2_, f32[8,96,128]{2,1,0:T(8,128)S(1)} %collective-permute-done.12.refs_3_, ...), custom_call_target="tpu_custom_call" | custom-call | flops 8388608 | tf_op jit(solution)/shard_map/pallas_call | solution.py:27
  49.5 5.5 %collective-permute-start.18 = (f32[8,96,128]{2,1,0:T(8,128)S(1)}, f32[8,96,128]{2,1,0:T(8,128)S(1)}, u32[]{:S(2)}, u32[]{:S(2)}) collective-permute-start(f32[8,96,128]{2,1,0:T(8,128)S(1)} %get-tuple-element.64), channel_id=1, source_target_pairs={{0,1},{1,2},{2,3},{3,4},{4,5},{5,6},{6,7},{7,8},{8,9},{9,10},{10,1... | collective-permute-start | bytes 1179656 | tf_op jit(solution)/shard_map/ppermute | solution.py:238
  57.8 2.0 %collective-permute-done.18.refs_3_ = f32[8,96,128]{2,1,0:T(8,128)S(1)} collective-permute-done((f32[8,96,128]{2,1,0:T(8,128)S(1)}, f32[8,96,128]{2,1,0:T(8,128)S(1)}, u32[]{:S(2)}, u32[]{:S(2)}) %collective-permute-start.18) | collective-permute-done | bytes 393248 | tf_op jit(solution)/shard_map/ppermute | solution.py:238
  59.7 2.7 %collective-permute-start.21 = (f32[8,8,128]{2,1,0:T(8,128)S(1)}, f32[8,8,128]{2,1,0:T(8,128)S(1)}, u32[]{:S(2)}, u32[]{:S(2)}) collective-permute-start(f32[8,8,128]{2,1,0:T(8,128)S(1)} %get-tuple-element.67), channel_id=1, source_target_pairs={{0,48},{16,0},{32,16},{48,32},{1,49},{17,1},{33,17},{49,33},{2,50}... | collective-permute-start | bytes 98312 | tf_op jit(solution)/shard_map/ppermute | solution.py:238
  62.5 2.0 %shard_map.70.refs_12_ = f32[6,96,8,128]{3,2,1,0:T(8,128)S(1)} custom-call(f32[96,8,128]{2,1,0:T(8,128)S(1)} %get-tuple-element.61.refs_0_, f32[6,96,8,128]{3,2,1,0:T(8,128)S(1)} %get-tuple-element.62.refs_1_, f32[96,8,128]{2,1,0:T(8,128)S(1)} %get-tuple-element.63.refs_2_, f32[8,96,128]{2,1,0:T(8,128)S(1)} %collective-permute-done.18.refs_3_, ...), custom_call_target="tpu_custom_call" | custom-call | flops 8388608 | tf_op jit(solution)/shard_map/pallas_call | solution.py:27
  66.6 1.7 %shard_map.72 = (f32[4,96,128]{2,1,0:T(8,128)S(1)}, f32[4,96,128]{2,1,0:T(8,128)S(1)}, f32[8,96,8,128]{3,2,1,0:T(8,128)}) custom-call(s32[1]{0:T(128)} %bitcast.core, f32[96,8,128]{2,1,0:T(8,128)S(1)} %get-tuple-element.68.low, f32[6,96,8,128]{3,2,1,0:T(8,128)S(1)} %get-tuple-element.69.inner, f32[96,8,128]{2,1,0:T(8,128)S(1)} %get-tuple-element.70.high), custom_call_target="tpu_custom_call" | custom-call | flops 2097152 | tf_op jit(solution)/shard_map/pallas_call | solution.py:27
  68.3 2.0 %collective-permute-start.24 = (f32[4,96,128]{2,1,0:T(8,128)S(1)}, f32[4,96,128]{2,1,0:T(8,128)S(1)}, u32[]{:S(2)}, u32[]{:S(2)}) collective-permute-start(f32[4,96,128]{2,1,0:T(8,128)S(1)} %get-tuple-element.72), channel_id=1, source_target_pairs={{0,1},{1,0},{2,3},{3,2},{4,5},{5,4},{6,7},{7,6},{8,9},{9,8},{10,11... | collective-permute-start | bytes 589832 | tf_op jit(solution)/shard_map/ppermute | solution.py:238
  71.3 13.4 %all_to_all.10.pieces = f32[8,48,128]{2,1,0:T(8,128)S(1)} all-to-all(f32[8,48,128]{2,1,0:T(8,128)S(1)} %bitcast.4), channel_id=1, replica_groups=mesh['south'=4,'east'=4,'chip'=8,'core'=2] {'chip'}, dimensions={0} | all-to-all | bytes 393216 | tf_op jit(solution)/shard_map/all_to_all | solution.py:282
  84.7 11.3 %all_to_all.11 = f32[8,48,128]{2,1,0:T(8,128)S(1)} all-to-all(f32[8,48,128]{2,1,0:T(8,128)S(1)} %shard_map.74), channel_id=1, replica_groups=mesh['south'=4,'east'=4,'chip'=8,'core'=2] {'chip'}, dimensions={0} | all-to-all | bytes 393216 | tf_op jit(solution)/shard_map/all_to_all | solution.py:284
  96.0 2.9 %collective-permute-start.25 = (f32[4,96,128]{2,1,0:T(8,128)S(1)}, f32[4,96,128]{2,1,0:T(8,128)S(1)}, u32[]{:S(2)}, u32[]{:S(2)}) collective-permute-start(f32[4,96,128]{2,1,0:T(8,128)S(1)} %get-tuple-element.74), channel_id=1, source_target_pairs={{0,1},{1,0},{2,3},{3,2},{4,5},{5,4},{6,7},{7,6},{8,9},{9,8},{10,11... | collective-permute-start | bytes 589832 | tf_op jit(solution)/shard_map/ppermute | solution.py:238
  100.1 2.7 %shard_map.76 = f32[8,96,8,128]{3,2,1,0:T(8,128)} custom-call(s32[1]{0:T(128)} %bitcast.core, f32[96,8,128]{2,1,0:T(8,128)S(1)} %get-tuple-element.68.low, f32[6,96,8,128]{3,2,1,0:T(8,128)S(1)} %get-tuple-element.69.inner, f32[96,8,128]{2,1,0:T(8,128)S(1)} %get-tuple-element.70.high, f32[4,96,128]{2,1,0:T(8,128)S(1)} %get-tuple-element.73.mine, ...), custom_call_target="tpu_custom_call" | custom-call | flops 2097152 | tf_op jit(solution)/shard_map/pallas_call | solution.py:27
  (58 shorter events, 19.7 us)
Async XLA Ops:
  2.7 7.8 %collective-permute-start = (f32[8,96,128]{2,1,0:T(8,128)S(1)}, f32[8,96,128]{2,1,0:T(8,128)S(1)}, u32[]{:S(2)}, u32[]{:S(2)}) collective-permute-start(f32[8,96,128]{2,1,0:T(8,128)S(1)} %get-tuple-element.41), channel_id=1, source_target_pairs={{0,1},{1,2},{2,3},{3,4},{4,5},{5,6},{6,7},{7,8},{8,9},{9,10},{10,1... | collective-permute-start | bytes 1179656 | tf_op jit(solution)/shard_map/ppermute | solution.py:238
  5.7 7.5 %collective-permute-start.1 = (f32[8,96,128]{2,1,0:T(8,128)S(1)}, f32[8,96,128]{2,1,0:T(8,128)S(1)}, u32[]{:S(2)}, u32[]{:S(2)}) collective-permute-start(f32[8,96,128]{2,1,0:T(8,128)S(1)} %get-tuple-element.42), channel_id=1, source_target_pairs={{0,15},{1,0},{2,1},{3,2},{4,3},{5,4},{6,5},{7,6},{8,7},{9,8},{10,9... | collective-permute-start | bytes 1179656 | tf_op jit(solution)/shard_map/ppermute | solution.py:238
  6.3 10.8 %collective-permute-start.4 = (f32[96,8,128]{2,1,0:T(8,128)S(1)}, f32[96,8,128]{2,1,0:T(8,128)S(1)}, u32[]{:S(2)}, u32[]{:S(2)}) collective-permute-start(f32[96,8,128]{2,1,0:T(8,128)S(1)} %get-tuple-element.45), channel_id=1, source_target_pairs={{0,64},{64,128},{128,192},{192,0},{1,65},{65,129},{129,193},{193,1... | collective-permute-start | bytes 1179656 | tf_op jit(solution)/shard_map/ppermute | solution.py:238
  7.4 9.7 %collective-permute-start.5 = (f32[96,8,128]{2,1,0:T(8,128)S(1)}, f32[96,8,128]{2,1,0:T(8,128)S(1)}, u32[]{:S(2)}, u32[]{:S(2)}) collective-permute-start(f32[96,8,128]{2,1,0:T(8,128)S(1)} %get-tuple-element.46), channel_id=1, source_target_pairs={{0,192},{64,0},{128,64},{192,128},{1,193},{65,1},{129,65},{193,129... | collective-permute-start | bytes 1179656 | tf_op jit(solution)/shard_map/ppermute | solution.py:238
  9.1 8.0 %collective-permute-start.2 = (f32[8,8,128]{2,1,0:T(8,128)S(1)}, f32[8,8,128]{2,1,0:T(8,128)S(1)}, u32[]{:S(2)}, u32[]{:S(2)}) collective-permute-start(f32[8,8,128]{2,1,0:T(8,128)S(1)} %get-tuple-element.43), channel_id=1, source_target_pairs={{0,16},{16,32},{32,48},{48,0},{1,17},{17,33},{33,49},{49,1},{2,18}... | collective-permute-start | bytes 98312 | tf_op jit(solution)/shard_map/ppermute | solution.py:238
  10.4 6.6 %collective-permute-start.3 = (f32[8,8,128]{2,1,0:T(8,128)S(1)}, f32[8,8,128]{2,1,0:T(8,128)S(1)}, u32[]{:S(2)}, u32[]{:S(2)}) collective-permute-start(f32[8,8,128]{2,1,0:T(8,128)S(1)} %get-tuple-element.44), channel_id=1, source_target_pairs={{0,48},{16,0},{32,16},{48,32},{1,49},{17,1},{33,17},{49,33},{2,50}... | collective-permute-start | bytes 98312 | tf_op jit(solution)/shard_map/ppermute | solution.py:238
  18.0 8.1 %collective-permute-start.6 = (f32[8,96,128]{2,1,0:T(8,128)S(1)}, f32[8,96,128]{2,1,0:T(8,128)S(1)}, u32[]{:S(2)}, u32[]{:S(2)}) collective-permute-start(f32[8,96,128]{2,1,0:T(8,128)S(1)} %get-tuple-element.50), channel_id=1, source_target_pairs={{0,1},{1,2},{2,3},{3,4},{4,5},{5,6},{6,7},{7,8},{8,9},{9,10},{10,1... | collective-permute-start | bytes 1179656 | tf_op jit(solution)/shard_map/ppermute | solution.py:238
  21.3 7.5 %collective-permute-start.7 = (f32[8,96,128]{2,1,0:T(8,128)S(1)}, f32[8,96,128]{2,1,0:T(8,128)S(1)}, u32[]{:S(2)}, u32[]{:S(2)}) collective-permute-start(f32[8,96,128]{2,1,0:T(8,128)S(1)} %get-tuple-element.51), channel_id=1, source_target_pairs={{0,15},{1,0},{2,1},{3,2},{4,3},{5,4},{6,5},{7,6},{8,7},{9,8},{10,9... | collective-permute-start | bytes 1179656 | tf_op jit(solution)/shard_map/ppermute | solution.py:238
  22.8 8.0 %collective-permute-start.11 = (f32[96,8,128]{2,1,0:T(8,128)S(1)}, f32[96,8,128]{2,1,0:T(8,128)S(1)}, u32[]{:S(2)}, u32[]{:S(2)}) collective-permute-start(f32[96,8,128]{2,1,0:T(8,128)S(1)} %get-tuple-element.47.refs_0_), channel_id=1, source_target_pairs={{0,192},{64,0},{128,64},{192,128},{1,193},{65,1},{129,65},{193,129... | collective-permute-start | bytes 1179656 | tf_op jit(solution)/shard_map/ppermute | solution.py:238
  25.3 8.7 %collective-permute-start.10 = (f32[96,8,128]{2,1,0:T(8,128)S(1)}, f32[96,8,128]{2,1,0:T(8,128)S(1)}, u32[]{:S(2)}, u32[]{:S(2)}) collective-permute-start(f32[96,8,128]{2,1,0:T(8,128)S(1)} %get-tuple-element.49.refs_2_), channel_id=1, source_target_pairs={{0,64},{64,128},{128,192},{192,0},{1,65},{65,129},{129,193},{193,1... | collective-permute-start | bytes 1179656 | tf_op jit(solution)/shard_map/ppermute | solution.py:238
  25.3 5.5 %collective-permute-start.8 = (f32[8,8,128]{2,1,0:T(8,128)S(1)}, f32[8,8,128]{2,1,0:T(8,128)S(1)}, u32[]{:S(2)}, u32[]{:S(2)}) collective-permute-start(f32[8,8,128]{2,1,0:T(8,128)S(1)} %get-tuple-element.52), channel_id=1, source_target_pairs={{0,16},{16,32},{32,48},{48,0},{1,17},{17,33},{33,49},{49,1},{2,18}... | collective-permute-start | bytes 98312 | tf_op jit(solution)/shard_map/ppermute | solution.py:238
  26.1 4.7 %collective-permute-start.9 = (f32[8,8,128]{2,1,0:T(8,128)S(1)}, f32[8,8,128]{2,1,0:T(8,128)S(1)}, u32[]{:S(2)}, u32[]{:S(2)}) collective-permute-start(f32[8,8,128]{2,1,0:T(8,128)S(1)} %get-tuple-element.53), channel_id=1, source_target_pairs={{0,48},{16,0},{32,16},{48,32},{1,49},{17,1},{33,17},{49,33},{2,50}... | collective-permute-start | bytes 98312 | tf_op jit(solution)/shard_map/ppermute | solution.py:238
  34.8 9.1 %collective-permute-start.12 = (f32[8,96,128]{2,1,0:T(8,128)S(1)}, f32[8,96,128]{2,1,0:T(8,128)S(1)}, u32[]{:S(2)}, u32[]{:S(2)}) collective-permute-start(f32[8,96,128]{2,1,0:T(8,128)S(1)} %get-tuple-element.57), channel_id=1, source_target_pairs={{0,1},{1,2},{2,3},{3,4},{4,5},{5,6},{6,7},{7,8},{8,9},{9,10},{10,1... | collective-permute-start | bytes 1179656 | tf_op jit(solution)/shard_map/ppermute | solution.py:238
  39.1 7.5 %collective-permute-start.13 = (f32[8,96,128]{2,1,0:T(8,128)S(1)}, f32[8,96,128]{2,1,0:T(8,128)S(1)}, u32[]{:S(2)}, u32[]{:S(2)}) collective-permute-start(f32[8,96,128]{2,1,0:T(8,128)S(1)} %get-tuple-element.58), channel_id=1, source_target_pairs={{0,15},{1,0},{2,1},{3,2},{4,3},{5,4},{6,5},{7,6},{8,7},{9,8},{10,9... | collective-permute-start | bytes 1179656 | tf_op jit(solution)/shard_map/ppermute | solution.py:238
  39.2 9.5 %collective-permute-start.17 = (f32[96,8,128]{2,1,0:T(8,128)S(1)}, f32[96,8,128]{2,1,0:T(8,128)S(1)}, u32[]{:S(2)}, u32[]{:S(2)}) collective-permute-start(f32[96,8,128]{2,1,0:T(8,128)S(1)} %get-tuple-element.54.refs_0_), channel_id=1, source_target_pairs={{0,192},{64,0},{128,64},{192,128},{1,193},{65,1},{129,65},{193,129... | collective-permute-start | bytes 1179656 | tf_op jit(solution)/shard_map/ppermute | solution.py:238
  39.2 9.5 %collective-permute-start.16 = (f32[96,8,128]{2,1,0:T(8,128)S(1)}, f32[96,8,128]{2,1,0:T(8,128)S(1)}, u32[]{:S(2)}, u32[]{:S(2)}) collective-permute-start(f32[96,8,128]{2,1,0:T(8,128)S(1)} %get-tuple-element.56.refs_2_), channel_id=1, source_target_pairs={{0,64},{64,128},{128,192},{192,0},{1,65},{65,129},{129,193},{193,1... | collective-permute-start | bytes 1179656 | tf_op jit(solution)/shard_map/ppermute | solution.py:238
  40.6 8.0 %collective-permute-start.14 = (f32[8,8,128]{2,1,0:T(8,128)S(1)}, f32[8,8,128]{2,1,0:T(8,128)S(1)}, u32[]{:S(2)}, u32[]{:S(2)}) collective-permute-start(f32[8,8,128]{2,1,0:T(8,128)S(1)} %get-tuple-element.59), channel_id=1, source_target_pairs={{0,16},{16,32},{32,48},{48,0},{1,17},{17,33},{33,49},{49,1},{2,18}... | collective-permute-start | bytes 98312 | tf_op jit(solution)/shard_map/ppermute | solution.py:238
  43.9 4.7 %collective-permute-start.15 = (f32[8,8,128]{2,1,0:T(8,128)S(1)}, f32[8,8,128]{2,1,0:T(8,128)S(1)}, u32[]{:S(2)}, u32[]{:S(2)}) collective-permute-start(f32[8,8,128]{2,1,0:T(8,128)S(1)} %get-tuple-element.60), channel_id=1, source_target_pairs={{0,48},{16,0},{32,16},{48,32},{1,49},{17,1},{33,17},{49,33},{2,50}... | collective-permute-start | bytes 98312 | tf_op jit(solution)/shard_map/ppermute | solution.py:238
  49.5 10.2 %collective-permute-start.18 = (f32[8,96,128]{2,1,0:T(8,128)S(1)}, f32[8,96,128]{2,1,0:T(8,128)S(1)}, u32[]{:S(2)}, u32[]{:S(2)}) collective-permute-start(f32[8,96,128]{2,1,0:T(8,128)S(1)} %get-tuple-element.64), channel_id=1, source_target_pairs={{0,1},{1,2},{2,3},{3,4},{4,5},{5,6},{6,7},{7,8},{8,9},{9,10},{10,1... | collective-permute-start | bytes 1179656 | tf_op jit(solution)/shard_map/ppermute | solution.py:238
  55.0 7.5 %collective-permute-start.19 = (f32[8,96,128]{2,1,0:T(8,128)S(1)}, f32[8,96,128]{2,1,0:T(8,128)S(1)}, u32[]{:S(2)}, u32[]{:S(2)}) collective-permute-start(f32[8,96,128]{2,1,0:T(8,128)S(1)} %get-tuple-element.65), channel_id=1, source_target_pairs={{0,15},{1,0},{2,1},{3,2},{4,3},{5,4},{6,5},{7,6},{8,7},{9,8},{10,9... | collective-permute-start | bytes 1179656 | tf_op jit(solution)/shard_map/ppermute | solution.py:238
  55.0 10.0 %collective-permute-start.23 = (f32[96,8,128]{2,1,0:T(8,128)S(1)}, f32[96,8,128]{2,1,0:T(8,128)S(1)}, u32[]{:S(2)}, u32[]{:S(2)}) collective-permute-start(f32[96,8,128]{2,1,0:T(8,128)S(1)} %get-tuple-element.61.refs_0_), channel_id=1, source_target_pairs={{0,192},{64,0},{128,64},{192,128},{1,193},{65,1},{129,65},{193,129... | collective-permute-start | bytes 1179656 | tf_op jit(solution)/shard_map/ppermute | solution.py:238
  55.0 10.9 %collective-permute-start.22 = (f32[96,8,128]{2,1,0:T(8,128)S(1)}, f32[96,8,128]{2,1,0:T(8,128)S(1)}, u32[]{:S(2)}, u32[]{:S(2)}) collective-permute-start(f32[96,8,128]{2,1,0:T(8,128)S(1)} %get-tuple-element.63.refs_2_), channel_id=1, source_target_pairs={{0,64},{64,128},{128,192},{192,0},{1,65},{65,129},{129,193},{193,1... | collective-permute-start | bytes 1179656 | tf_op jit(solution)/shard_map/ppermute | solution.py:238
  56.5 8.0 %collective-permute-start.20 = (f32[8,8,128]{2,1,0:T(8,128)S(1)}, f32[8,8,128]{2,1,0:T(8,128)S(1)}, u32[]{:S(2)}, u32[]{:S(2)}) collective-permute-start(f32[8,8,128]{2,1,0:T(8,128)S(1)} %get-tuple-element.66), channel_id=1, source_target_pairs={{0,16},{16,32},{32,48},{48,0},{1,17},{17,33},{33,49},{49,1},{2,18}... | collective-permute-start | bytes 98312 | tf_op jit(solution)/shard_map/ppermute | solution.py:238
  59.7 4.7 %collective-permute-start.21 = (f32[8,8,128]{2,1,0:T(8,128)S(1)}, f32[8,8,128]{2,1,0:T(8,128)S(1)}, u32[]{:S(2)}, u32[]{:S(2)}) collective-permute-start(f32[8,8,128]{2,1,0:T(8,128)S(1)} %get-tuple-element.67), channel_id=1, source_target_pairs={{0,48},{16,0},{32,16},{48,32},{1,49},{17,1},{33,17},{49,33},{2,50}... | collective-permute-start | bytes 98312 | tf_op jit(solution)/shard_map/ppermute | solution.py:238
  (7 other events, 43.1 us)

commit v2 on v1

v2 whole, which is shorter than its diff:
```python
import functools

import jax
import jax.numpy as jnp
from jax import lax
from jax.experimental import pallas as pl
from jax.experimental.pallas import tpu as pltpu
from jax.sharding import Mesh
from jax.sharding import PartitionSpec as P

STEPS = 4
RATE = 0.05
BLOCK = 8
GROUP = 3
VMEM = 5 << 20


DOWN = ("chip", "core")
IN_VMEM = pl.BlockSpec(memory_space=pltpu.VMEM)
IN_HBM = pl.BlockSpec(memory_space=pltpu.HBM)


def shape(*dims):
    return jax.ShapeDtypeStruct(dims, jnp.float32)


def call(kernel, outs, *args, flops=1 << 21, in_specs=None, out_specs=None, scratch=(), alias=None, vmem=VMEM):
    return pl.pallas_call(
        kernel,
        out_shape=outs,
        in_specs=in_specs or [IN_VMEM] * len(args),
        out_specs=out_specs or [IN_VMEM] * len(outs),
        scratch_shapes=scratch,
        input_output_aliases=alias or {},
        compiler_params=pltpu.CompilerParams(vmem_limit_bytes=vmem),
        cost_estimate=pl.CostEstimate(flops=flops, bytes_accessed=0, transcendentals=0),
    )(*args)


def advance(here, up, down, left, right, ahead, behind, fy, fx, fz):
    around = ((up + down) + (left + right)) + (ahead + behind)
    carried = (fy * (up - down) + fx * (right - left)) + fz * (ahead - behind)
    return ((1.0 - 6.0 * RATE) * here + RATE * around) - carried


def turned(here):
    return pltpu.roll(here, 7, 0), pltpu.roll(here, 1, 0)


def along_z(here, zlo, zhi, y, x):
    sublane = lax.broadcasted_iota(jnp.int32, (8, 128), 0)
    ahead, behind = turned(here)
    head = jnp.broadcast_to(zhi[y, pl.ds(x, 1), :], (8, 128))
    tail = jnp.broadcast_to(zlo[y, pl.ds(x, 1), :], (8, 128))
    return jnp.where(sublane == 7, head, ahead), jnp.where(sublane == 0, tail, behind)


def march(cells, column_at, cell, left):
    def run(start, first, last, left, mid):
        for k in range(first, last):
            right = column_at(start + k + 1)
            cell(start + k, left, mid, right)
            left, mid = mid, right
        return left, mid

    def body(i, carry):
        return run(pl.multiple_of(i * BLOCK, BLOCK), 0, BLOCK, *carry)

    if left is None:
        carry = run(0, 1, BLOCK, column_at(0), column_at(1))
    else:
        carry = run(0, 0, BLOCK, left, column_at(0))
    carry = lax.fori_loop(1, cells // BLOCK - 1, body, carry)
    return run(cells - BLOCK, 0, BLOCK - 1, *carry)


def reader(ref, *at):
    return lambda x: ref[(*at, x)]


def planes_of(refs, height):
    if len(refs) == 1:
        return [refs[0].at[y] for y in range(height)]
    low, inner, high = refs
    return [low, *(inner.at[y] for y in range(height - 2)), high]


def pack(plane, at):
    cells = plane.shape[0]
    return plane.reshape(cells * 8, 128)[pl.ds(at, cells, 8), :]


def inner_kernel(parts, height, *refs):
    field, (fy, fx, fz), out = refs[:parts], refs[parts : parts + 3], refs[parts + 3]
    cells = fy.shape[1]
    rows = [reader(plane) for plane in planes_of(field, height)]
    for start in range(1, height - 1, GROUP):
        ys = list(range(start, min(start + GROUP, height - 1)))

        def cell(x, left, mid, right, ys=ys):
            column = [rows[ys[0] - 1](x), *mid, rows[ys[-1] + 1](x)]
            for g, y in enumerate(ys):
                out[y - 1, x] = advance(
                    mid[g], column[g + 2], column[g], left[g], right[g], *turned(mid[g]), fy[y, x], fx[y, x], fz[y, x]
                )

        march(cells, lambda x, ys=ys: [rows[y](x) for y in ys], cell, None)


def mend_kernel(parts, height, *refs):
    field, (fy, fx, fz) = refs[:parts], refs[parts : parts + 3]
    (zlo, zhi), (first, last) = refs[parts + 3 : parts + 5], refs[parts + 5 : parts + 7]
    to_first, to_last = refs[parts + 7 : parts + 9]
    sides, out = refs[parts + 9 : parts + 11], refs[parts + 12]
    cells = fy.shape[1]
    rows = [reader(plane) for plane in planes_of(field, height)]
    for y in range(1, height - 1):
        flat = out.at[y - 1].reshape(cells * 8, 128)
        flat[pl.ds(0, cells, 8), :] += to_first[y] * (zlo[y] - last[y])
        flat[pl.ds(7, cells, 8), :] += to_last[y] * (zhi[y] - first[y])
        for x, left, right in (
            (0, sides[0][y], rows[y](1)),
            (cells - 1, rows[y](cells - 2), sides[1][y]),
        ):
            here = rows[y](x)
            out[y - 1, x] = advance(
                *(here, rows[y + 1](x), rows[y - 1](x), left, right),
                *along_z(here, zlo, zhi, y, x),
                *(fy[y, x], fx[y, x], fz[y, x]),
            )


def rim_kernel(parts, height, top, *refs):
    field, (fy, fx, fz) = refs[:parts], refs[parts : parts + 3]
    (zlo, zhi), sides = refs[parts + 3 : parts + 5], refs[parts + 5 : parts + 7]
    beyond, out = refs[parts + 7 :]
    cells = fy.shape[1]
    rows = [reader(plane) for plane in planes_of(field, height)]
    y = height - 1 if top else 0
    here = rows[y]
    above, below = (reader(beyond), rows[y - 1]) if top else (rows[1], reader(beyond))

    def cell(x, left, mid, right):
        out[x] = advance(
            mid, above(x), below(x), left, right, *along_z(mid, zlo, zhi, y, x), fy[y, x], fx[y, x], fz[y, x]
        )

    carry = march(cells, here, cell, sides[0][y])
    cell(cells - 1, *carry, sides[1][y])


def near_kernel(fz, to_first, to_last):
    for y in range(fz.shape[0]):
        to_first[y] = RATE + pack(fz.at[y], 0)
        to_last[y] = RATE - pack(fz.at[y], 7)


def rows_kernel(field, low, high, done):
    copies = [
        pltpu.make_async_copy(field.at[0], low, done.at[0]),
        pltpu.make_async_copy(field.at[field.shape[0] - 1], high, done.at[1]),
    ]
    for copy in copies:
        copy.start()
    for copy in copies:
        copy.wait()


def faces_kernel(parts, height, *refs):
    field, (first, last, left, right) = refs[:parts], refs[parts:]
    for y, plane in enumerate(planes_of(field, height)):
        first[y] = pack(plane, 0)
        last[y] = pack(plane, 7)
        left[y] = plane[0]
        right[y] = plane[plane.shape[0] - 1]


def running_sums(scale, plane, put):
    sublane = lax.broadcasted_iota(jnp.int32, (8, 128), 0)

    def body(i, carry):
        start = pl.multiple_of(i * BLOCK, BLOCK)
        for k in range(BLOCK):
            value = plane[start + k] * scale
            for reach in (1, 2, 4):
                value = value + jnp.where(sublane >= reach, pltpu.roll(value, reach, 0), 0.0)
            put(start + k, value)
        return carry

    lax.fori_loop(0, plane.shape[0] // BLOCK, body, 0)


def inner_sums_kernel(scale, inner, held, end, done):
    count = inner.shape[0]
    copy = pltpu.make_async_copy(inner, end.at[pl.ds(1, count)], done.at[0])
    copy.start()
    for y in range(count):

        def put(x, value, y=y):
            held[y, x] = value

        running_sums(scale, inner.at[y], put)
    copy.wait()


def rim_sums_kernel(scale, core, low, high, inner_held, end_in, own, other, held, end, done):
    half = own.shape[0]
    copies = [
        pltpu.make_async_copy(low, end.at[0], done.at[0]),
        pltpu.make_async_copy(high, end.at[2 * half - 1], done.at[1]),
    ]
    for copy in copies:
        copy.start()
    for k, plane in enumerate((low, high)):

        def put(x, value, k=k):
            held[k, x] = value

        running_sums(scale, plane, put)
    planes = planes_of((held.at[0], inner_held, held.at[1]), 2 * half)

    @pl.when(core[0] == 0)
    def _():
        for y in range(half):
            own[y] = pack(planes[y], 7)
            other[y] = pack(planes[half + y], 7)

    @pl.when(core[0] != 0)
    def _():
        for y in range(half):
            own[y] = pack(planes[half + y], 7)
            other[y] = pack(planes[y], 7)

    for copy in copies:
        copy.wait()


def add_kernel(a, b, out):
    out[...] = a[...] + b[...]


def before_kernel(pieces, out):
    so_far = jnp.zeros(pieces.shape[1:], jnp.float32)
    for k in range(pieces.shape[0]):
        out[k] = so_far
        so_far = so_far + pieces[k]


def split_kernel(core, chips, own, got, mine, partners):
    @pl.when(core[0] == 0)
    def _():
        mine[...] = chips[...]
        partners[...] = chips[...] + own[...]

    @pl.when(core[0] != 0)
    def _():
        mine[...] = chips[...] + got[...]
        partners[...] = chips[...]


def potential_kernel(core, inner_held, rim_held, mine, theirs, out, done_rows, done):
    half, cells = mine.shape[:2]
    planes = planes_of((rim_held.at[0], inner_held, rim_held.at[1]), 2 * half)

    def fill(y, before, j):
        def body(i, carry):
            start = pl.multiple_of(i * BLOCK, BLOCK)
            for k in range(BLOCK):
                x = start + k
                done_rows[y, x] = planes[y][x] + jnp.broadcast_to(before[j, pl.ds(x, 1), :], (8, 128))
            return carry

        lax.fori_loop(0, cells // BLOCK, body, 0)
        pltpu.make_async_copy(done_rows.at[y], out.at[y], done.at[y]).start()

    @pl.when(core[0] == 0)
    def _():
        for y in range(2 * half):
            fill(y, (mine, theirs)[y // half], y % half)

    @pl.when(core[0] != 0)
    def _():
        for y in range(2 * half):
            fill(y, (theirs, mine)[y // half], y % half)

    for y in range(2 * half):
        pltpu.make_async_copy(done_rows.at[y], out.at[y], done.at[y]).wait()


def sent(array, axis, by):
    size = lax.axis_size(axis)
    return lax.ppermute(array, axis, [(i, (i + by) % size) for i in range(size)])


def local(field_values, flow_y, flow_x, flow_z):
    core, field_values = lax.optimization_barrier((lax.axis_index("core").reshape(1), field_values))
    height, cells = field_values.shape[:2]
    flows = (flow_y, flow_x, flow_z)
    row, pair = shape(cells, 8, 128), shape(2, cells, 8, 128)
    inner = shape(height - 2, cells, 8, 128)
    whole = shape(*field_values.shape)
    edge, side = shape(height, cells, 128), shape(height, 8, 128)
    scalar = pl.BlockSpec(memory_space=pltpu.SMEM)

    def send_faces(field):
        first, last, left, right = call(
            functools.partial(faces_kernel, len(field), height), (edge, edge, side, side), *field
        )
        downs = sent(last, DOWN, 1), sent(first, DOWN, -1)
        sides = sent(right, "east", 1), sent(left, "east", -1)
        return (first, last), downs, sides

    def send_rim(low, high):
        return sent(high, "south", 1), sent(low, "south", -1)

    low, high = call(
        rows_kernel, (row, row), field_values, in_specs=[IN_HBM], scratch=[pltpu.SemaphoreType.DMA((2,))], vmem=52 << 20
    )
    slo, shi = send_rim(low, high)
    field = (field_values,)
    faces, downs, sides = send_faces(field)
    near = call(near_kernel, (edge, edge), flow_z)
    for step in range(1, STEPS + 1):
        parts = len(field)
        (mid,) = call(functools.partial(inner_kernel, parts, height), (inner,), *(*field, *flows), flops=1 << 23)
        (mid,) = call(
            functools.partial(mend_kernel, parts, height),
            (inner,),
            *(*field, *flows, *downs, *faces, *near, *sides, mid),
            alias={parts + 11: 0},
        )
        low, high = (
            call(
                functools.partial(rim_kernel, parts, height, top), (row,), *(*field, *flows, *downs, *sides, beyond)
            )[0]
            for top, beyond in ((False, slo), (True, shi))
        )
        field = (low, mid, high)
        if step < STEPS:
            slo, shi = send_rim(low, high)
            faces, downs, sides = send_faces(field)
    chips = lax.axis_size("chip")
    scale = 1.0 / (8 * chips * 2)
    inner_held, end = call(
        functools.partial(inner_sums_kernel, scale),
        (inner, whole),
        mid,
        out_specs=[IN_VMEM, IN_HBM],
        scratch=[pltpu.SemaphoreType.DMA((1,))],
    )
    quarter = shape(height // 2, cells, 128)
    own, other, rim_held, end = call(
        functools.partial(rim_sums_kernel, scale),
        (quarter, quarter, pair, whole),
        *(core, low, high, inner_held, end),
        in_specs=[scalar, *[IN_VMEM] * 3, IN_HBM],
        out_specs=[*[IN_VMEM] * 3, IN_HBM],
        scratch=[pltpu.SemaphoreType.DMA((2,))],
        alias={4: 3},
    )
    got = sent(other, "core", 1)
    (total,) = call(add_kernel, (quarter,), own, got)
    pieces = lax.all_to_all(total.reshape(chips, -1, 128), "chip", 0, 0, tiled=True)
    (pieces,) = call(before_kernel, (shape(*pieces.shape),), pieces)
    below = lax.all_to_all(pieces, "chip", 0, 0, tiled=True).reshape(total.shape)
    mine, partners = call(split_kernel, (quarter, quarter), core, below, own, got, in_specs=[scalar, *[IN_VMEM] * 3])
    theirs = sent(partners, "core", 1)
    (potential,) = call(
        potential_kernel,
        (whole,),
        *(core, inner_held, rim_held, mine, theirs),
        in_specs=[scalar, *[IN_VMEM] * 4],
        out_specs=[IN_HBM],
        scratch=[pltpu.VMEM(whole.shape, jnp.float32), pltpu.SemaphoreType.DMA((height,))],
    )
    return potential, end


def solution(mesh):
    finer = Mesh(
        mesh.devices.reshape(mesh.shape["south"], mesh.shape["east"], -1, 2), ("south", "east", "chip", "core")
    )
    spec = P("south", "east", DOWN, None)
    return jax.shard_map(local, mesh=finer, in_specs=(spec,) * 4, out_specs=(spec, spec), check_vma=False)
```

time: 103 us -> 110 us (1.068)
  waiting for transfers between devices: 11.8 us -> 24.1 us
  starting transfers between devices: 45.6 us -> 38.9 us
  blocking collectives: 24.7 us -> 26.4 us
    ppermute x26, waiting for transfers between devices: 11.8 us -> 24.1 us  [sent(): lax.ppermute(array, axis, [(i, (i + by) % size) for i in range(size)])]
    ppermute x26, starting transfers between devices: 45.6 us -> 38.9 us  [sent(): lax.ppermute(array, axis, [(i, (i + by) % size) for i in range(size)])]
    all_to_all x1, blocking collectives: 13.4 us -> 15.1 us  [local(): lax.all_to_all(total.reshape(chips, -1, 128), 'chip', 0, 0, tiled=True)]
    pallas_call x18 -> x28, Pallas kernels: 16 us -> 15.8 us  [call(): pl.pallas_call(kernel, out_shape=outs, in_specs=in_specs or [IN_VMEM] * l...]
  transfers between devices with their start and end apart: 26 -> 26, of which waited for: 9 -> 11; matrix products, arithmetic and copies ran while one was open for 0% -> 0% of each run, Pallas kernels for 8% -> 10%
where the time goes in v2:
time: 110 us
  starting transfers between devices  38.9 us (35%)
  blocking collectives  26.4 us (24%)
  waiting for transfers between devices  24.1 us (22%)
  Pallas kernels  15.8 us (14%)
  local copies, waits for them, and re-layouts  3.79 us (3%)
    ppermute x26, starting transfers between devices, sent(): lax.ppermute(array, axis, [(i, (i + by) % size) for i in range(size)])  38.9 us
    ppermute x26, waiting for transfers between devices, sent(): lax.ppermute(array, axis, [(i, (i + by) % size) for i in range(size)])  24.1 us
    pallas_call x28, Pallas kernels, call(): pl.pallas_call(kernel, out_shape=outs, in_specs=in_specs or [IN_VMEM] * l...  15.8 us
    all_to_all x1, blocking collectives, local(): lax.all_to_all(total.reshape(chips, -1, 128), 'chip', 0, 0, tiled=True)  15.1 us
    all_to_all x1, blocking collectives, local(): lax.all_to_all(pieces, 'chip', 0, 0, tiled=True).reshape(total.shape)  11.3 us
    unnamed x10, local copies, waits for them, and re-layouts  3.79 us
  transfers between devices with their start and end apart: 26, of which 11 were waited for; matrix products, arithmetic and copies ran while one was open for 0% of the time, Pallas kernels for 10%

profile of v2, /device:TPU:1, one launch (start us, length us, event | category | flops | bytes accessed | tf_op | source)
XLA Modules:
  0.0 110.0 jit_solution(17375576388217983541)
XLA Ops:
  0.6 1.9 %copy-done.3 = f32[8,96,8,128]{3,2,1,0:T(8,128)S(1)} copy-done((f32[8,96,8,128]{3,2,1,0:T(8,128)S(1)}, f32[8,96,8,128]{3,2,1,0:T(8,128)}, u32[]{:S(2)}) %copy-start.3) | copy-done | bytes 3145752
  2.7 3.0 %collective-permute-start = (f32[8,96,128]{2,1,0:T(8,128)S(1)}, f32[8,96,128]{2,1,0:T(8,128)S(1)}, u32[]{:S(2)}, u32[]{:S(2)}) collective-permute-start(f32[8,96,128]{2,1,0:T(8,128)S(1)} %get-tuple-element.34.refs_7_), channel_id=1, source_target_pairs={{0,1},{1,2},{2,3},{3,4},{4,5},{5,6},{6,7},{7,8},{8,9},{9,10},{10,1... | collective-permute-start | bytes 1179656 | tf_op jit(solution)/shard_map/ppermute | solution.py:292
  7.1 2.3 %collective-permute-start.5 = (f32[96,8,128]{2,1,0:T(8,128)S(1)}, f32[96,8,128]{2,1,0:T(8,128)S(1)}, u32[]{:S(2)}, u32[]{:S(2)}) collective-permute-start(f32[96,8,128]{2,1,0:T(8,128)S(1)} %get-tuple-element.41), channel_id=1, source_target_pairs={{0,192},{64,0},{128,64},{192,128},{1,193},{65,1},{129,65},{193,129... | collective-permute-start | bytes 1179656 | tf_op jit(solution)/shard_map/ppermute | solution.py:292
  10.7 3.0 %collective-permute-done.2.refs_6_.refs_10_ = f32[8,8,128]{2,1,0:T(8,128)S(1)} collective-permute-done((f32[8,8,128]{2,1,0:T(8,128)S(1)}, f32[8,8,128]{2,1,0:T(8,128)S(1)}, u32[]{:S(2)}, u32[]{:S(2)}) %collective-permute-start.2) | collective-permute-done | bytes 32800 | tf_op jit(solution)/shard_map/ppermute | solution.py:292
  15.4 1.9 %copy-done.4 = f32[8,96,8,128]{3,2,1,0:T(8,128)S(1)} copy-done((f32[8,96,8,128]{3,2,1,0:T(8,128)S(1)}, f32[8,96,8,128]{3,2,1,0:T(8,128)}, u32[]{:S(2)}) %copy-start.4) | copy-done | bytes 3145752
  20.0 4.5 %collective-permute-start.6 = (f32[8,96,128]{2,1,0:T(8,128)S(1)}, f32[8,96,128]{2,1,0:T(8,128)S(1)}, u32[]{:S(2)}, u32[]{:S(2)}) collective-permute-start(f32[8,96,128]{2,1,0:T(8,128)S(1)} %get-tuple-element.42.refs_9_), channel_id=1, source_target_pairs={{0,1},{1,2},{2,3},{3,4},{4,5},{5,6},{6,7},{7,8},{8,9},{9,10},{10,1... | collective-permute-start | bytes 1179656 | tf_op jit(solution)/shard_map/ppermute | solution.py:292
  25.2 3.0 %collective-permute-start.11 = (f32[96,8,128]{2,1,0:T(8,128)S(1)}, f32[96,8,128]{2,1,0:T(8,128)S(1)}, u32[]{:S(2)}, u32[]{:S(2)}) collective-permute-start(f32[96,8,128]{2,1,0:T(8,128)S(1)} %shard_map.61.refs_0_), channel_id=1, source_target_pairs={{0,192},{64,0},{128,64},{192,128},{1,193},{65,1},{129,65},{193,129... | collective-permute-start | bytes 1179656 | tf_op jit(solution)/shard_map/ppermute | solution.py:292
  28.2 4.3 %collective-permute-done.8.refs_8_.refs_12_ = f32[8,8,128]{2,1,0:T(8,128)S(1)} collective-permute-done((f32[8,8,128]{2,1,0:T(8,128)S(1)}, f32[8,8,128]{2,1,0:T(8,128)S(1)}, u32[]{:S(2)}, u32[]{:S(2)}) %collective-permute-start.8) | collective-permute-done | bytes 32800 | tf_op jit(solution)/shard_map/ppermute | solution.py:292
  32.4 1.5 %shard_map.68.refs_14_ = f32[6,96,8,128]{3,2,1,0:T(8,128)S(1)} custom-call(f32[96,8,128]{2,1,0:T(8,128)S(1)} %shard_map.61.refs_0_, f32[6,96,8,128]{3,2,1,0:T(8,128)S(1)} %shard_map.64.refs_1_, f32[96,8,128]{2,1,0:T(8,128)S(1)} %shard_map.65.refs_2_, f32[8,96,8,128]{3,2,1,0:T(8,128)S(1)} %copy-done.1, f32[8,96,8,128]{3,2,1,0:T(8,128)S(1)} %copy-done.2, ...), custom_call_target="tpu_custom_call" | custom-call | flops 8388608 | tf_op jit(solution)/shard_map/pallas_call | solution.py:28
  34.0 1.5 %collective-permute-done.9.refs_9_.refs_13_ = f32[8,8,128]{2,1,0:T(8,128)S(1)} collective-permute-done((f32[8,8,128]{2,1,0:T(8,128)S(1)}, f32[8,8,128]{2,1,0:T(8,128)S(1)}, u32[]{:S(2)}, u32[]{:S(2)}) %collective-permute-start.9) | collective-permute-done | bytes 32800 | tf_op jit(solution)/shard_map/ppermute | solution.py:292
  37.3 3.5 %collective-permute-start.12 = (f32[8,96,128]{2,1,0:T(8,128)S(1)}, f32[8,96,128]{2,1,0:T(8,128)S(1)}, u32[]{:S(2)}, u32[]{:S(2)}) collective-permute-start(f32[8,96,128]{2,1,0:T(8,128)S(1)} %get-tuple-element.46.refs_9_), channel_id=1, source_target_pairs={{0,1},{1,2},{2,3},{3,4},{4,5},{5,6},{6,7},{7,8},{8,9},{9,10},{10,1... | collective-permute-start | bytes 1179656 | tf_op jit(solution)/shard_map/ppermute | solution.py:292
  41.6 3.0 %collective-permute-start.17 = (f32[96,8,128]{2,1,0:T(8,128)S(1)}, f32[96,8,128]{2,1,0:T(8,128)S(1)}, u32[]{:S(2)}, u32[]{:S(2)}) collective-permute-start(f32[96,8,128]{2,1,0:T(8,128)S(1)} %shard_map.67.refs_0_), channel_id=1, source_target_pairs={{0,192},{64,0},{128,64},{192,128},{1,193},{65,1},{129,65},{193,129... | collective-permute-start | bytes 1179656 | tf_op jit(solution)/shard_map/ppermute | solution.py:292
  44.5 4.3 %collective-permute-done.14.refs_8_.refs_12_ = f32[8,8,128]{2,1,0:T(8,128)S(1)} collective-permute-done((f32[8,8,128]{2,1,0:T(8,128)S(1)}, f32[8,8,128]{2,1,0:T(8,128)S(1)}, u32[]{:S(2)}, u32[]{:S(2)}) %collective-permute-start.14) | collective-permute-done | bytes 32800 | tf_op jit(solution)/shard_map/ppermute | solution.py:292
  48.8 1.5 %shard_map.73.refs_14_ = f32[6,96,8,128]{3,2,1,0:T(8,128)S(1)} custom-call(f32[96,8,128]{2,1,0:T(8,128)S(1)} %shard_map.67.refs_0_, f32[6,96,8,128]{3,2,1,0:T(8,128)S(1)} %shard_map.69.refs_1_, f32[96,8,128]{2,1,0:T(8,128)S(1)} %shard_map.70.refs_2_, f32[8,96,8,128]{3,2,1,0:T(8,128)S(1)} %copy-done.1, f32[8,96,8,128]{3,2,1,0:T(8,128)S(1)} %copy-done.2, ...), custom_call_target="tpu_custom_call" | custom-call | flops 8388608 | tf_op jit(solution)/shard_map/pallas_call | solution.py:28
  50.3 1.5 %collective-permute-done.15.refs_9_.refs_13_ = f32[8,8,128]{2,1,0:T(8,128)S(1)} collective-permute-done((f32[8,8,128]{2,1,0:T(8,128)S(1)}, f32[8,8,128]{2,1,0:T(8,128)S(1)}, u32[]{:S(2)}, u32[]{:S(2)}) %collective-permute-start.15) | collective-permute-done | bytes 32800 | tf_op jit(solution)/shard_map/ppermute | solution.py:292
  53.7 2.9 %collective-permute-start.18 = (f32[8,96,128]{2,1,0:T(8,128)S(1)}, f32[8,96,128]{2,1,0:T(8,128)S(1)}, u32[]{:S(2)}, u32[]{:S(2)}) collective-permute-start(f32[8,96,128]{2,1,0:T(8,128)S(1)} %get-tuple-element.50.refs_9_), channel_id=1, source_target_pairs={{0,1},{1,2},{2,3},{3,4},{4,5},{5,6},{6,7},{7,8},{8,9},{9,10},{10,1... | collective-permute-start | bytes 1179656 | tf_op jit(solution)/shard_map/ppermute | solution.py:292
  57.9 3.0 %collective-permute-start.23 = (f32[96,8,128]{2,1,0:T(8,128)S(1)}, f32[96,8,128]{2,1,0:T(8,128)S(1)}, u32[]{:S(2)}, u32[]{:S(2)}) collective-permute-start(f32[96,8,128]{2,1,0:T(8,128)S(1)} %shard_map.72.refs_0_), channel_id=1, source_target_pairs={{0,192},{64,0},{128,64},{192,128},{1,193},{65,1},{129,65},{193,129... | collective-permute-start | bytes 1179656 | tf_op jit(solution)/shard_map/ppermute | solution.py:292
  60.9 4.3 %collective-permute-done.20.refs_12_.refs_8_ = f32[8,8,128]{2,1,0:T(8,128)S(1)} collective-permute-done((f32[8,8,128]{2,1,0:T(8,128)S(1)}, f32[8,8,128]{2,1,0:T(8,128)S(1)}, u32[]{:S(2)}, u32[]{:S(2)}) %collective-permute-start.20) | collective-permute-done | bytes 32800 | tf_op jit(solution)/shard_map/ppermute | solution.py:292
  66.7 1.5 %collective-permute-done.21.refs_13_.refs_9_ = f32[8,8,128]{2,1,0:T(8,128)S(1)} collective-permute-done((f32[8,8,128]{2,1,0:T(8,128)S(1)}, f32[8,8,128]{2,1,0:T(8,128)S(1)}, u32[]{:S(2)}, u32[]{:S(2)}) %collective-permute-start.21) | collective-permute-done | bytes 32800 | tf_op jit(solution)/shard_map/ppermute | solution.py:292
  71.5 5.0 %collective-permute-start.24 = (f32[4,96,128]{2,1,0:T(8,128)S(1)}, f32[4,96,128]{2,1,0:T(8,128)S(1)}, u32[]{:S(2)}, u32[]{:S(2)}) collective-permute-start(f32[4,96,128]{2,1,0:T(8,128)S(1)} %get-tuple-element.58), channel_id=1, source_target_pairs={{0,1},{1,0},{2,3},{3,2},{4,5},{5,4},{6,7},{7,6},{8,9},{9,8},{10,11... | collective-permute-start | bytes 589832 | tf_op jit(solution)/shard_map/ppermute | solution.py:292
  77.6 15.1 %all_to_all.10.pieces = f32[8,48,128]{2,1,0:T(8,128)S(1)} all-to-all(f32[8,48,128]{2,1,0:T(8,128)S(1)} %bitcast.4), channel_id=1, replica_groups=mesh['south'=4,'east'=4,'chip'=8,'core'=2] {'chip'}, dimensions={0} | all-to-all | bytes 393216 | tf_op jit(solution)/shard_map/all_to_all | solution.py:363
  92.7 11.3 %all_to_all.11 = f32[8,48,128]{2,1,0:T(8,128)S(1)} all-to-all(f32[8,48,128]{2,1,0:T(8,128)S(1)} %shard_map.84), channel_id=1, replica_groups=mesh['south'=4,'east'=4,'chip'=8,'core'=2] {'chip'}, dimensions={0} | all-to-all | bytes 393216 | tf_op jit(solution)/shard_map/all_to_all | solution.py:365
  104.0 2.9 %collective-permute-start.25 = (f32[4,96,128]{2,1,0:T(8,128)S(1)}, f32[4,96,128]{2,1,0:T(8,128)S(1)}, u32[]{:S(2)}, u32[]{:S(2)}) collective-permute-start(f32[4,96,128]{2,1,0:T(8,128)S(1)} %get-tuple-element.60), channel_id=1, source_target_pairs={{0,1},{1,0},{2,3},{3,2},{4,5},{5,4},{6,7},{7,6},{8,9},{9,8},{10,11... | collective-permute-start | bytes 589832 | tf_op jit(solution)/shard_map/ppermute | solution.py:292
  108.0 1.8 %shard_map.86 = f32[8,96,8,128]{3,2,1,0:T(8,128)} custom-call(s32[1]{0:T(128)} %bitcast.core, f32[6,96,8,128]{3,2,1,0:T(8,128)S(1)} %get-tuple-element.54.inner_held, f32[2,96,8,128]{3,2,1,0:T(8,128)S(1)} %get-tuple-element.56.rim_held, f32[4,96,128]{2,1,0:T(8,128)S(1)} %get-tuple-element.59.mine, f32[4,96,128]{2,1,0:T(8,128)S(1)} %collective-permute-done.25.theirs), custom_call_target="tpu_custom_call" | custom-call | flops 2097152 | tf_op jit(solution)/shard_map/pallas_call | solution.py:28
  (68 shorter events, 20.5 us)
Async XLA Ops:
  2.7 16.1 %collective-permute-start = (f32[8,96,128]{2,1,0:T(8,128)S(1)}, f32[8,96,128]{2,1,0:T(8,128)S(1)}, u32[]{:S(2)}, u32[]{:S(2)}) collective-permute-start(f32[8,96,128]{2,1,0:T(8,128)S(1)} %get-tuple-element.34.refs_7_), channel_id=1, source_target_pairs={{0,1},{1,2},{2,3},{3,4},{4,5},{5,6},{6,7},{7,8},{8,9},{9,10},{10,1... | collective-permute-start | bytes 1179656 | tf_op jit(solution)/shard_map/ppermute | solution.py:292
  5.7 13.1 %collective-permute-start.1 = (f32[8,96,128]{2,1,0:T(8,128)S(1)}, f32[8,96,128]{2,1,0:T(8,128)S(1)}, u32[]{:S(2)}, u32[]{:S(2)}) collective-permute-start(f32[8,96,128]{2,1,0:T(8,128)S(1)} %get-tuple-element.35.refs_6_), channel_id=1, source_target_pairs={{0,15},{1,0},{2,1},{3,2},{4,3},{5,4},{6,5},{7,6},{8,7},{9,8},{10,9... | collective-permute-start | bytes 1179656 | tf_op jit(solution)/shard_map/ppermute | solution.py:292
  7.1 11.8 %collective-permute-start.5 = (f32[96,8,128]{2,1,0:T(8,128)S(1)}, f32[96,8,128]{2,1,0:T(8,128)S(1)}, u32[]{:S(2)}, u32[]{:S(2)}) collective-permute-start(f32[96,8,128]{2,1,0:T(8,128)S(1)} %get-tuple-element.41), channel_id=1, source_target_pairs={{0,192},{64,0},{128,64},{192,128},{1,193},{65,1},{129,65},{193,129... | collective-permute-start | bytes 1179656 | tf_op jit(solution)/shard_map/ppermute | solution.py:292
  9.4 9.8 %collective-permute-start.4 = (f32[96,8,128]{2,1,0:T(8,128)S(1)}, f32[96,8,128]{2,1,0:T(8,128)S(1)}, u32[]{:S(2)}, u32[]{:S(2)}) collective-permute-start(f32[96,8,128]{2,1,0:T(8,128)S(1)} %get-tuple-element.38), channel_id=1, source_target_pairs={{0,64},{64,128},{128,192},{192,0},{1,65},{65,129},{129,193},{193,1... | collective-permute-start | bytes 1179656 | tf_op jit(solution)/shard_map/ppermute | solution.py:292
  9.4 4.3 %collective-permute-start.2 = (f32[8,8,128]{2,1,0:T(8,128)S(1)}, f32[8,8,128]{2,1,0:T(8,128)S(1)}, u32[]{:S(2)}, u32[]{:S(2)}) collective-permute-start(f32[8,8,128]{2,1,0:T(8,128)S(1)} %get-tuple-element.36), channel_id=1, source_target_pairs={{0,16},{16,32},{32,48},{48,0},{1,17},{17,33},{33,49},{49,1},{2,18}... | collective-permute-start | bytes 98312 | tf_op jit(solution)/shard_map/ppermute | solution.py:292
  13.8 5.1 %collective-permute-start.3 = (f32[8,8,128]{2,1,0:T(8,128)S(1)}, f32[8,8,128]{2,1,0:T(8,128)S(1)}, u32[]{:S(2)}, u32[]{:S(2)}) collective-permute-start(f32[8,8,128]{2,1,0:T(8,128)S(1)} %get-tuple-element.37), channel_id=1, source_target_pairs={{0,48},{16,0},{32,16},{48,32},{1,49},{17,1},{33,17},{49,33},{2,50}... | collective-permute-start | bytes 98312 | tf_op jit(solution)/shard_map/ppermute | solution.py:292
  20.0 15.5 %collective-permute-start.6 = (f32[8,96,128]{2,1,0:T(8,128)S(1)}, f32[8,96,128]{2,1,0:T(8,128)S(1)}, u32[]{:S(2)}, u32[]{:S(2)}) collective-permute-start(f32[8,96,128]{2,1,0:T(8,128)S(1)} %get-tuple-element.42.refs_9_), channel_id=1, source_target_pairs={{0,1},{1,2},{2,3},{3,4},{4,5},{5,6},{6,7},{7,8},{8,9},{9,10},{10,1... | collective-permute-start | bytes 1179656 | tf_op jit(solution)/shard_map/ppermute | solution.py:292
  24.4 11.1 %collective-permute-start.7 = (f32[8,96,128]{2,1,0:T(8,128)S(1)}, f32[8,96,128]{2,1,0:T(8,128)S(1)}, u32[]{:S(2)}, u32[]{:S(2)}) collective-permute-start(f32[8,96,128]{2,1,0:T(8,128)S(1)} %get-tuple-element.43.refs_8_), channel_id=1, source_target_pairs={{0,15},{1,0},{2,1},{3,2},{4,3},{5,4},{6,5},{7,6},{8,7},{9,8},{10,9... | collective-permute-start | bytes 1179656 | tf_op jit(solution)/shard_map/ppermute | solution.py:292
  25.2 10.3 %collective-permute-start.11 = (f32[96,8,128]{2,1,0:T(8,128)S(1)}, f32[96,8,128]{2,1,0:T(8,128)S(1)}, u32[]{:S(2)}, u32[]{:S(2)}) collective-permute-start(f32[96,8,128]{2,1,0:T(8,128)S(1)} %shard_map.61.refs_0_), channel_id=1, source_target_pairs={{0,192},{64,0},{128,64},{192,128},{1,193},{65,1},{129,65},{193,129... | collective-permute-start | bytes 1179656 | tf_op jit(solution)/shard_map/ppermute | solution.py:292
  28.2 8.7 %collective-permute-start.10 = (f32[96,8,128]{2,1,0:T(8,128)S(1)}, f32[96,8,128]{2,1,0:T(8,128)S(1)}, u32[]{:S(2)}, u32[]{:S(2)}) collective-permute-start(f32[96,8,128]{2,1,0:T(8,128)S(1)} %shard_map.65.refs_2_), channel_id=1, source_target_pairs={{0,64},{64,128},{128,192},{192,0},{1,65},{65,129},{129,193},{193,1... | collective-permute-start | bytes 1179656 | tf_op jit(solution)/shard_map/ppermute | solution.py:292
  28.2 4.3 %collective-permute-start.8 = (f32[8,8,128]{2,1,0:T(8,128)S(1)}, f32[8,8,128]{2,1,0:T(8,128)S(1)}, u32[]{:S(2)}, u32[]{:S(2)}) collective-permute-start(f32[8,8,128]{2,1,0:T(8,128)S(1)} %get-tuple-element.44), channel_id=1, source_target_pairs={{0,16},{16,32},{32,48},{48,0},{1,17},{17,33},{33,49},{49,1},{2,18}... | collective-permute-start | bytes 98312 | tf_op jit(solution)/shard_map/ppermute | solution.py:292
  37.3 14.5 %collective-permute-start.12 = (f32[8,96,128]{2,1,0:T(8,128)S(1)}, f32[8,96,128]{2,1,0:T(8,128)S(1)}, u32[]{:S(2)}, u32[]{:S(2)}) collective-permute-start(f32[8,96,128]{2,1,0:T(8,128)S(1)} %get-tuple-element.46.refs_9_), channel_id=1, source_target_pairs={{0,1},{1,2},{2,3},{3,4},{4,5},{5,6},{6,7},{7,8},{8,9},{9,10},{10,1... | collective-permute-start | bytes 1179656 | tf_op jit(solution)/shard_map/ppermute | solution.py:292
  40.9 11.0 %collective-permute-start.13 = (f32[8,96,128]{2,1,0:T(8,128)S(1)}, f32[8,96,128]{2,1,0:T(8,128)S(1)}, u32[]{:S(2)}, u32[]{:S(2)}) collective-permute-start(f32[8,96,128]{2,1,0:T(8,128)S(1)} %get-tuple-element.47.refs_8_), channel_id=1, source_target_pairs={{0,15},{1,0},{2,1},{3,2},{4,3},{5,4},{6,5},{7,6},{8,7},{9,8},{10,9... | collective-permute-start | bytes 1179656 | tf_op jit(solution)/shard_map/ppermute | solution.py:292
  41.6 10.3 %collective-permute-start.17 = (f32[96,8,128]{2,1,0:T(8,128)S(1)}, f32[96,8,128]{2,1,0:T(8,128)S(1)}, u32[]{:S(2)}, u32[]{:S(2)}) collective-permute-start(f32[96,8,128]{2,1,0:T(8,128)S(1)} %shard_map.67.refs_0_), channel_id=1, source_target_pairs={{0,192},{64,0},{128,64},{192,128},{1,193},{65,1},{129,65},{193,129... | collective-permute-start | bytes 1179656 | tf_op jit(solution)/shard_map/ppermute | solution.py:292
  44.5 8.7 %collective-permute-start.16 = (f32[96,8,128]{2,1,0:T(8,128)S(1)}, f32[96,8,128]{2,1,0:T(8,128)S(1)}, u32[]{:S(2)}, u32[]{:S(2)}) collective-permute-start(f32[96,8,128]{2,1,0:T(8,128)S(1)} %shard_map.70.refs_2_), channel_id=1, source_target_pairs={{0,64},{64,128},{128,192},{192,0},{1,65},{65,129},{129,193},{193,1... | collective-permute-start | bytes 1179656 | tf_op jit(solution)/shard_map/ppermute | solution.py:292
  44.5 4.3 %collective-permute-start.14 = (f32[8,8,128]{2,1,0:T(8,128)S(1)}, f32[8,8,128]{2,1,0:T(8,128)S(1)}, u32[]{:S(2)}, u32[]{:S(2)}) collective-permute-start(f32[8,8,128]{2,1,0:T(8,128)S(1)} %get-tuple-element.48), channel_id=1, source_target_pairs={{0,16},{16,32},{32,48},{48,0},{1,17},{17,33},{33,49},{49,1},{2,18}... | collective-permute-start | bytes 98312 | tf_op jit(solution)/shard_map/ppermute | solution.py:292
  48.8 3.1 %collective-permute-start.15 = (f32[8,8,128]{2,1,0:T(8,128)S(1)}, f32[8,8,128]{2,1,0:T(8,128)S(1)}, u32[]{:S(2)}, u32[]{:S(2)}) collective-permute-start(f32[8,8,128]{2,1,0:T(8,128)S(1)} %get-tuple-element.49), channel_id=1, source_target_pairs={{0,48},{16,0},{32,16},{48,32},{1,49},{17,1},{33,17},{49,33},{2,50}... | collective-permute-start | bytes 98312 | tf_op jit(solution)/shard_map/ppermute | solution.py:292
  53.7 14.5 %collective-permute-start.18 = (f32[8,96,128]{2,1,0:T(8,128)S(1)}, f32[8,96,128]{2,1,0:T(8,128)S(1)}, u32[]{:S(2)}, u32[]{:S(2)}) collective-permute-start(f32[8,96,128]{2,1,0:T(8,128)S(1)} %get-tuple-element.50.refs_9_), channel_id=1, source_target_pairs={{0,1},{1,2},{2,3},{3,4},{4,5},{5,6},{6,7},{7,8},{8,9},{9,10},{10,1... | collective-permute-start | bytes 1179656 | tf_op jit(solution)/shard_map/ppermute | solution.py:292
  56.6 11.7 %collective-permute-start.19 = (f32[8,96,128]{2,1,0:T(8,128)S(1)}, f32[8,96,128]{2,1,0:T(8,128)S(1)}, u32[]{:S(2)}, u32[]{:S(2)}) collective-permute-start(f32[8,96,128]{2,1,0:T(8,128)S(1)} %get-tuple-element.51.refs_8_), channel_id=1, source_target_pairs={{0,15},{1,0},{2,1},{3,2},{4,3},{5,4},{6,5},{7,6},{8,7},{9,8},{10,9... | collective-permute-start | bytes 1179656 | tf_op jit(solution)/shard_map/ppermute | solution.py:292
  57.9 12.0 %collective-permute-start.23 = (f32[96,8,128]{2,1,0:T(8,128)S(1)}, f32[96,8,128]{2,1,0:T(8,128)S(1)}, u32[]{:S(2)}, u32[]{:S(2)}) collective-permute-start(f32[96,8,128]{2,1,0:T(8,128)S(1)} %shard_map.72.refs_0_), channel_id=1, source_target_pairs={{0,192},{64,0},{128,64},{192,128},{1,193},{65,1},{129,65},{193,129... | collective-permute-start | bytes 1179656 | tf_op jit(solution)/shard_map/ppermute | solution.py:292
  60.9 9.4 %collective-permute-start.22 = (f32[96,8,128]{2,1,0:T(8,128)S(1)}, f32[96,8,128]{2,1,0:T(8,128)S(1)}, u32[]{:S(2)}, u32[]{:S(2)}) collective-permute-start(f32[96,8,128]{2,1,0:T(8,128)S(1)} %shard_map.75.refs_2_), channel_id=1, source_target_pairs={{0,64},{64,128},{128,192},{192,0},{1,65},{65,129},{129,193},{193,1... | collective-permute-start | bytes 1179656 | tf_op jit(solution)/shard_map/ppermute | solution.py:292
  60.9 4.3 %collective-permute-start.20 = (f32[8,8,128]{2,1,0:T(8,128)S(1)}, f32[8,8,128]{2,1,0:T(8,128)S(1)}, u32[]{:S(2)}, u32[]{:S(2)}) collective-permute-start(f32[8,8,128]{2,1,0:T(8,128)S(1)} %get-tuple-element.52), channel_id=1, source_target_pairs={{0,16},{16,32},{32,48},{48,0},{1,17},{17,33},{33,49},{49,1},{2,18}... | collective-permute-start | bytes 98312 | tf_op jit(solution)/shard_map/ppermute | solution.py:292
  71.5 6.1 %collective-permute-start.24 = (f32[4,96,128]{2,1,0:T(8,128)S(1)}, f32[4,96,128]{2,1,0:T(8,128)S(1)}, u32[]{:S(2)}, u32[]{:S(2)}) collective-permute-start(f32[4,96,128]{2,1,0:T(8,128)S(1)} %get-tuple-element.58), channel_id=1, source_target_pairs={{0,1},{1,0},{2,3},{3,2},{4,5},{5,4},{6,7},{7,6},{8,9},{9,8},{10,11... | collective-permute-start | bytes 589832 | tf_op jit(solution)/shard_map/ppermute | solution.py:292
  104.0 4.0 %collective-permute-start.25 = (f32[4,96,128]{2,1,0:T(8,128)S(1)}, f32[4,96,128]{2,1,0:T(8,128)S(1)}, u32[]{:S(2)}, u32[]{:S(2)}) collective-permute-start(f32[4,96,128]{2,1,0:T(8,128)S(1)} %get-tuple-element.60), channel_id=1, source_target_pairs={{0,1},{1,0},{2,3},{3,2},{4,5},{5,4},{6,7},{7,6},{8,9},{9,8},{10,11... | collective-permute-start | bytes 589832 | tf_op jit(solution)/shard_map/ppermute | solution.py:292
  (7 other events, 43.7 us)

commit v3 on v2

--- a/solution.py
+++ b/solution.py
@@ -203,14 +203,8 @@
     copy.wait()
 
 
-def rim_sums_kernel(scale, core, low, high, inner_held, end_in, own, other, held, end, done):
+def rim_sums_kernel(scale, core, low, high, inner_held, own, other, held):
     half = own.shape[0]
-    copies = [
-        pltpu.make_async_copy(low, end.at[0], done.at[0]),
-        pltpu.make_async_copy(high, end.at[2 * half - 1], done.at[1]),
-    ]
-    for copy in copies:
-        copy.start()
     for k, plane in enumerate((low, high)):
 
         def put(x, value, k=k):
@@ -230,9 +224,6 @@
         for y in range(half):
             own[y] = pack(planes[half + y], 7)
             other[y] = pack(planes[y], 7)
-
-    for copy in copies:
-        copy.wait()
 
 
 def add_kernel(a, b, out):
@@ -258,33 +249,49 @@
         partners[...] = chips[...]
 
 
-def potential_kernel(core, inner_held, rim_held, mine, theirs, out, done_rows, done):
-    half, cells = mine.shape[:2]
+def half_potential(side, inner_held, rim_held, before, out, filled, done):
+    half, cells = before.shape[:2]
     planes = planes_of((rim_held.at[0], inner_held, rim_held.at[1]), 2 * half)
 
-    def fill(y, before, j):
-        def body(i, carry):
-            start = pl.multiple_of(i * BLOCK, BLOCK)
-            for k in range(BLOCK):
-                x = start + k
-                done_rows[y, x] = planes[y][x] + jnp.broadcast_to(before[j, pl.ds(x, 1), :], (8, 128))
-            return carry
-
-        lax.fori_loop(0, cells // BLOCK, body, 0)
-        pltpu.make_async_copy(done_rows.at[y], out.at[y], done.at[y]).start()
-
-    @pl.when(core[0] == 0)
-    def _():
-        for y in range(2 * half):
-            fill(y, (mine, theirs)[y // half], y % half)
-
-    @pl.when(core[0] != 0)
-    def _():
-        for y in range(2 * half):
-            fill(y, (theirs, mine)[y // half], y % half)
-
-    for y in range(2 * half):
-        pltpu.make_async_copy(done_rows.at[y], out.at[y], done.at[y]).wait()
+    def fill(which):
+        for j in range(half):
+            y = which * half + j
+
+            def body(i, carry, y=y, j=j):
+                start = pl.multiple_of(i * BLOCK, BLOCK)
+                for k in range(BLOCK):
+                    x = start + k
+                    filled[j, x] = planes[y][x] + jnp.broadcast_to(before[j, pl.ds(x, 1), :], (8, 128))
+                return carry
+
+            lax.fori_loop(0, cells // BLOCK, body, 0)
+            pltpu.make_async_copy(filled.at[j], out.at[y], done.at[j]).start()
+        for j in range(half):
+            pltpu.make_async_copy(filled.at[j], out.at[which * half + j], done.at[j]).wait()
+
+    @pl.when(side == 0)
+    def _():
+        fill(0)
+
+    @pl.when(side != 0)
+    def _():
+        fill(1)
+
+
+def own_half_kernel(core, low, high, inner_held, rim_held, before, end_in, out, end, filled, done, done_rims):
+    copies = [
+        pltpu.make_async_copy(low, end.at[0], done_rims.at[0]),
+        pltpu.make_async_copy(high, end.at[end.shape[0] - 1], done_rims.at[1]),
+    ]
+    for copy in copies:
+        copy.start()
+    half_potential(core[0], inner_held, rim_held, before, out, filled, done)
+    for copy in copies:
+        copy.wait()
+
+
+def other_half_kernel(core, inner_held, rim_held, before, out_in, out, filled, done):
+    half_potential(1 - core[0], inner_held, rim_held, before, out, filled, done)
 
 
 def sent(array, axis, by):
@@ -314,7 +321,7 @@
         return sent(high, "south", 1), sent(low, "south", -1)
 
     low, high = call(
-        rows_kernel, (row, row), field_values, in_specs=[IN_HBM], scratch=[pltpu.SemaphoreType.DMA((2,))], vmem=52 << 20
+        rows_kernel, (row, row), field_values, in_specs=[IN_HBM], scratch=[pltpu.SemaphoreType.DMA((2,))], vmem=48 << 20
     )
     slo, shi = send_rim(low, high)
     field = (field_values,)
@@ -349,14 +356,11 @@
         scratch=[pltpu.SemaphoreType.DMA((1,))],
     )
     quarter = shape(height // 2, cells, 128)
-    own, other, rim_held, end = call(
+    own, other, rim_held = call(
         functools.partial(rim_sums_kernel, scale),
-        (quarter, quarter, pair, whole),
-        *(core, low, high, inner_held, end),
-        in_specs=[scalar, *[IN_VMEM] * 3, IN_HBM],
-        out_specs=[*[IN_VMEM] * 3, IN_HBM],
-        scratch=[pltpu.SemaphoreType.DMA((2,))],
-        alias={4: 3},
+        (quarter, quarter, pair),
+        *(core, low, high, inner_held),
+        in_specs=[scalar, *[IN_VMEM] * 3],
     )
     got = sent(other, "core", 1)
     (total,) = call(add_kernel, (quarter,), own, got)
@@ -365,13 +369,24 @@
     below = lax.all_to_all(pieces, "chip", 0, 0, tiled=True).reshape(total.shape)
     mine, partners = call(split_kernel, (quarter, quarter), core, below, own, got, in_specs=[scalar, *[IN_VMEM] * 3])
     theirs = sent(partners, "core", 1)
+    rows_out = [pltpu.VMEM((height // 2, cells, 8, 128), jnp.float32), pltpu.SemaphoreType.DMA((height // 2,))]
+    potential, end = call(
+        own_half_kernel,
+        (whole, whole),
+        *(core, low, high, inner_held, rim_held, mine, end),
+        in_specs=[scalar, *[IN_VMEM] * 5, IN_HBM],
+        out_specs=[IN_HBM, IN_HBM],
+        scratch=[*rows_out, pltpu.SemaphoreType.DMA((2,))],
+        alias={6: 1},
+    )
     (potential,) = call(
-        potential_kernel,
+        other_half_kernel,
         (whole,),
-        *(core, inner_held, rim_held, mine, theirs),
-        in_specs=[scalar, *[IN_VMEM] * 4],
+        *(core, inner_held, rim_held, theirs, potential),
+        in_specs=[scalar, *[IN_VMEM] * 3, IN_HBM],
         out_specs=[IN_HBM],
-        scratch=[pltpu.VMEM(whole.shape, jnp.float32), pltpu.SemaphoreType.DMA((height,))],
+        scratch=rows_out,
+        alias={4: 0},
     )
     return potential, end
 

time: 110 us -> 106 us (0.964)
  waiting for transfers between devices: 24.1 us -> 18.4 us
  starting transfers between devices: 38.9 us -> 42.6 us
  local copies, waits for them, and re-layouts: 3.79 us -> 1.9 us
    ppermute x26, waiting for transfers between devices: 24.1 us -> 18.4 us  [sent(): lax.ppermute(array, axis, [(i, (i + by) % size) for i in range(size)])]
    ppermute x26, starting transfers between devices: 38.9 us -> 42.6 us  [sent(): lax.ppermute(array, axis, [(i, (i + by) % size) for i in range(size)])]
    unnamed x10 -> x8, local copies, waits for them, and re-layouts: 3.79 us -> 1.9 us
    pallas_call x28 -> x29, Pallas kernels: 15.8 us -> 15.6 us  [call(): pl.pallas_call(kernel, out_shape=outs, in_specs=in_specs or [IN_VMEM] * l...]
  transfers between devices with their start and end apart: 26 -> 26, of which waited for: 11 -> 10; matrix products, arithmetic and copies ran while one was open for 0% -> 0% of each run, Pallas kernels for 10% -> 12%
where the time goes in v3:
time: 106 us
  starting transfers between devices  42.6 us (40%)
  blocking collectives  26.6 us (25%)
  waiting for transfers between devices  18.4 us (17%)
  Pallas kernels  15.6 us (15%)
  local copies, waits for them, and re-layouts  1.9 us (2%)
    ppermute x26, starting transfers between devices, sent(): lax.ppermute(array, axis, [(i, (i + by) % size) for i in range(size)])  42.6 us
    ppermute x26, waiting for transfers between devices, sent(): lax.ppermute(array, axis, [(i, (i + by) % size) for i in range(size)])  18.4 us
    pallas_call x29, Pallas kernels, call(): pl.pallas_call(kernel, out_shape=outs, in_specs=in_specs or [IN_VMEM] * l...  15.6 us
    all_to_all x1, blocking collectives, local(): lax.all_to_all(total.reshape(chips, -1, 128), 'chip', 0, 0, tiled=True)  15.3 us
    all_to_all x1, blocking collectives, local(): lax.all_to_all(pieces, 'chip', 0, 0, tiled=True).reshape(total.shape)  11.3 us
  transfers between devices with their start and end apart: 26, of which 10 were waited for; matrix products, arithmetic and copies ran while one was open for 0% of the time, Pallas kernels for 12%

profile of v3, /device:TPU:1, one launch (start us, length us, event | category | flops | bytes accessed | tf_op | source)
XLA Modules:
  0.0 106.2 jit_solution(8917375699376257801)
XLA Ops:
  0.6 1.9 %copy-done.3 = f32[8,96,8,128]{3,2,1,0:T(8,128)S(1)} copy-done((f32[8,96,8,128]{3,2,1,0:T(8,128)S(1)}, f32[8,96,8,128]{3,2,1,0:T(8,128)}, u32[]{:S(2)}) %copy-start.3) | copy-done | bytes 3145752
  2.9 3.4 %collective-permute-start.5 = (f32[96,8,128]{2,1,0:T(8,128)S(1)}, f32[96,8,128]{2,1,0:T(8,128)S(1)}, u32[]{:S(2)}, u32[]{:S(2)}) collective-permute-start(f32[96,8,128]{2,1,0:T(8,128)S(1)} %get-tuple-element.42), channel_id=1, source_target_pairs={{0,192},{64,0},{128,64},{192,128},{1,193},{65,1},{129,65},{193,129... | collective-permute-start | bytes 1179656 | tf_op jit(solution)/shard_map/ppermute | solution.py:299
  6.5 2.5 %collective-permute-start = (f32[8,96,128]{2,1,0:T(8,128)S(1)}, f32[8,96,128]{2,1,0:T(8,128)S(1)}, u32[]{:S(2)}, u32[]{:S(2)}) collective-permute-start(f32[8,96,128]{2,1,0:T(8,128)S(1)} %get-tuple-element.35.refs_7_), channel_id=1, source_target_pairs={{0,1},{1,2},{2,3},{3,4},{4,5},{5,6},{6,7},{7,8},{8,9},{9,10},{10,1... | collective-permute-start | bytes 1179656 | tf_op jit(solution)/shard_map/ppermute | solution.py:299
  10.3 2.7 %collective-permute-done.2.refs_6_.refs_10_ = f32[8,8,128]{2,1,0:T(8,128)S(1)} collective-permute-done((f32[8,8,128]{2,1,0:T(8,128)S(1)}, f32[8,8,128]{2,1,0:T(8,128)S(1)}, u32[]{:S(2)}, u32[]{:S(2)}) %collective-permute-start.2) | collective-permute-done | bytes 32800 | tf_op jit(solution)/shard_map/ppermute | solution.py:299
  13.0 1.8 %collective-permute-start.3 = (f32[8,8,128]{2,1,0:T(8,128)S(1)}, f32[8,8,128]{2,1,0:T(8,128)S(1)}, u32[]{:S(2)}, u32[]{:S(2)}) collective-permute-start(f32[8,8,128]{2,1,0:T(8,128)S(1)} %get-tuple-element.38), channel_id=1, source_target_pairs={{0,48},{16,0},{32,16},{48,32},{1,49},{17,1},{33,17},{49,33},{2,50}... | collective-permute-start | bytes 98312 | tf_op jit(solution)/shard_map/ppermute | solution.py:299
  14.9 1.5 %shard_map.63.refs_12_ = f32[6,96,8,128]{3,2,1,0:T(8,128)S(1)} custom-call(f32[8,96,8,128]{3,2,1,0:T(8,128)S(1)} %copy-done.3, f32[8,96,8,128]{3,2,1,0:T(8,128)S(1)} %copy-done.1, f32[8,96,8,128]{3,2,1,0:T(8,128)S(1)} %copy-done.2, f32[8,96,8,128]{3,2,1,0:T(8,128)S(1)} %copy-done), custom_call_target="tpu_custom_call" | custom-call | flops 8388608 | tf_op jit(solution)/shard_map/pallas_call | solution.py:28
  18.1 6.4 %collective-permute-start.6 = (f32[8,96,128]{2,1,0:T(8,128)S(1)}, f32[8,96,128]{2,1,0:T(8,128)S(1)}, u32[]{:S(2)}, u32[]{:S(2)}) collective-permute-start(f32[8,96,128]{2,1,0:T(8,128)S(1)} %get-tuple-element.43.refs_9_), channel_id=1, source_target_pairs={{0,1},{1,2},{2,3},{3,4},{4,5},{5,6},{6,7},{7,8},{8,9},{9,10},{10,1... | collective-permute-start | bytes 1179656 | tf_op jit(solution)/shard_map/ppermute | solution.py:299
  25.8 4.2 %collective-permute-done.8.refs_8_.refs_12_ = f32[8,8,128]{2,1,0:T(8,128)S(1)} collective-permute-done((f32[8,8,128]{2,1,0:T(8,128)S(1)}, f32[8,8,128]{2,1,0:T(8,128)S(1)}, u32[]{:S(2)}, u32[]{:S(2)}) %collective-permute-start.8) | collective-permute-done | bytes 32800 | tf_op jit(solution)/shard_map/ppermute | solution.py:299
  30.0 1.5 %collective-permute-start.9 = (f32[8,8,128]{2,1,0:T(8,128)S(1)}, f32[8,8,128]{2,1,0:T(8,128)S(1)}, u32[]{:S(2)}, u32[]{:S(2)}) collective-permute-start(f32[8,8,128]{2,1,0:T(8,128)S(1)} %get-tuple-element.46), channel_id=1, source_target_pairs={{0,48},{16,0},{32,16},{48,32},{1,49},{17,1},{33,17},{49,33},{2,50}... | collective-permute-start | bytes 98312 | tf_op jit(solution)/shard_map/ppermute | solution.py:299
  31.5 1.5 %shard_map.68.refs_14_ = f32[6,96,8,128]{3,2,1,0:T(8,128)S(1)} custom-call(f32[96,8,128]{2,1,0:T(8,128)S(1)} %shard_map.61.refs_0_, f32[6,96,8,128]{3,2,1,0:T(8,128)S(1)} %shard_map.64.refs_1_, f32[96,8,128]{2,1,0:T(8,128)S(1)} %shard_map.65.refs_2_, f32[8,96,8,128]{3,2,1,0:T(8,128)S(1)} %copy-done.1, f32[8,96,8,128]{3,2,1,0:T(8,128)S(1)} %copy-done.2, ...), custom_call_target="tpu_custom_call" | custom-call | flops 8388608 | tf_op jit(solution)/shard_map/pallas_call | solution.py:28
  33.5 1.8 %collective-permute-start.17 = (f32[96,8,128]{2,1,0:T(8,128)S(1)}, f32[96,8,128]{2,1,0:T(8,128)S(1)}, u32[]{:S(2)}, u32[]{:S(2)}) collective-permute-start(f32[96,8,128]{2,1,0:T(8,128)S(1)} %shard_map.67.refs_0_), channel_id=1, source_target_pairs={{0,192},{64,0},{128,64},{192,128},{1,193},{65,1},{129,65},{193,129... | collective-permute-start | bytes 1179656 | tf_op jit(solution)/shard_map/ppermute | solution.py:299
  36.0 2.7 %collective-permute-start.12 = (f32[8,96,128]{2,1,0:T(8,128)S(1)}, f32[8,96,128]{2,1,0:T(8,128)S(1)}, u32[]{:S(2)}, u32[]{:S(2)}) collective-permute-start(f32[8,96,128]{2,1,0:T(8,128)S(1)} %get-tuple-element.47.refs_9_), channel_id=1, source_target_pairs={{0,1},{1,2},{2,3},{3,4},{4,5},{5,6},{6,7},{7,8},{8,9},{9,10},{10,1... | collective-permute-start | bytes 1179656 | tf_op jit(solution)/shard_map/ppermute | solution.py:299
  38.8 2.4 %collective-permute-start.13 = (f32[8,96,128]{2,1,0:T(8,128)S(1)}, f32[8,96,128]{2,1,0:T(8,128)S(1)}, u32[]{:S(2)}, u32[]{:S(2)}) collective-permute-start(f32[8,96,128]{2,1,0:T(8,128)S(1)} %get-tuple-element.48.refs_8_), channel_id=1, source_target_pairs={{0,15},{1,0},{2,1},{3,2},{4,3},{5,4},{6,5},{7,6},{8,7},{9,8},{10,9... | collective-permute-start | bytes 1179656 | tf_op jit(solution)/shard_map/ppermute | solution.py:299
  41.2 4.3 %collective-permute-done.14.refs_8_.refs_12_ = f32[8,8,128]{2,1,0:T(8,128)S(1)} collective-permute-done((f32[8,8,128]{2,1,0:T(8,128)S(1)}, f32[8,8,128]{2,1,0:T(8,128)S(1)}, u32[]{:S(2)}, u32[]{:S(2)}) %collective-permute-start.14) | collective-permute-done | bytes 32800 | tf_op jit(solution)/shard_map/ppermute | solution.py:299
  45.5 1.5 %collective-permute-start.15 = (f32[8,8,128]{2,1,0:T(8,128)S(1)}, f32[8,8,128]{2,1,0:T(8,128)S(1)}, u32[]{:S(2)}, u32[]{:S(2)}) collective-permute-start(f32[8,8,128]{2,1,0:T(8,128)S(1)} %get-tuple-element.50), channel_id=1, source_target_pairs={{0,48},{16,0},{32,16},{48,32},{1,49},{17,1},{33,17},{49,33},{2,50}... | collective-permute-start | bytes 98312 | tf_op jit(solution)/shard_map/ppermute | solution.py:299
  47.0 1.5 %shard_map.73.refs_14_ = f32[6,96,8,128]{3,2,1,0:T(8,128)S(1)} custom-call(f32[96,8,128]{2,1,0:T(8,128)S(1)} %shard_map.67.refs_0_, f32[6,96,8,128]{3,2,1,0:T(8,128)S(1)} %shard_map.69.refs_1_, f32[96,8,128]{2,1,0:T(8,128)S(1)} %shard_map.70.refs_2_, f32[8,96,8,128]{3,2,1,0:T(8,128)S(1)} %copy-done.1, f32[8,96,8,128]{3,2,1,0:T(8,128)S(1)} %copy-done.2, ...), custom_call_target="tpu_custom_call" | custom-call | flops 8388608 | tf_op jit(solution)/shard_map/pallas_call | solution.py:28
  50.9 2.6 %collective-permute-start.18 = (f32[8,96,128]{2,1,0:T(8,128)S(1)}, f32[8,96,128]{2,1,0:T(8,128)S(1)}, u32[]{:S(2)}, u32[]{:S(2)}) collective-permute-start(f32[8,96,128]{2,1,0:T(8,128)S(1)} %get-tuple-element.51.refs_9_), channel_id=1, source_target_pairs={{0,1},{1,2},{2,3},{3,4},{4,5},{5,6},{6,7},{7,8},{8,9},{9,10},{10,1... | collective-permute-start | bytes 1179656 | tf_op jit(solution)/shard_map/ppermute | solution.py:299
  54.7 2.6 %collective-permute-start.23 = (f32[96,8,128]{2,1,0:T(8,128)S(1)}, f32[96,8,128]{2,1,0:T(8,128)S(1)}, u32[]{:S(2)}, u32[]{:S(2)}) collective-permute-start(f32[96,8,128]{2,1,0:T(8,128)S(1)} %shard_map.72.refs_0_), channel_id=1, source_target_pairs={{0,192},{64,0},{128,64},{192,128},{1,193},{65,1},{129,65},{193,129... | collective-permute-start | bytes 1179656 | tf_op jit(solution)/shard_map/ppermute | solution.py:299
  57.3 4.3 %collective-permute-done.20.refs_12_.refs_8_ = f32[8,8,128]{2,1,0:T(8,128)S(1)} collective-permute-done((f32[8,8,128]{2,1,0:T(8,128)S(1)}, f32[8,8,128]{2,1,0:T(8,128)S(1)}, u32[]{:S(2)}, u32[]{:S(2)}) %collective-permute-start.20) | collective-permute-done | bytes 32800 | tf_op jit(solution)/shard_map/ppermute | solution.py:299
  63.1 1.5 %shard_map.77.refs_14_ = f32[6,96,8,128]{3,2,1,0:T(8,128)S(1)} custom-call(f32[96,8,128]{2,1,0:T(8,128)S(1)} %shard_map.72.refs_0_, f32[6,96,8,128]{3,2,1,0:T(8,128)S(1)} %shard_map.74.refs_1_, f32[96,8,128]{2,1,0:T(8,128)S(1)} %shard_map.75.refs_2_, f32[8,96,8,128]{3,2,1,0:T(8,128)S(1)} %copy-done.1, f32[8,96,8,128]{3,2,1,0:T(8,128)S(1)} %copy-done.2, ...), custom_call_target="tpu_custom_call" | custom-call | flops 8388608 | tf_op jit(solution)/shard_map/pallas_call | solution.py:28
  67.6 4.9 %collective-permute-start.24 = (f32[4,96,128]{2,1,0:T(8,128)S(1)}, f32[4,96,128]{2,1,0:T(8,128)S(1)}, u32[]{:S(2)}, u32[]{:S(2)}) collective-permute-start(f32[4,96,128]{2,1,0:T(8,128)S(1)} %get-tuple-element.58), channel_id=1, source_target_pairs={{0,1},{1,0},{2,3},{3,2},{4,5},{5,4},{6,7},{7,6},{8,9},{9,8},{10,11... | collective-permute-start | bytes 589832 | tf_op jit(solution)/shard_map/ppermute | solution.py:299
  73.6 15.3 %all_to_all.10.pieces = f32[8,48,128]{2,1,0:T(8,128)S(1)} all-to-all(f32[8,48,128]{2,1,0:T(8,128)S(1)} %bitcast.4), channel_id=1, replica_groups=mesh['south'=4,'east'=4,'chip'=8,'core'=2] {'chip'}, dimensions={0} | all-to-all | bytes 393216 | tf_op jit(solution)/shard_map/all_to_all | solution.py:367
  89.0 11.3 %all_to_all.11 = f32[8,48,128]{2,1,0:T(8,128)S(1)} all-to-all(f32[8,48,128]{2,1,0:T(8,128)S(1)} %shard_map.84), channel_id=1, replica_groups=mesh['south'=4,'east'=4,'chip'=8,'core'=2] {'chip'}, dimensions={0} | all-to-all | bytes 393216 | tf_op jit(solution)/shard_map/all_to_all | solution.py:369
  100.3 2.9 %collective-permute-start.25 = (f32[4,96,128]{2,1,0:T(8,128)S(1)}, f32[4,96,128]{2,1,0:T(8,128)S(1)}, u32[]{:S(2)}, u32[]{:S(2)}) collective-permute-start(f32[4,96,128]{2,1,0:T(8,128)S(1)} %get-tuple-element.59), channel_id=1, source_target_pairs={{0,1},{1,0},{2,3},{3,2},{4,5},{5,4},{6,7},{7,6},{8,9},{9,8},{10,11... | collective-permute-start | bytes 589832 | tf_op jit(solution)/shard_map/ppermute | solution.py:299
  (67 shorter events, 18.0 us)
Async XLA Ops:
  2.9 13.6 %collective-permute-start.5 = (f32[96,8,128]{2,1,0:T(8,128)S(1)}, f32[96,8,128]{2,1,0:T(8,128)S(1)}, u32[]{:S(2)}, u32[]{:S(2)}) collective-permute-start(f32[96,8,128]{2,1,0:T(8,128)S(1)} %get-tuple-element.42), channel_id=1, source_target_pairs={{0,192},{64,0},{128,64},{192,128},{1,193},{65,1},{129,65},{193,129... | collective-permute-start | bytes 1179656 | tf_op jit(solution)/shard_map/ppermute | solution.py:299
  6.5 10.0 %collective-permute-start = (f32[8,96,128]{2,1,0:T(8,128)S(1)}, f32[8,96,128]{2,1,0:T(8,128)S(1)}, u32[]{:S(2)}, u32[]{:S(2)}) collective-permute-start(f32[8,96,128]{2,1,0:T(8,128)S(1)} %get-tuple-element.35.refs_7_), channel_id=1, source_target_pairs={{0,1},{1,2},{2,3},{3,4},{4,5},{5,6},{6,7},{7,8},{8,9},{9,10},{10,1... | collective-permute-start | bytes 1179656 | tf_op jit(solution)/shard_map/ppermute | solution.py:299
  9.0 7.5 %collective-permute-start.1 = (f32[8,96,128]{2,1,0:T(8,128)S(1)}, f32[8,96,128]{2,1,0:T(8,128)S(1)}, u32[]{:S(2)}, u32[]{:S(2)}) collective-permute-start(f32[8,96,128]{2,1,0:T(8,128)S(1)} %get-tuple-element.36.refs_6_), channel_id=1, source_target_pairs={{0,15},{1,0},{2,1},{3,2},{4,3},{5,4},{6,5},{7,6},{8,7},{9,8},{10,9... | collective-permute-start | bytes 1179656 | tf_op jit(solution)/shard_map/ppermute | solution.py:299
  9.0 8.4 %collective-permute-start.4 = (f32[96,8,128]{2,1,0:T(8,128)S(1)}, f32[96,8,128]{2,1,0:T(8,128)S(1)}, u32[]{:S(2)}, u32[]{:S(2)}) collective-permute-start(f32[96,8,128]{2,1,0:T(8,128)S(1)} %get-tuple-element.39), channel_id=1, source_target_pairs={{0,64},{64,128},{128,192},{192,0},{1,65},{65,129},{129,193},{193,1... | collective-permute-start | bytes 1179656 | tf_op jit(solution)/shard_map/ppermute | solution.py:299
  9.0 4.0 %collective-permute-start.2 = (f32[8,8,128]{2,1,0:T(8,128)S(1)}, f32[8,8,128]{2,1,0:T(8,128)S(1)}, u32[]{:S(2)}, u32[]{:S(2)}) collective-permute-start(f32[8,8,128]{2,1,0:T(8,128)S(1)} %get-tuple-element.37), channel_id=1, source_target_pairs={{0,16},{16,32},{32,48},{48,0},{1,17},{17,33},{33,49},{49,1},{2,18}... | collective-permute-start | bytes 98312 | tf_op jit(solution)/shard_map/ppermute | solution.py:299
  13.0 3.5 %collective-permute-start.3 = (f32[8,8,128]{2,1,0:T(8,128)S(1)}, f32[8,8,128]{2,1,0:T(8,128)S(1)}, u32[]{:S(2)}, u32[]{:S(2)}) collective-permute-start(f32[8,8,128]{2,1,0:T(8,128)S(1)} %get-tuple-element.38), channel_id=1, source_target_pairs={{0,48},{16,0},{32,16},{48,32},{1,49},{17,1},{33,17},{49,33},{2,50}... | collective-permute-start | bytes 98312 | tf_op jit(solution)/shard_map/ppermute | solution.py:299
  16.9 16.3 %collective-permute-start.10 = (f32[96,8,128]{2,1,0:T(8,128)S(1)}, f32[96,8,128]{2,1,0:T(8,128)S(1)}, u32[]{:S(2)}, u32[]{:S(2)}) collective-permute-start(f32[96,8,128]{2,1,0:T(8,128)S(1)} %shard_map.65.refs_2_), channel_id=1, source_target_pairs={{0,64},{64,128},{128,192},{192,0},{1,65},{65,129},{129,193},{193,1... | collective-permute-start | bytes 1179656 | tf_op jit(solution)/shard_map/ppermute | solution.py:299
  18.1 15.0 %collective-permute-start.6 = (f32[8,96,128]{2,1,0:T(8,128)S(1)}, f32[8,96,128]{2,1,0:T(8,128)S(1)}, u32[]{:S(2)}, u32[]{:S(2)}) collective-permute-start(f32[8,96,128]{2,1,0:T(8,128)S(1)} %get-tuple-element.43.refs_9_), channel_id=1, source_target_pairs={{0,1},{1,2},{2,3},{3,4},{4,5},{5,6},{6,7},{7,8},{8,9},{9,10},{10,1... | collective-permute-start | bytes 1179656 | tf_op jit(solution)/shard_map/ppermute | solution.py:299
  24.4 8.7 %collective-permute-start.7 = (f32[8,96,128]{2,1,0:T(8,128)S(1)}, f32[8,96,128]{2,1,0:T(8,128)S(1)}, u32[]{:S(2)}, u32[]{:S(2)}) collective-permute-start(f32[8,96,128]{2,1,0:T(8,128)S(1)} %get-tuple-element.44.refs_8_), channel_id=1, source_target_pairs={{0,15},{1,0},{2,1},{3,2},{4,3},{5,4},{6,5},{7,6},{8,7},{9,8},{10,9... | collective-permute-start | bytes 1179656 | tf_op jit(solution)/shard_map/ppermute | solution.py:299
  24.4 10.8 %collective-permute-start.11 = (f32[96,8,128]{2,1,0:T(8,128)S(1)}, f32[96,8,128]{2,1,0:T(8,128)S(1)}, u32[]{:S(2)}, u32[]{:S(2)}) collective-permute-start(f32[96,8,128]{2,1,0:T(8,128)S(1)} %shard_map.61.refs_0_), channel_id=1, source_target_pairs={{0,192},{64,0},{128,64},{192,128},{1,193},{65,1},{129,65},{193,129... | collective-permute-start | bytes 1179656 | tf_op jit(solution)/shard_map/ppermute | solution.py:299
  25.7 4.3 %collective-permute-start.8 = (f32[8,8,128]{2,1,0:T(8,128)S(1)}, f32[8,8,128]{2,1,0:T(8,128)S(1)}, u32[]{:S(2)}, u32[]{:S(2)}) collective-permute-start(f32[8,8,128]{2,1,0:T(8,128)S(1)} %get-tuple-element.45), channel_id=1, source_target_pairs={{0,16},{16,32},{32,48},{48,0},{1,17},{17,33},{33,49},{49,1},{2,18}... | collective-permute-start | bytes 98312 | tf_op jit(solution)/shard_map/ppermute | solution.py:299
  33.5 15.1 %collective-permute-start.17 = (f32[96,8,128]{2,1,0:T(8,128)S(1)}, f32[96,8,128]{2,1,0:T(8,128)S(1)}, u32[]{:S(2)}, u32[]{:S(2)}) collective-permute-start(f32[96,8,128]{2,1,0:T(8,128)S(1)} %shard_map.67.refs_0_), channel_id=1, source_target_pairs={{0,192},{64,0},{128,64},{192,128},{1,193},{65,1},{129,65},{193,129... | collective-permute-start | bytes 1179656 | tf_op jit(solution)/shard_map/ppermute | solution.py:299
  36.0 12.6 %collective-permute-start.12 = (f32[8,96,128]{2,1,0:T(8,128)S(1)}, f32[8,96,128]{2,1,0:T(8,128)S(1)}, u32[]{:S(2)}, u32[]{:S(2)}) collective-permute-start(f32[8,96,128]{2,1,0:T(8,128)S(1)} %get-tuple-element.47.refs_9_), channel_id=1, source_target_pairs={{0,1},{1,2},{2,3},{3,4},{4,5},{5,6},{6,7},{7,8},{8,9},{9,10},{10,1... | collective-permute-start | bytes 1179656 | tf_op jit(solution)/shard_map/ppermute | solution.py:299
  38.8 9.8 %collective-permute-start.13 = (f32[8,96,128]{2,1,0:T(8,128)S(1)}, f32[8,96,128]{2,1,0:T(8,128)S(1)}, u32[]{:S(2)}, u32[]{:S(2)}) collective-permute-start(f32[8,96,128]{2,1,0:T(8,128)S(1)} %get-tuple-element.48.refs_8_), channel_id=1, source_target_pairs={{0,15},{1,0},{2,1},{3,2},{4,3},{5,4},{6,5},{7,6},{8,7},{9,8},{10,9... | collective-permute-start | bytes 1179656 | tf_op jit(solution)/shard_map/ppermute | solution.py:299
  41.2 8.9 %collective-permute-start.16 = (f32[96,8,128]{2,1,0:T(8,128)S(1)}, f32[96,8,128]{2,1,0:T(8,128)S(1)}, u32[]{:S(2)}, u32[]{:S(2)}) collective-permute-start(f32[96,8,128]{2,1,0:T(8,128)S(1)} %shard_map.70.refs_2_), channel_id=1, source_target_pairs={{0,64},{64,128},{128,192},{192,0},{1,65},{65,129},{129,193},{193,1... | collective-permute-start | bytes 1179656 | tf_op jit(solution)/shard_map/ppermute | solution.py:299
  41.2 4.3 %collective-permute-start.14 = (f32[8,8,128]{2,1,0:T(8,128)S(1)}, f32[8,8,128]{2,1,0:T(8,128)S(1)}, u32[]{:S(2)}, u32[]{:S(2)}) collective-permute-start(f32[8,8,128]{2,1,0:T(8,128)S(1)} %get-tuple-element.49), channel_id=1, source_target_pairs={{0,16},{16,32},{32,48},{48,0},{1,17},{17,33},{33,49},{49,1},{2,18}... | collective-permute-start | bytes 98312 | tf_op jit(solution)/shard_map/ppermute | solution.py:299
  45.5 3.1 %collective-permute-start.15 = (f32[8,8,128]{2,1,0:T(8,128)S(1)}, f32[8,8,128]{2,1,0:T(8,128)S(1)}, u32[]{:S(2)}, u32[]{:S(2)}) collective-permute-start(f32[8,8,128]{2,1,0:T(8,128)S(1)} %get-tuple-element.50), channel_id=1, source_target_pairs={{0,48},{16,0},{32,16},{48,32},{1,49},{17,1},{33,17},{49,33},{2,50}... | collective-permute-start | bytes 98312 | tf_op jit(solution)/shard_map/ppermute | solution.py:299
  50.9 13.8 %collective-permute-start.18 = (f32[8,96,128]{2,1,0:T(8,128)S(1)}, f32[8,96,128]{2,1,0:T(8,128)S(1)}, u32[]{:S(2)}, u32[]{:S(2)}) collective-permute-start(f32[8,96,128]{2,1,0:T(8,128)S(1)} %get-tuple-element.51.refs_9_), channel_id=1, source_target_pairs={{0,1},{1,2},{2,3},{3,4},{4,5},{5,6},{6,7},{7,8},{8,9},{9,10},{10,1... | collective-permute-start | bytes 1179656 | tf_op jit(solution)/shard_map/ppermute | solution.py:299
  53.5 11.2 %collective-permute-start.19 = (f32[8,96,128]{2,1,0:T(8,128)S(1)}, f32[8,96,128]{2,1,0:T(8,128)S(1)}, u32[]{:S(2)}, u32[]{:S(2)}) collective-permute-start(f32[8,96,128]{2,1,0:T(8,128)S(1)} %get-tuple-element.52.refs_8_), channel_id=1, source_target_pairs={{0,15},{1,0},{2,1},{3,2},{4,3},{5,4},{6,5},{7,6},{8,7},{9,8},{10,9... | collective-permute-start | bytes 1179656 | tf_op jit(solution)/shard_map/ppermute | solution.py:299
  54.7 11.6 %collective-permute-start.23 = (f32[96,8,128]{2,1,0:T(8,128)S(1)}, f32[96,8,128]{2,1,0:T(8,128)S(1)}, u32[]{:S(2)}, u32[]{:S(2)}) collective-permute-start(f32[96,8,128]{2,1,0:T(8,128)S(1)} %shard_map.72.refs_0_), channel_id=1, source_target_pairs={{0,192},{64,0},{128,64},{192,128},{1,193},{65,1},{129,65},{193,129... | collective-permute-start | bytes 1179656 | tf_op jit(solution)/shard_map/ppermute | solution.py:299
  57.3 9.4 %collective-permute-start.22 = (f32[96,8,128]{2,1,0:T(8,128)S(1)}, f32[96,8,128]{2,1,0:T(8,128)S(1)}, u32[]{:S(2)}, u32[]{:S(2)}) collective-permute-start(f32[96,8,128]{2,1,0:T(8,128)S(1)} %shard_map.75.refs_2_), channel_id=1, source_target_pairs={{0,64},{64,128},{128,192},{192,0},{1,65},{65,129},{129,193},{193,1... | collective-permute-start | bytes 1179656 | tf_op jit(solution)/shard_map/ppermute | solution.py:299
  57.3 4.3 %collective-permute-start.20 = (f32[8,8,128]{2,1,0:T(8,128)S(1)}, f32[8,8,128]{2,1,0:T(8,128)S(1)}, u32[]{:S(2)}, u32[]{:S(2)}) collective-permute-start(f32[8,8,128]{2,1,0:T(8,128)S(1)} %get-tuple-element.53), channel_id=1, source_target_pairs={{0,16},{16,32},{32,48},{48,0},{1,17},{17,33},{33,49},{49,1},{2,18}... | collective-permute-start | bytes 98312 | tf_op jit(solution)/shard_map/ppermute | solution.py:299
  67.6 6.0 %collective-permute-start.24 = (f32[4,96,128]{2,1,0:T(8,128)S(1)}, f32[4,96,128]{2,1,0:T(8,128)S(1)}, u32[]{:S(2)}, u32[]{:S(2)}) collective-permute-start(f32[4,96,128]{2,1,0:T(8,128)S(1)} %get-tuple-element.58), channel_id=1, source_target_pairs={{0,1},{1,0},{2,3},{3,2},{4,5},{5,4},{6,7},{7,6},{8,9},{9,8},{10,11... | collective-permute-start | bytes 589832 | tf_op jit(solution)/shard_map/ppermute | solution.py:299
  100.3 4.4 %collective-permute-start.25 = (f32[4,96,128]{2,1,0:T(8,128)S(1)}, f32[4,96,128]{2,1,0:T(8,128)S(1)}, u32[]{:S(2)}, u32[]{:S(2)}) collective-permute-start(f32[4,96,128]{2,1,0:T(8,128)S(1)} %get-tuple-element.59), channel_id=1, source_target_pairs={{0,1},{1,0},{2,3},{3,2},{4,5},{5,4},{6,7},{7,6},{8,9},{9,8},{10,11... | collective-permute-start | bytes 589832 | tf_op jit(solution)/shard_map/ppermute | solution.py:299
  (6 other events, 40.7 us)

commit v4 on v3

--- a/solution.py
+++ b/solution.py
@@ -11,7 +11,7 @@
 STEPS = 4
 RATE = 0.05
 BLOCK = 8
-GROUP = 3
+GROUP = 4
 VMEM = 5 << 20
 
 
@@ -55,7 +55,7 @@
     return jnp.where(sublane == 7, head, ahead), jnp.where(sublane == 0, tail, behind)
 
 
-def march(cells, column_at, cell, left):
+def march(cells, column_at, cell):
     def run(start, first, last, left, mid):
         for k in range(first, last):
             right = column_at(start + k + 1)
@@ -66,12 +66,9 @@
     def body(i, carry):
         return run(pl.multiple_of(i * BLOCK, BLOCK), 0, BLOCK, *carry)
 
-    if left is None:
-        carry = run(0, 1, BLOCK, column_at(0), column_at(1))
-    else:
-        carry = run(0, 0, BLOCK, left, column_at(0))
+    carry = run(0, 1, BLOCK, column_at(0), column_at(1))
     carry = lax.fori_loop(1, cells // BLOCK - 1, body, carry)
-    return run(cells - BLOCK, 0, BLOCK - 1, *carry)
+    run(cells - BLOCK, 0, BLOCK - 1, *carry)
 
 
 def reader(ref, *at):
@@ -91,20 +88,22 @@
 
 
 def inner_kernel(parts, height, *refs):
-    field, (fy, fx, fz), out = refs[:parts], refs[parts : parts + 3], refs[parts + 3]
+    field, (fy, fx, fz), (out, low, high) = refs[:parts], refs[parts : parts + 3], refs[parts + 3 :]
     cells = fy.shape[1]
-    rows = [reader(plane) for plane in planes_of(field, height)]
-    for start in range(1, height - 1, GROUP):
-        ys = list(range(start, min(start + GROUP, height - 1)))
+    planes = [low, *(out.at[y] for y in range(height - 2)), high]
+    nothing = lambda x: jnp.zeros((8, 128), jnp.float32)
+    rows = [nothing, *(reader(plane) for plane in planes_of(field, height)), nothing]
+    for start in range(0, height, GROUP):
+        ys = list(range(start, min(start + GROUP, height)))
 
         def cell(x, left, mid, right, ys=ys):
-            column = [rows[ys[0] - 1](x), *mid, rows[ys[-1] + 1](x)]
+            column = [rows[ys[0]](x), *mid, rows[ys[-1] + 2](x)]
             for g, y in enumerate(ys):
-                out[y - 1, x] = advance(
+                planes[y][x] = advance(
                     mid[g], column[g + 2], column[g], left[g], right[g], *turned(mid[g]), fy[y, x], fx[y, x], fz[y, x]
                 )
 
-        march(cells, lambda x, ys=ys: [rows[y](x) for y in ys], cell, None)
+        march(cells, lambda x, ys=ys: [rows[y + 1](x) for y in ys], cell)
 
 
 def mend_kernel(parts, height, *refs):
@@ -132,21 +131,36 @@
 
 def rim_kernel(parts, height, top, *refs):
     field, (fy, fx, fz) = refs[:parts], refs[parts : parts + 3]
-    (zlo, zhi), sides = refs[parts + 3 : parts + 5], refs[parts + 5 : parts + 7]
-    beyond, out = refs[parts + 7 :]
+    (zlo, zhi), (first, last) = refs[parts + 3 : parts + 5], refs[parts + 5 : parts + 7]
+    to_first, to_last = refs[parts + 7 : parts + 9]
+    sides, beyond, out = refs[parts + 9 : parts + 11], refs[parts + 11], refs[parts + 13]
     cells = fy.shape[1]
     rows = [reader(plane) for plane in planes_of(field, height)]
     y = height - 1 if top else 0
-    here = rows[y]
+
+    def body(i, carry):
+        start = pl.multiple_of(i * BLOCK, BLOCK)
+        for k in range(BLOCK):
+            x = start + k
+            rate = RATE - fy[y, x] if top else RATE + fy[y, x]
+            out[x] += rate * beyond[x]
+        return carry
+
+    lax.fori_loop(0, cells // BLOCK, body, 0)
+    flat = out.reshape(cells * 8, 128)
+    flat[pl.ds(0, cells, 8), :] += to_first[y] * (zlo[y] - last[y])
+    flat[pl.ds(7, cells, 8), :] += to_last[y] * (zhi[y] - first[y])
     above, below = (reader(beyond), rows[y - 1]) if top else (rows[1], reader(beyond))
-
-    def cell(x, left, mid, right):
+    for x, left, right in (
+        (0, sides[0][y], rows[y](1)),
+        (cells - 1, rows[y](cells - 2), sides[1][y]),
+    ):
+        here = rows[y](x)
         out[x] = advance(
-            mid, above(x), below(x), left, right, *along_z(mid, zlo, zhi, y, x), fy[y, x], fx[y, x], fz[y, x]
+            *(here, above(x), below(x), left, right),
+            *along_z(here, zlo, zhi, y, x),
+            *(fy[y, x], fx[y, x], fz[y, x]),
         )
-
-    carry = march(cells, here, cell, sides[0][y])
-    cell(cells - 1, *carry, sides[1][y])
 
 
 def near_kernel(fz, to_first, to_last):
@@ -329,7 +343,9 @@
     near = call(near_kernel, (edge, edge), flow_z)
     for step in range(1, STEPS + 1):
         parts = len(field)
-        (mid,) = call(functools.partial(inner_kernel, parts, height), (inner,), *(*field, *flows), flops=1 << 23)
+        mid, *rims = call(
+            functools.partial(inner_kernel, parts, height), (inner, row, row), *(*field, *flows), flops=1 << 23
+        )
         (mid,) = call(
             functools.partial(mend_kernel, parts, height),
             (inner,),
@@ -338,9 +354,12 @@
         )
         low, high = (
             call(
-                functools.partial(rim_kernel, parts, height, top), (row,), *(*field, *flows, *downs, *sides, beyond)
+                functools.partial(rim_kernel, parts, height, top),
+                (row,),
+                *(*field, *flows, *downs, *faces, *near, *sides, beyond, rim),
+                alias={parts + 12: 0},
             )[0]
-            for top, beyond in ((False, slo), (True, shi))
+            for top, beyond, rim in ((False, slo, rims[0]), (True, shi, rims[1]))
         )
         field = (low, mid, high)
         if step < STEPS:

time: 106 us -> 108 us (1.019)
  local copies, waits for them, and re-layouts: 1.9 us -> 3.79 us
  waiting for transfers between devices: 18.4 us -> 17.3 us
    unnamed x8 -> x10, local copies, waits for them, and re-layouts: 1.9 us -> 3.79 us
    ppermute x26, waiting for transfers between devices: 18.4 us -> 17.3 us  [sent(): lax.ppermute(array, axis, [(i, (i + by) % size) for i in range(size)])]
  transfers between devices with their start and end apart: 26 -> 26, of which waited for: 10 -> 7; matrix products, arithmetic and copies ran while one was open for 0% -> 0% of each run, Pallas kernels for 12% -> 12%
where the time goes in v4:
time: 108 us
  starting transfers between devices  43.3 us (40%)
  blocking collectives  26.4 us (24%)
  waiting for transfers between devices  17.3 us (16%)
  Pallas kernels  15.9 us (15%)
  local copies, waits for them, and re-layouts  3.79 us (4%)
  between operations  1.18 us (1%)
    ppermute x26, starting transfers between devices, sent(): lax.ppermute(array, axis, [(i, (i + by) % size) for i in range(size)])  43.3 us
    ppermute x26, waiting for transfers between devices, sent(): lax.ppermute(array, axis, [(i, (i + by) % size) for i in range(size)])  17.3 us
    pallas_call x29, Pallas kernels, call(): pl.pallas_call(kernel, out_shape=outs, in_specs=in_specs or [IN_VMEM] * l...  15.9 us
    all_to_all x1, blocking collectives, local(): lax.all_to_all(total.reshape(chips, -1, 128), 'chip', 0, 0, tiled=True)  15.1 us
    all_to_all x1, blocking collectives, local(): lax.all_to_all(pieces, 'chip', 0, 0, tiled=True).reshape(total.shape)  11.3 us
    unnamed x10, local copies, waits for them, and re-layouts  3.79 us
  transfers between devices with their start and end apart: 26, of which 7 were waited for; matrix products, arithmetic and copies ran while one was open for 0% of the time, Pallas kernels for 12%

profile of v4, /device:TPU:1, one launch (start us, length us, event | category | flops | bytes accessed | tf_op | source)
XLA Modules:
  0.0 107.8 jit_solution(8954509228641929072)
XLA Ops:
  0.6 1.9 %copy-done.3 = f32[8,96,8,128]{3,2,1,0:T(8,128)S(1)} copy-done((f32[8,96,8,128]{3,2,1,0:T(8,128)S(1)}, f32[8,96,8,128]{3,2,1,0:T(8,128)}, u32[]{:S(2)}) %copy-start.3) | copy-done | bytes 3145752
  2.7 3.0 %collective-permute-start = (f32[8,96,128]{2,1,0:T(8,128)S(1)}, f32[8,96,128]{2,1,0:T(8,128)S(1)}, u32[]{:S(2)}, u32[]{:S(2)}) collective-permute-start(f32[8,96,128]{2,1,0:T(8,128)S(1)} %get-tuple-element.47.refs_7_), channel_id=1, source_target_pairs={{0,1},{1,2},{2,3},{3,4},{4,5},{5,6},{6,7},{7,8},{8,9},{9,10},{10,1... | collective-permute-start | bytes 1179656 | tf_op jit(solution)/shard_map/ppermute | solution.py:313
  5.9 1.9 %copy-done.4 = f32[8,96,8,128]{3,2,1,0:T(8,128)S(1)} copy-done((f32[8,96,8,128]{3,2,1,0:T(8,128)S(1)}, f32[8,96,8,128]{3,2,1,0:T(8,128)}, u32[]{:S(2)}) %copy-start.4) | copy-done | bytes 3145752
  8.2 2.3 %collective-permute-start.5 = (f32[96,8,128]{2,1,0:T(8,128)S(1)}, f32[96,8,128]{2,1,0:T(8,128)S(1)}, u32[]{:S(2)}, u32[]{:S(2)}) collective-permute-start(f32[96,8,128]{2,1,0:T(8,128)S(1)} %get-tuple-element.56), channel_id=1, source_target_pairs={{0,192},{64,0},{128,64},{192,128},{1,193},{65,1},{129,65},{193,129... | collective-permute-start | bytes 1179656 | tf_op jit(solution)/shard_map/ppermute | solution.py:313
  11.9 2.7 %collective-permute-done.2.refs_10_ = f32[8,8,128]{2,1,0:T(8,128)S(1)} collective-permute-done((f32[8,8,128]{2,1,0:T(8,128)S(1)}, f32[8,8,128]{2,1,0:T(8,128)S(1)}, u32[]{:S(2)}, u32[]{:S(2)}) %collective-permute-start.2) | collective-permute-done | bytes 32800 | tf_op jit(solution)/shard_map/ppermute | solution.py:313
  14.6 1.8 %collective-permute-start.3 = (f32[8,8,128]{2,1,0:T(8,128)S(1)}, f32[8,8,128]{2,1,0:T(8,128)S(1)}, u32[]{:S(2)}, u32[]{:S(2)}) collective-permute-start(f32[8,8,128]{2,1,0:T(8,128)S(1)} %get-tuple-element.52), channel_id=1, source_target_pairs={{0,48},{16,0},{32,16},{48,32},{1,49},{17,1},{33,17},{49,33},{2,50}... | collective-permute-start | bytes 98312 | tf_op jit(solution)/shard_map/ppermute | solution.py:313
  16.6 1.9 %shard_map.62 = (f32[6,96,8,128]{3,2,1,0:T(8,128)S(1)}, f32[96,8,128]{2,1,0:T(8,128)S(1)}, f32[96,8,128]{2,1,0:T(8,128)S(1)}) custom-call(f32[8,96,8,128]{3,2,1,0:T(8,128)S(1)} %copy-done.4, f32[8,96,8,128]{3,2,1,0:T(8,128)S(1)} %copy-done.1, f32[8,96,8,128]{3,2,1,0:T(8,128)S(1)} %copy-done.2, f32[8,96,8,128]{3,2,1,0:T(8,128)S(1)} %copy-done), custom_call_target="tpu_custom_call" | custom-call | flops 8388608 | tf_op jit(solution)/shard_map/pallas_call | solution.py:28
  19.3 5.9 %collective-permute-start.6 = (f32[8,96,128]{2,1,0:T(8,128)S(1)}, f32[8,96,128]{2,1,0:T(8,128)S(1)}, u32[]{:S(2)}, u32[]{:S(2)}) collective-permute-start(f32[8,96,128]{2,1,0:T(8,128)S(1)} %get-tuple-element.58.refs_9_), channel_id=1, source_target_pairs={{0,1},{1,2},{2,3},{3,4},{4,5},{5,6},{6,7},{7,8},{8,9},{9,10},{10,1... | collective-permute-start | bytes 1179656 | tf_op jit(solution)/shard_map/ppermute | solution.py:313
  25.2 2.3 %collective-permute-start.11 = (f32[96,8,128]{2,1,0:T(8,128)S(1)}, f32[96,8,128]{2,1,0:T(8,128)S(1)}, u32[]{:S(2)}, u32[]{:S(2)}) collective-permute-start(f32[96,8,128]{2,1,0:T(8,128)S(1)} %shard_map.63.refs_0_), channel_id=1, source_target_pairs={{0,192},{64,0},{128,64},{192,128},{1,193},{65,1},{129,65},{193,129... | collective-permute-start | bytes 1179656 | tf_op jit(solution)/shard_map/ppermute | solution.py:313
  27.9 3.9 %collective-permute-done.8.refs_12_ = f32[8,8,128]{2,1,0:T(8,128)S(1)} collective-permute-done((f32[8,8,128]{2,1,0:T(8,128)S(1)}, f32[8,8,128]{2,1,0:T(8,128)S(1)}, u32[]{:S(2)}, u32[]{:S(2)}) %collective-permute-start.8) | collective-permute-done | bytes 32800 | tf_op jit(solution)/shard_map/ppermute | solution.py:313
  33.3 1.9 %shard_map.67 = (f32[6,96,8,128]{3,2,1,0:T(8,128)S(1)}, f32[96,8,128]{2,1,0:T(8,128)S(1)}, f32[96,8,128]{2,1,0:T(8,128)S(1)}) custom-call(f32[96,8,128]{2,1,0:T(8,128)S(1)} %shard_map.63.refs_0_, f32[6,96,8,128]{3,2,1,0:T(8,128)S(1)} %shard_map.64.refs_1_, f32[96,8,128]{2,1,0:T(8,128)S(1)} %shard_map.65.refs_2_, f32[8,96,8,128]{3,2,1,0:T(8,128)S(1)} %copy-done.1, ...), custom_call_target="tpu_custom_call" | custom-call | flops 8388608 | tf_op jit(solution)/shard_map/pallas_call | solution.py:28
  36.5 3.5 %collective-permute-start.12 = (f32[8,96,128]{2,1,0:T(8,128)S(1)}, f32[8,96,128]{2,1,0:T(8,128)S(1)}, u32[]{:S(2)}, u32[]{:S(2)}) collective-permute-start(f32[8,96,128]{2,1,0:T(8,128)S(1)} %get-tuple-element.65.refs_9_), channel_id=1, source_target_pairs={{0,1},{1,2},{2,3},{3,4},{4,5},{5,6},{6,7},{7,8},{8,9},{9,10},{10,1... | collective-permute-start | bytes 1179656 | tf_op jit(solution)/shard_map/ppermute | solution.py:313
  40.6 2.9 %collective-permute-start.17 = (f32[96,8,128]{2,1,0:T(8,128)S(1)}, f32[96,8,128]{2,1,0:T(8,128)S(1)}, u32[]{:S(2)}, u32[]{:S(2)}) collective-permute-start(f32[96,8,128]{2,1,0:T(8,128)S(1)} %shard_map.68.refs_0_), channel_id=1, source_target_pairs={{0,192},{64,0},{128,64},{192,128},{1,193},{65,1},{129,65},{193,129... | collective-permute-start | bytes 1179656 | tf_op jit(solution)/shard_map/ppermute | solution.py:313
  43.5 4.3 %collective-permute-done.14.refs_12_ = f32[8,8,128]{2,1,0:T(8,128)S(1)} collective-permute-done((f32[8,8,128]{2,1,0:T(8,128)S(1)}, f32[8,8,128]{2,1,0:T(8,128)S(1)}, u32[]{:S(2)}, u32[]{:S(2)}) %collective-permute-start.14) | collective-permute-done | bytes 32800 | tf_op jit(solution)/shard_map/ppermute | solution.py:313
  47.8 1.5 %collective-permute-start.15 = (f32[8,8,128]{2,1,0:T(8,128)S(1)}, f32[8,8,128]{2,1,0:T(8,128)S(1)}, u32[]{:S(2)}, u32[]{:S(2)}) collective-permute-start(f32[8,8,128]{2,1,0:T(8,128)S(1)} %get-tuple-element.68), channel_id=1, source_target_pairs={{0,48},{16,0},{32,16},{48,32},{1,49},{17,1},{33,17},{49,33},{2,50}... | collective-permute-start | bytes 98312 | tf_op jit(solution)/shard_map/ppermute | solution.py:313
  49.3 1.9 %shard_map.72 = (f32[6,96,8,128]{3,2,1,0:T(8,128)S(1)}, f32[96,8,128]{2,1,0:T(8,128)S(1)}, f32[96,8,128]{2,1,0:T(8,128)S(1)}) custom-call(f32[96,8,128]{2,1,0:T(8,128)S(1)} %shard_map.68.refs_0_, f32[6,96,8,128]{3,2,1,0:T(8,128)S(1)} %shard_map.69.refs_1_, f32[96,8,128]{2,1,0:T(8,128)S(1)} %shard_map.70.refs_2_, f32[8,96,8,128]{3,2,1,0:T(8,128)S(1)} %copy-done.1, ...), custom_call_target="tpu_custom_call" | custom-call | flops 8388608 | tf_op jit(solution)/shard_map/pallas_call | solution.py:28
  52.5 2.7 %collective-permute-start.18 = (f32[8,96,128]{2,1,0:T(8,128)S(1)}, f32[8,96,128]{2,1,0:T(8,128)S(1)}, u32[]{:S(2)}, u32[]{:S(2)}) collective-permute-start(f32[8,96,128]{2,1,0:T(8,128)S(1)} %get-tuple-element.72.refs_9_), channel_id=1, source_target_pairs={{0,1},{1,2},{2,3},{3,4},{4,5},{5,6},{6,7},{7,8},{8,9},{9,10},{10,1... | collective-permute-start | bytes 1179656 | tf_op jit(solution)/shard_map/ppermute | solution.py:313
  56.6 2.9 %collective-permute-start.23 = (f32[96,8,128]{2,1,0:T(8,128)S(1)}, f32[96,8,128]{2,1,0:T(8,128)S(1)}, u32[]{:S(2)}, u32[]{:S(2)}) collective-permute-start(f32[96,8,128]{2,1,0:T(8,128)S(1)} %shard_map.73.refs_0_), channel_id=1, source_target_pairs={{0,192},{64,0},{128,64},{192,128},{1,193},{65,1},{129,65},{193,129... | collective-permute-start | bytes 1179656 | tf_op jit(solution)/shard_map/ppermute | solution.py:313
  59.5 4.3 %collective-permute-done.20.refs_12_ = f32[8,8,128]{2,1,0:T(8,128)S(1)} collective-permute-done((f32[8,8,128]{2,1,0:T(8,128)S(1)}, f32[8,8,128]{2,1,0:T(8,128)S(1)}, u32[]{:S(2)}, u32[]{:S(2)}) %collective-permute-start.20) | collective-permute-done | bytes 32800 | tf_op jit(solution)/shard_map/ppermute | solution.py:313
  65.3 1.9 %shard_map.77 = (f32[6,96,8,128]{3,2,1,0:T(8,128)S(1)}, f32[96,8,128]{2,1,0:T(8,128)S(1)}, f32[96,8,128]{2,1,0:T(8,128)S(1)}) custom-call(f32[96,8,128]{2,1,0:T(8,128)S(1)} %shard_map.73.refs_0_, f32[6,96,8,128]{3,2,1,0:T(8,128)S(1)} %shard_map.74.refs_1_, f32[96,8,128]{2,1,0:T(8,128)S(1)} %shard_map.75.refs_2_, f32[8,96,8,128]{3,2,1,0:T(8,128)S(1)} %copy-done.1, ...), custom_call_target="tpu_custom_call" | custom-call | flops 8388608 | tf_op jit(solution)/shard_map/pallas_call | solution.py:28
  69.8 4.6 %collective-permute-start.24 = (f32[4,96,128]{2,1,0:T(8,128)S(1)}, f32[4,96,128]{2,1,0:T(8,128)S(1)}, u32[]{:S(2)}, u32[]{:S(2)}) collective-permute-start(f32[4,96,128]{2,1,0:T(8,128)S(1)} %get-tuple-element.82), channel_id=1, source_target_pairs={{0,1},{1,0},{2,3},{3,2},{4,5},{5,4},{6,7},{7,6},{8,9},{9,8},{10,11... | collective-permute-start | bytes 589832 | tf_op jit(solution)/shard_map/ppermute | solution.py:313
  75.6 15.1 %all_to_all.10.pieces = f32[8,48,128]{2,1,0:T(8,128)S(1)} all-to-all(f32[8,48,128]{2,1,0:T(8,128)S(1)} %bitcast.4), channel_id=1, replica_groups=mesh['south'=4,'east'=4,'chip'=8,'core'=2] {'chip'}, dimensions={0} | all-to-all | bytes 393216 | tf_op jit(solution)/shard_map/all_to_all | solution.py:386
  90.6 11.3 %all_to_all.11 = f32[8,48,128]{2,1,0:T(8,128)S(1)} all-to-all(f32[8,48,128]{2,1,0:T(8,128)S(1)} %shard_map.84), channel_id=1, replica_groups=mesh['south'=4,'east'=4,'chip'=8,'core'=2] {'chip'}, dimensions={0} | all-to-all | bytes 393216 | tf_op jit(solution)/shard_map/all_to_all | solution.py:388
  102.0 2.9 %collective-permute-start.25 = (f32[4,96,128]{2,1,0:T(8,128)S(1)}, f32[4,96,128]{2,1,0:T(8,128)S(1)}, u32[]{:S(2)}, u32[]{:S(2)}) collective-permute-start(f32[4,96,128]{2,1,0:T(8,128)S(1)} %get-tuple-element.83), channel_id=1, source_target_pairs={{0,1},{1,0},{2,3},{3,2},{4,5},{5,4},{6,7},{7,6},{8,9},{9,8},{10,11... | collective-permute-start | bytes 589832 | tf_op jit(solution)/shard_map/ppermute | solution.py:313
  (69 shorter events, 17.1 us)
Async XLA Ops:
  2.7 15.8 %collective-permute-start = (f32[8,96,128]{2,1,0:T(8,128)S(1)}, f32[8,96,128]{2,1,0:T(8,128)S(1)}, u32[]{:S(2)}, u32[]{:S(2)}) collective-permute-start(f32[8,96,128]{2,1,0:T(8,128)S(1)} %get-tuple-element.47.refs_7_), channel_id=1, source_target_pairs={{0,1},{1,2},{2,3},{3,4},{4,5},{5,6},{6,7},{7,8},{8,9},{9,10},{10,1... | collective-permute-start | bytes 1179656 | tf_op jit(solution)/shard_map/ppermute | solution.py:313
  5.7 12.8 %collective-permute-start.1 = (f32[8,96,128]{2,1,0:T(8,128)S(1)}, f32[8,96,128]{2,1,0:T(8,128)S(1)}, u32[]{:S(2)}, u32[]{:S(2)}) collective-permute-start(f32[8,96,128]{2,1,0:T(8,128)S(1)} %get-tuple-element.48.refs_6_), channel_id=1, source_target_pairs={{0,15},{1,0},{2,1},{3,2},{4,3},{5,4},{6,5},{7,6},{8,7},{9,8},{10,9... | collective-permute-start | bytes 1179656 | tf_op jit(solution)/shard_map/ppermute | solution.py:313
  8.2 10.6 %collective-permute-start.5 = (f32[96,8,128]{2,1,0:T(8,128)S(1)}, f32[96,8,128]{2,1,0:T(8,128)S(1)}, u32[]{:S(2)}, u32[]{:S(2)}) collective-permute-start(f32[96,8,128]{2,1,0:T(8,128)S(1)} %get-tuple-element.56), channel_id=1, source_target_pairs={{0,192},{64,0},{128,64},{192,128},{1,193},{65,1},{129,65},{193,129... | collective-permute-start | bytes 1179656 | tf_op jit(solution)/shard_map/ppermute | solution.py:313
  10.6 8.4 %collective-permute-start.4 = (f32[96,8,128]{2,1,0:T(8,128)S(1)}, f32[96,8,128]{2,1,0:T(8,128)S(1)}, u32[]{:S(2)}, u32[]{:S(2)}) collective-permute-start(f32[96,8,128]{2,1,0:T(8,128)S(1)} %get-tuple-element.53), channel_id=1, source_target_pairs={{0,64},{64,128},{128,192},{192,0},{1,65},{65,129},{129,193},{193,1... | collective-permute-start | bytes 1179656 | tf_op jit(solution)/shard_map/ppermute | solution.py:313
  10.6 4.0 %collective-permute-start.2 = (f32[8,8,128]{2,1,0:T(8,128)S(1)}, f32[8,8,128]{2,1,0:T(8,128)S(1)}, u32[]{:S(2)}, u32[]{:S(2)}) collective-permute-start(f32[8,8,128]{2,1,0:T(8,128)S(1)} %get-tuple-element.51), channel_id=1, source_target_pairs={{0,16},{16,32},{32,48},{48,0},{1,17},{17,33},{33,49},{49,1},{2,18}... | collective-permute-start | bytes 98312 | tf_op jit(solution)/shard_map/ppermute | solution.py:313
  14.6 3.9 %collective-permute-start.3 = (f32[8,8,128]{2,1,0:T(8,128)S(1)}, f32[8,8,128]{2,1,0:T(8,128)S(1)}, u32[]{:S(2)}, u32[]{:S(2)}) collective-permute-start(f32[8,8,128]{2,1,0:T(8,128)S(1)} %get-tuple-element.52), channel_id=1, source_target_pairs={{0,48},{16,0},{32,16},{48,32},{1,49},{17,1},{33,17},{49,33},{2,50}... | collective-permute-start | bytes 98312 | tf_op jit(solution)/shard_map/ppermute | solution.py:313
  19.3 15.9 %collective-permute-start.6 = (f32[8,96,128]{2,1,0:T(8,128)S(1)}, f32[8,96,128]{2,1,0:T(8,128)S(1)}, u32[]{:S(2)}, u32[]{:S(2)}) collective-permute-start(f32[8,96,128]{2,1,0:T(8,128)S(1)} %get-tuple-element.58.refs_9_), channel_id=1, source_target_pairs={{0,1},{1,2},{2,3},{3,4},{4,5},{5,6},{6,7},{7,8},{8,9},{9,10},{10,1... | collective-permute-start | bytes 1179656 | tf_op jit(solution)/shard_map/ppermute | solution.py:313
  25.2 10.1 %collective-permute-start.7 = (f32[8,96,128]{2,1,0:T(8,128)S(1)}, f32[8,96,128]{2,1,0:T(8,128)S(1)}, u32[]{:S(2)}, u32[]{:S(2)}) collective-permute-start(f32[8,96,128]{2,1,0:T(8,128)S(1)} %get-tuple-element.59.refs_8_), channel_id=1, source_target_pairs={{0,15},{1,0},{2,1},{3,2},{4,3},{5,4},{6,5},{7,6},{8,7},{9,8},{10,9... | collective-permute-start | bytes 1179656 | tf_op jit(solution)/shard_map/ppermute | solution.py:313
  25.2 10.3 %collective-permute-start.11 = (f32[96,8,128]{2,1,0:T(8,128)S(1)}, f32[96,8,128]{2,1,0:T(8,128)S(1)}, u32[]{:S(2)}, u32[]{:S(2)}) collective-permute-start(f32[96,8,128]{2,1,0:T(8,128)S(1)} %shard_map.63.refs_0_), channel_id=1, source_target_pairs={{0,192},{64,0},{128,64},{192,128},{1,193},{65,1},{129,65},{193,129... | collective-permute-start | bytes 1179656 | tf_op jit(solution)/shard_map/ppermute | solution.py:313
  27.5 8.7 %collective-permute-start.10 = (f32[96,8,128]{2,1,0:T(8,128)S(1)}, f32[96,8,128]{2,1,0:T(8,128)S(1)}, u32[]{:S(2)}, u32[]{:S(2)}) collective-permute-start(f32[96,8,128]{2,1,0:T(8,128)S(1)} %shard_map.65.refs_2_), channel_id=1, source_target_pairs={{0,64},{64,128},{128,192},{192,0},{1,65},{65,129},{129,193},{193,1... | collective-permute-start | bytes 1179656 | tf_op jit(solution)/shard_map/ppermute | solution.py:313
  27.5 4.3 %collective-permute-start.8 = (f32[8,8,128]{2,1,0:T(8,128)S(1)}, f32[8,8,128]{2,1,0:T(8,128)S(1)}, u32[]{:S(2)}, u32[]{:S(2)}) collective-permute-start(f32[8,8,128]{2,1,0:T(8,128)S(1)} %get-tuple-element.60), channel_id=1, source_target_pairs={{0,16},{16,32},{32,48},{48,0},{1,17},{17,33},{33,49},{49,1},{2,18}... | collective-permute-start | bytes 98312 | tf_op jit(solution)/shard_map/ppermute | solution.py:313
  36.5 14.7 %collective-permute-start.12 = (f32[8,96,128]{2,1,0:T(8,128)S(1)}, f32[8,96,128]{2,1,0:T(8,128)S(1)}, u32[]{:S(2)}, u32[]{:S(2)}) collective-permute-start(f32[8,96,128]{2,1,0:T(8,128)S(1)} %get-tuple-element.65.refs_9_), channel_id=1, source_target_pairs={{0,1},{1,2},{2,3},{3,4},{4,5},{5,6},{6,7},{7,8},{8,9},{9,10},{10,1... | collective-permute-start | bytes 1179656 | tf_op jit(solution)/shard_map/ppermute | solution.py:313
  40.0 11.2 %collective-permute-start.13 = (f32[8,96,128]{2,1,0:T(8,128)S(1)}, f32[8,96,128]{2,1,0:T(8,128)S(1)}, u32[]{:S(2)}, u32[]{:S(2)}) collective-permute-start(f32[8,96,128]{2,1,0:T(8,128)S(1)} %get-tuple-element.66.refs_8_), channel_id=1, source_target_pairs={{0,15},{1,0},{2,1},{3,2},{4,3},{5,4},{6,5},{7,6},{8,7},{9,8},{10,9... | collective-permute-start | bytes 1179656 | tf_op jit(solution)/shard_map/ppermute | solution.py:313
  40.6 10.9 %collective-permute-start.17 = (f32[96,8,128]{2,1,0:T(8,128)S(1)}, f32[96,8,128]{2,1,0:T(8,128)S(1)}, u32[]{:S(2)}, u32[]{:S(2)}) collective-permute-start(f32[96,8,128]{2,1,0:T(8,128)S(1)} %shard_map.68.refs_0_), channel_id=1, source_target_pairs={{0,192},{64,0},{128,64},{192,128},{1,193},{65,1},{129,65},{193,129... | collective-permute-start | bytes 1179656 | tf_op jit(solution)/shard_map/ppermute | solution.py:313
  43.5 8.7 %collective-permute-start.16 = (f32[96,8,128]{2,1,0:T(8,128)S(1)}, f32[96,8,128]{2,1,0:T(8,128)S(1)}, u32[]{:S(2)}, u32[]{:S(2)}) collective-permute-start(f32[96,8,128]{2,1,0:T(8,128)S(1)} %shard_map.70.refs_2_), channel_id=1, source_target_pairs={{0,64},{64,128},{128,192},{192,0},{1,65},{65,129},{129,193},{193,1... | collective-permute-start | bytes 1179656 | tf_op jit(solution)/shard_map/ppermute | solution.py:313
  43.5 4.3 %collective-permute-start.14 = (f32[8,8,128]{2,1,0:T(8,128)S(1)}, f32[8,8,128]{2,1,0:T(8,128)S(1)}, u32[]{:S(2)}, u32[]{:S(2)}) collective-permute-start(f32[8,8,128]{2,1,0:T(8,128)S(1)} %get-tuple-element.67), channel_id=1, source_target_pairs={{0,16},{16,32},{32,48},{48,0},{1,17},{17,33},{33,49},{49,1},{2,18}... | collective-permute-start | bytes 98312 | tf_op jit(solution)/shard_map/ppermute | solution.py:313
  47.8 3.4 %collective-permute-start.15 = (f32[8,8,128]{2,1,0:T(8,128)S(1)}, f32[8,8,128]{2,1,0:T(8,128)S(1)}, u32[]{:S(2)}, u32[]{:S(2)}) collective-permute-start(f32[8,8,128]{2,1,0:T(8,128)S(1)} %get-tuple-element.68), channel_id=1, source_target_pairs={{0,48},{16,0},{32,16},{48,32},{1,49},{17,1},{33,17},{49,33},{2,50}... | collective-permute-start | bytes 98312 | tf_op jit(solution)/shard_map/ppermute | solution.py:313
  52.5 14.7 %collective-permute-start.18 = (f32[8,96,128]{2,1,0:T(8,128)S(1)}, f32[8,96,128]{2,1,0:T(8,128)S(1)}, u32[]{:S(2)}, u32[]{:S(2)}) collective-permute-start(f32[8,96,128]{2,1,0:T(8,128)S(1)} %get-tuple-element.72.refs_9_), channel_id=1, source_target_pairs={{0,1},{1,2},{2,3},{3,4},{4,5},{5,6},{6,7},{7,8},{8,9},{9,10},{10,1... | collective-permute-start | bytes 1179656 | tf_op jit(solution)/shard_map/ppermute | solution.py:313
  55.2 12.0 %collective-permute-start.19 = (f32[8,96,128]{2,1,0:T(8,128)S(1)}, f32[8,96,128]{2,1,0:T(8,128)S(1)}, u32[]{:S(2)}, u32[]{:S(2)}) collective-permute-start(f32[8,96,128]{2,1,0:T(8,128)S(1)} %get-tuple-element.73.refs_8_), channel_id=1, source_target_pairs={{0,15},{1,0},{2,1},{3,2},{4,3},{5,4},{6,5},{7,6},{8,7},{9,8},{10,9... | collective-permute-start | bytes 1179656 | tf_op jit(solution)/shard_map/ppermute | solution.py:313
  56.6 12.3 %collective-permute-start.23 = (f32[96,8,128]{2,1,0:T(8,128)S(1)}, f32[96,8,128]{2,1,0:T(8,128)S(1)}, u32[]{:S(2)}, u32[]{:S(2)}) collective-permute-start(f32[96,8,128]{2,1,0:T(8,128)S(1)} %shard_map.73.refs_0_), channel_id=1, source_target_pairs={{0,192},{64,0},{128,64},{192,128},{1,193},{65,1},{129,65},{193,129... | collective-permute-start | bytes 1179656 | tf_op jit(solution)/shard_map/ppermute | solution.py:313
  59.5 9.6 %collective-permute-start.22 = (f32[96,8,128]{2,1,0:T(8,128)S(1)}, f32[96,8,128]{2,1,0:T(8,128)S(1)}, u32[]{:S(2)}, u32[]{:S(2)}) collective-permute-start(f32[96,8,128]{2,1,0:T(8,128)S(1)} %shard_map.75.refs_2_), channel_id=1, source_target_pairs={{0,64},{64,128},{128,192},{192,0},{1,65},{65,129},{129,193},{193,1... | collective-permute-start | bytes 1179656 | tf_op jit(solution)/shard_map/ppermute | solution.py:313
  59.5 4.3 %collective-permute-start.20 = (f32[8,8,128]{2,1,0:T(8,128)S(1)}, f32[8,8,128]{2,1,0:T(8,128)S(1)}, u32[]{:S(2)}, u32[]{:S(2)}) collective-permute-start(f32[8,8,128]{2,1,0:T(8,128)S(1)} %get-tuple-element.74), channel_id=1, source_target_pairs={{0,16},{16,32},{32,48},{48,0},{1,17},{17,33},{33,49},{49,1},{2,18}... | collective-permute-start | bytes 98312 | tf_op jit(solution)/shard_map/ppermute | solution.py:313
  69.8 5.7 %collective-permute-start.24 = (f32[4,96,128]{2,1,0:T(8,128)S(1)}, f32[4,96,128]{2,1,0:T(8,128)S(1)}, u32[]{:S(2)}, u32[]{:S(2)}) collective-permute-start(f32[4,96,128]{2,1,0:T(8,128)S(1)} %get-tuple-element.82), channel_id=1, source_target_pairs={{0,1},{1,0},{2,3},{3,2},{4,5},{5,4},{6,7},{7,6},{8,9},{9,8},{10,11... | collective-permute-start | bytes 589832 | tf_op jit(solution)/shard_map/ppermute | solution.py:313
  102.0 4.4 %collective-permute-start.25 = (f32[4,96,128]{2,1,0:T(8,128)S(1)}, f32[4,96,128]{2,1,0:T(8,128)S(1)}, u32[]{:S(2)}, u32[]{:S(2)}) collective-permute-start(f32[4,96,128]{2,1,0:T(8,128)S(1)} %get-tuple-element.83), channel_id=1, source_target_pairs={{0,1},{1,0},{2,3},{3,2},{4,5},{5,4},{6,7},{7,6},{8,9},{9,8},{10,11... | collective-permute-start | bytes 589832 | tf_op jit(solution)/shard_map/ppermute | solution.py:313
  (7 other events, 46.7 us)

commit v5 on v4

--- a/solution.py
+++ b/solution.py
@@ -87,8 +87,9 @@
     return plane.reshape(cells * 8, 128)[pl.ds(at, cells, 8), :]
 
 
-def inner_kernel(parts, height, *refs):
-    field, (fy, fx, fz), (out, low, high) = refs[:parts], refs[parts : parts + 3], refs[parts + 3 :]
+def inner_kernel(parts, height, scale, *refs):
+    field, (fy, fx, fz) = refs[:parts], refs[parts : parts + 3]
+    (out, low, high), sums = refs[parts + 3 : parts + 6], refs[parts + 6 :]
     cells = fy.shape[1]
     planes = [low, *(out.at[y] for y in range(height - 2)), high]
     nothing = lambda x: jnp.zeros((8, 128), jnp.float32)
@@ -104,13 +105,21 @@
                 )
 
         march(cells, lambda x, ys=ys: [rows[y + 1](x) for y in ys], cell)
-
-
-def mend_kernel(parts, height, *refs):
+    for held in sums:
+        for k in range(height - 2):
+
+            def put(x, value, k=k):
+                held[k, x] = value
+
+            running_sums(scale, out.at[k], put)
+
+
+def mend_kernel(parts, height, scale, *refs):
     field, (fy, fx, fz) = refs[:parts], refs[parts : parts + 3]
     (zlo, zhi), (first, last) = refs[parts + 3 : parts + 5], refs[parts + 5 : parts + 7]
     to_first, to_last = refs[parts + 7 : parts + 9]
-    sides, out = refs[parts + 9 : parts + 11], refs[parts + 12]
+    sides, outs = refs[parts + 9 : parts + 11], refs[parts + 12 :]
+    out, held, lift = (outs[0], None, None) if scale is None else outs[1:]
     cells = fy.shape[1]
     rows = [reader(plane) for plane in planes_of(field, height)]
     for y in range(1, height - 1):
@@ -127,6 +136,13 @@
                 *along_z(here, zlo, zhi, y, x),
                 *(fy[y, x], fx[y, x], fz[y, x]),
             )
+        if held is not None:
+            lift[y - 1] = (to_first[y] * (zlo[y] - last[y])) * scale
+            sums = held.at[y - 1].reshape(cells * 8, 128)
+            sums[pl.ds(7, cells, 8), :] += (to_last[y] * (zhi[y] - first[y])) * scale
+            for x in (0, cells - 1):
+                held[y - 1, x] = summed(out[y - 1, x] * scale)
+                lift[y - 1, pl.ds(x, 1), :] = jnp.zeros((1, 128), jnp.float32)
 
 
 def rim_kernel(parts, height, top, *refs):
@@ -189,35 +205,30 @@
         right[y] = plane[plane.shape[0] - 1]
 
 
+def summed(value):
+    sublane = lax.broadcasted_iota(jnp.int32, (8, 128), 0)
+    for reach in (1, 2, 4):
+        value = value + jnp.where(sublane >= reach, pltpu.roll(value, reach, 0), 0.0)
+    return value
+
+
 def running_sums(scale, plane, put):
-    sublane = lax.broadcasted_iota(jnp.int32, (8, 128), 0)
-
     def body(i, carry):
         start = pl.multiple_of(i * BLOCK, BLOCK)
         for k in range(BLOCK):
-            value = plane[start + k] * scale
-            for reach in (1, 2, 4):
-                value = value + jnp.where(sublane >= reach, pltpu.roll(value, reach, 0), 0.0)
-            put(start + k, value)
+            put(start + k, summed(plane[start + k] * scale))
         return carry
 
     lax.fori_loop(0, plane.shape[0] // BLOCK, body, 0)
 
 
-def inner_sums_kernel(scale, inner, held, end, done):
-    count = inner.shape[0]
-    copy = pltpu.make_async_copy(inner, end.at[pl.ds(1, count)], done.at[0])
+def write_kernel(inner, end, done):
+    copy = pltpu.make_async_copy(inner, end.at[pl.ds(1, inner.shape[0])], done.at[0])
     copy.start()
-    for y in range(count):
-
-        def put(x, value, y=y):
-            held[y, x] = value
-
-        running_sums(scale, inner.at[y], put)
     copy.wait()
 
 
-def rim_sums_kernel(scale, core, low, high, inner_held, own, other, held):
+def rim_sums_kernel(scale, core, low, high, inner_held, lift, own, other, held):
     half = own.shape[0]
     for k, plane in enumerate((low, high)):
 
@@ -227,17 +238,21 @@
         running_sums(scale, plane, put)
     planes = planes_of((held.at[0], inner_held, held.at[1]), 2 * half)
 
+    def total(y):
+        over = pack(planes[y], 7)
+        return over if y in (0, 2 * half - 1) else over + lift[y - 1]
+
     @pl.when(core[0] == 0)
     def _():
         for y in range(half):
-            own[y] = pack(planes[y], 7)
-            other[y] = pack(planes[half + y], 7)
+            own[y] = total(y)
+            other[y] = total(half + y)
 
     @pl.when(core[0] != 0)
     def _():
         for y in range(half):
-            own[y] = pack(planes[half + y], 7)
-            other[y] = pack(planes[y], 7)
+            own[y] = total(half + y)
+            other[y] = total(y)
 
 
 def add_kernel(a, b, out):
@@ -263,19 +278,20 @@
         partners[...] = chips[...]
 
 
-def half_potential(side, inner_held, rim_held, before, out, filled, done):
+def half_potential(side, inner_held, rim_held, lift, before, out, filled, base, done):
     half, cells = before.shape[:2]
     planes = planes_of((rim_held.at[0], inner_held, rim_held.at[1]), 2 * half)
 
     def fill(which):
         for j in range(half):
             y = which * half + j
+            base[j] = before[j] if y in (0, 2 * half - 1) else before[j] + lift[y - 1]
 
             def body(i, carry, y=y, j=j):
                 start = pl.multiple_of(i * BLOCK, BLOCK)
                 for k in range(BLOCK):
                     x = start + k
-                    filled[j, x] = planes[y][x] + jnp.broadcast_to(before[j, pl.ds(x, 1), :], (8, 128))
+                    filled[j, x] = planes[y][x] + jnp.broadcast_to(base[j, pl.ds(x, 1), :], (8, 128))
                 return carry
 
             lax.fori_loop(0, cells // BLOCK, body, 0)
@@ -292,20 +308,20 @@
         fill(1)
 
 
-def own_half_kernel(core, low, high, inner_held, rim_held, before, end_in, out, end, filled, done, done_rims):
+def own_half_kernel(core, low, high, inner_held, rim_held, lift, before, end_in, out, end, filled, base, done, done_rims):
     copies = [
         pltpu.make_async_copy(low, end.at[0], done_rims.at[0]),
         pltpu.make_async_copy(high, end.at[end.shape[0] - 1], done_rims.at[1]),
     ]
     for copy in copies:
         copy.start()
-    half_potential(core[0], inner_held, rim_held, before, out, filled, done)
+    half_potential(core[0], inner_held, rim_held, lift, before, out, filled, base, done)
     for copy in copies:
         copy.wait()
 
 
-def other_half_kernel(core, inner_held, rim_held, before, out_in, out, filled, done):
-    half_potential(1 - core[0], inner_held, rim_held, before, out, filled, done)
+def other_half_kernel(core, inner_held, rim_held, lift, before, out_in, out, filled, base, done):
+    half_potential(1 - core[0], inner_held, rim_held, lift, before, out, filled, base, done)
 
 
 def sent(array, axis, by):
@@ -322,6 +338,8 @@
     whole = shape(*field_values.shape)
     edge, side = shape(height, cells, 128), shape(height, 8, 128)
     scalar = pl.BlockSpec(memory_space=pltpu.SMEM)
+    chips = lax.axis_size("chip")
+    scale = 1.0 / (8 * chips * 2)
 
     def send_faces(field):
         first, last, left, right = call(
@@ -343,14 +361,19 @@
     near = call(near_kernel, (edge, edge), flow_z)
     for step in range(1, STEPS + 1):
         parts = len(field)
-        mid, *rims = call(
-            functools.partial(inner_kernel, parts, height), (inner, row, row), *(*field, *flows), flops=1 << 23
+        last_scale = scale if step == STEPS else None
+        sums = () if last_scale is None else (inner,)
+        mid, low_part, high_part, *held = call(
+            functools.partial(inner_kernel, parts, height, scale),
+            (inner, row, row, *sums),
+            *(*field, *flows),
+            flops=1 << 23,
         )
-        (mid,) = call(
-            functools.partial(mend_kernel, parts, height),
-            (inner,),
-            *(*field, *flows, *downs, *faces, *near, *sides, mid),
-            alias={parts + 11: 0},
+        mid, *held = call(
+            functools.partial(mend_kernel, parts, height, last_scale),
+            (inner, inner, shape(height - 2, cells, 128)) if held else (inner,),
+            *(*field, *flows, *downs, *faces, *near, *sides, mid, *held),
+            alias={parts + 11: 0, parts + 12: 1} if held else {parts + 11: 0},
         )
         low, high = (
             call(
@@ -359,53 +382,46 @@
                 *(*field, *flows, *downs, *faces, *near, *sides, beyond, rim),
                 alias={parts + 12: 0},
             )[0]
-            for top, beyond, rim in ((False, slo, rims[0]), (True, shi, rims[1]))
+            for top, beyond, rim in ((False, slo, low_part), (True, shi, high_part))
         )
         field = (low, mid, high)
         if step < STEPS:
             slo, shi = send_rim(low, high)
             faces, downs, sides = send_faces(field)
-    chips = lax.axis_size("chip")
-    scale = 1.0 / (8 * chips * 2)
-    inner_held, end = call(
-        functools.partial(inner_sums_kernel, scale),
-        (inner, whole),
-        mid,
-        out_specs=[IN_VMEM, IN_HBM],
-        scratch=[pltpu.SemaphoreType.DMA((1,))],
-    )
+    inner_held, lift = held
     quarter = shape(height // 2, cells, 128)
     own, other, rim_held = call(
         functools.partial(rim_sums_kernel, scale),
         (quarter, quarter, pair),
-        *(core, low, high, inner_held),
-        in_specs=[scalar, *[IN_VMEM] * 3],
+        *(core, low, high, inner_held, lift),
+        in_specs=[scalar, *[IN_VMEM] * 4],
     )
     got = sent(other, "core", 1)
+    (end,) = call(write_kernel, (whole,), mid, out_specs=[IN_HBM], scratch=[pltpu.SemaphoreType.DMA((1,))])
     (total,) = call(add_kernel, (quarter,), own, got)
     pieces = lax.all_to_all(total.reshape(chips, -1, 128), "chip", 0, 0, tiled=True)
     (pieces,) = call(before_kernel, (shape(*pieces.shape),), pieces)
     below = lax.all_to_all(pieces, "chip", 0, 0, tiled=True).reshape(total.shape)
     mine, partners = call(split_kernel, (quarter, quarter), core, below, own, got, in_specs=[scalar, *[IN_VMEM] * 3])
     theirs = sent(partners, "core", 1)
-    rows_out = [pltpu.VMEM((height // 2, cells, 8, 128), jnp.float32), pltpu.SemaphoreType.DMA((height // 2,))]
+    rows_out = [pltpu.VMEM((height // 2, cells, 8, 128), jnp.float32), pltpu.VMEM(quarter.shape, jnp.float32), pltpu.SemaphoreType.DMA((height // 2,))]
     potential, end = call(
         own_half_kernel,
         (whole, whole),
-        *(core, low, high, inner_held, rim_held, mine, end),
-        in_specs=[scalar, *[IN_VMEM] * 5, IN_HBM],
+        *(core, low, high, inner_held, rim_held, lift, mine, end),
+        in_specs=[scalar, *[IN_VMEM] * 6, IN_HBM],
         out_specs=[IN_HBM, IN_HBM],
         scratch=[*rows_out, pltpu.SemaphoreType.DMA((2,))],
-        alias={6: 1},
+        alias={7: 1},
     )
     (potential,) = call(
         other_half_kernel,
         (whole,),
-        *(core, inner_held, rim_held, theirs, potential),
-        in_specs=[scalar, *[IN_VMEM] * 3, IN_HBM],
+        *(core, inner_held, rim_held, lift, theirs, potential),
+        in_specs=[scalar, *[IN_VMEM] * 4, IN_HBM],
         out_specs=[IN_HBM],
         scratch=rows_out,
-        alias={4: 0},
+        alias={5: 0},
     )
     return potential, end
 

time: 108 us -> 106 us (0.981)
  starting transfers between devices: 43.3 us -> 40.8 us
  local copies, waits for them, and re-layouts: 3.79 us -> 1.9 us
  Pallas kernels: 15.9 us -> 17.4 us
    ppermute x26, starting transfers between devices: 43.3 us -> 40.8 us  [sent(): lax.ppermute(array, axis, [(i, (i + by) % size) for i in range(size)])]
    unnamed x10 -> x8, local copies, waits for them, and re-layouts: 3.79 us -> 1.9 us
    pallas_call x29, Pallas kernels: 15.9 us -> 17.4 us  [call(): pl.pallas_call(kernel, out_shape=outs, in_specs=in_specs or [IN_VMEM] * l...]
  transfers between devices with their start and end apart: 26 -> 26, of which waited for: 7 -> 6; matrix products, arithmetic and copies ran while one was open for 0% -> 0% of each run, Pallas kernels for 12% -> 14%
where the time goes in v5:
time: 106 us; the launch traced here: 105 us
  starting transfers between devices  40.8 us (38%)
  blocking collectives  26.6 us (25%)
  waiting for transfers between devices  17.6 us (17%)
  Pallas kernels  17.4 us (16%)
  local copies, waits for them, and re-layouts  1.9 us (2%)
  between operations  1.19 us (1%)
    ppermute x26, starting transfers between devices, sent(): lax.ppermute(array, axis, [(i, (i + by) % size) for i in range(size)])  40.8 us
    ppermute x26, waiting for transfers between devices, sent(): lax.ppermute(array, axis, [(i, (i + by) % size) for i in range(size)])  17.6 us
    pallas_call x29, Pallas kernels, call(): pl.pallas_call(kernel, out_shape=outs, in_specs=in_specs or [IN_VMEM] * l...  17.4 us
    all_to_all x1, blocking collectives, local(): lax.all_to_all(total.reshape(chips, -1, 128), 'chip', 0, 0, tiled=True)  15.3 us
    all_to_all x1, blocking collectives, local(): lax.all_to_all(pieces, 'chip', 0, 0, tiled=True).reshape(total.shape)  11.3 us
  transfers between devices with their start and end apart: 26, of which 6 were waited for; matrix products, arithmetic and copies ran while one was open for 0% of the time, Pallas kernels for 14%

profile of v5, /device:TPU:1, one launch (start us, length us, event | category | flops | bytes accessed | tf_op | source)
XLA Modules:
  0.0 105.5 jit_solution(9771483719062985379)
XLA Ops:
  0.6 1.9 %copy-done.3 = f32[8,96,8,128]{3,2,1,0:T(8,128)S(1)} copy-done((f32[8,96,8,128]{3,2,1,0:T(8,128)S(1)}, f32[8,96,8,128]{3,2,1,0:T(8,128)}, u32[]{:S(2)}) %copy-start.3) | copy-done | bytes 3145752
  2.9 2.1 %collective-permute-start.4 = (f32[96,8,128]{2,1,0:T(8,128)S(1)}, f32[96,8,128]{2,1,0:T(8,128)S(1)}, u32[]{:S(2)}, u32[]{:S(2)}) collective-permute-start(f32[96,8,128]{2,1,0:T(8,128)S(1)} %get-tuple-element.55), channel_id=1, source_target_pairs={{0,64},{64,128},{128,192},{192,0},{1,65},{65,129},{129,193},{193,1... | collective-permute-start | bytes 1179656 | tf_op jit(solution)/shard_map/ppermute | solution.py:329
  5.2 2.5 %collective-permute-start = (f32[8,96,128]{2,1,0:T(8,128)S(1)}, f32[8,96,128]{2,1,0:T(8,128)S(1)}, u32[]{:S(2)}, u32[]{:S(2)}) collective-permute-start(f32[8,96,128]{2,1,0:T(8,128)S(1)} %get-tuple-element.49.refs_7_), channel_id=1, source_target_pairs={{0,1},{1,2},{2,3},{3,4},{4,5},{5,6},{6,7},{7,8},{8,9},{9,10},{10,1... | collective-permute-start | bytes 1179656 | tf_op jit(solution)/shard_map/ppermute | solution.py:329
  7.7 1.7 %collective-permute-start.5 = (f32[96,8,128]{2,1,0:T(8,128)S(1)}, f32[96,8,128]{2,1,0:T(8,128)S(1)}, u32[]{:S(2)}, u32[]{:S(2)}) collective-permute-start(f32[96,8,128]{2,1,0:T(8,128)S(1)} %get-tuple-element.58), channel_id=1, source_target_pairs={{0,192},{64,0},{128,64},{192,128},{1,193},{65,1},{129,65},{193,129... | collective-permute-start | bytes 1179656 | tf_op jit(solution)/shard_map/ppermute | solution.py:329
  10.5 3.2 %collective-permute-done.2.refs_10_ = f32[8,8,128]{2,1,0:T(8,128)S(1)} collective-permute-done((f32[8,8,128]{2,1,0:T(8,128)S(1)}, f32[8,8,128]{2,1,0:T(8,128)S(1)}, u32[]{:S(2)}, u32[]{:S(2)}) %collective-permute-start.2) | collective-permute-done | bytes 32800 | tf_op jit(solution)/shard_map/ppermute | solution.py:329
  15.1 1.9 %shard_map.62 = (f32[6,96,8,128]{3,2,1,0:T(8,128)S(1)}, f32[96,8,128]{2,1,0:T(8,128)S(1)}, f32[96,8,128]{2,1,0:T(8,128)S(1)}) custom-call(f32[8,96,8,128]{3,2,1,0:T(8,128)S(1)} %copy-done.3, f32[8,96,8,128]{3,2,1,0:T(8,128)S(1)} %copy-done.1, f32[8,96,8,128]{3,2,1,0:T(8,128)S(1)} %copy-done.2, f32[8,96,8,128]{3,2,1,0:T(8,128)S(1)} %copy-done), custom_call_target="tpu_custom_call" | custom-call | flops 8388608 | tf_op jit(solution)/shard_map/pallas_call | solution.py:28
  19.2 3.5 %collective-permute-start.6 = (f32[8,96,128]{2,1,0:T(8,128)S(1)}, f32[8,96,128]{2,1,0:T(8,128)S(1)}, u32[]{:S(2)}, u32[]{:S(2)}) collective-permute-start(f32[8,96,128]{2,1,0:T(8,128)S(1)} %get-tuple-element.60.refs_9_), channel_id=1, source_target_pairs={{0,1},{1,2},{2,3},{3,4},{4,5},{5,6},{6,7},{7,8},{8,9},{9,10},{10,1... | collective-permute-start | bytes 1179656 | tf_op jit(solution)/shard_map/ppermute | solution.py:329
  22.7 1.8 %collective-permute-start.7 = (f32[8,96,128]{2,1,0:T(8,128)S(1)}, f32[8,96,128]{2,1,0:T(8,128)S(1)}, u32[]{:S(2)}, u32[]{:S(2)}) collective-permute-start(f32[8,96,128]{2,1,0:T(8,128)S(1)} %get-tuple-element.61.refs_8_), channel_id=1, source_target_pairs={{0,15},{1,0},{2,1},{3,2},{4,3},{5,4},{6,5},{7,6},{8,7},{9,8},{10,9... | collective-permute-start | bytes 1179656 | tf_op jit(solution)/shard_map/ppermute | solution.py:329
  24.7 4.2 %collective-permute-done.8.refs_12_ = f32[8,8,128]{2,1,0:T(8,128)S(1)} collective-permute-done((f32[8,8,128]{2,1,0:T(8,128)S(1)}, f32[8,8,128]{2,1,0:T(8,128)S(1)}, u32[]{:S(2)}, u32[]{:S(2)}) %collective-permute-start.8) | collective-permute-done | bytes 32800 | tf_op jit(solution)/shard_map/ppermute | solution.py:329
  28.9 1.5 %collective-permute-start.9 = (f32[8,8,128]{2,1,0:T(8,128)S(1)}, f32[8,8,128]{2,1,0:T(8,128)S(1)}, u32[]{:S(2)}, u32[]{:S(2)}) collective-permute-start(f32[8,8,128]{2,1,0:T(8,128)S(1)} %get-tuple-element.63), channel_id=1, source_target_pairs={{0,48},{16,0},{32,16},{48,32},{1,49},{17,1},{33,17},{49,33},{2,50}... | collective-permute-start | bytes 98312 | tf_op jit(solution)/shard_map/ppermute | solution.py:329
  30.4 1.9 %shard_map.67 = (f32[6,96,8,128]{3,2,1,0:T(8,128)S(1)}, f32[96,8,128]{2,1,0:T(8,128)S(1)}, f32[96,8,128]{2,1,0:T(8,128)S(1)}) custom-call(f32[96,8,128]{2,1,0:T(8,128)S(1)} %shard_map.63.refs_0_, f32[6,96,8,128]{3,2,1,0:T(8,128)S(1)} %shard_map.64.refs_1_, f32[96,8,128]{2,1,0:T(8,128)S(1)} %shard_map.65.refs_2_, f32[8,96,8,128]{3,2,1,0:T(8,128)S(1)} %copy-done.1, ...), custom_call_target="tpu_custom_call" | custom-call | flops 8388608 | tf_op jit(solution)/shard_map/pallas_call | solution.py:28
  33.7 3.6 %collective-permute-start.12 = (f32[8,96,128]{2,1,0:T(8,128)S(1)}, f32[8,96,128]{2,1,0:T(8,128)S(1)}, u32[]{:S(2)}, u32[]{:S(2)}) collective-permute-start(f32[8,96,128]{2,1,0:T(8,128)S(1)} %get-tuple-element.67.refs_9_), channel_id=1, source_target_pairs={{0,1},{1,2},{2,3},{3,4},{4,5},{5,6},{6,7},{7,8},{8,9},{9,10},{10,1... | collective-permute-start | bytes 1179656 | tf_op jit(solution)/shard_map/ppermute | solution.py:329
  38.1 2.7 %collective-permute-start.17 = (f32[96,8,128]{2,1,0:T(8,128)S(1)}, f32[96,8,128]{2,1,0:T(8,128)S(1)}, u32[]{:S(2)}, u32[]{:S(2)}) collective-permute-start(f32[96,8,128]{2,1,0:T(8,128)S(1)} %shard_map.68.refs_0_), channel_id=1, source_target_pairs={{0,192},{64,0},{128,64},{192,128},{1,193},{65,1},{129,65},{193,129... | collective-permute-start | bytes 1179656 | tf_op jit(solution)/shard_map/ppermute | solution.py:329
  40.8 4.3 %collective-permute-done.14.refs_12_ = f32[8,8,128]{2,1,0:T(8,128)S(1)} collective-permute-done((f32[8,8,128]{2,1,0:T(8,128)S(1)}, f32[8,8,128]{2,1,0:T(8,128)S(1)}, u32[]{:S(2)}, u32[]{:S(2)}) %collective-permute-start.14) | collective-permute-done | bytes 32800 | tf_op jit(solution)/shard_map/ppermute | solution.py:329
  45.0 1.5 %collective-permute-start.15 = (f32[8,8,128]{2,1,0:T(8,128)S(1)}, f32[8,8,128]{2,1,0:T(8,128)S(1)}, u32[]{:S(2)}, u32[]{:S(2)}) collective-permute-start(f32[8,8,128]{2,1,0:T(8,128)S(1)} %get-tuple-element.70), channel_id=1, source_target_pairs={{0,48},{16,0},{32,16},{48,32},{1,49},{17,1},{33,17},{49,33},{2,50}... | collective-permute-start | bytes 98312 | tf_op jit(solution)/shard_map/ppermute | solution.py:329
  46.5 1.9 %shard_map.72 = (f32[6,96,8,128]{3,2,1,0:T(8,128)S(1)}, f32[96,8,128]{2,1,0:T(8,128)S(1)}, f32[96,8,128]{2,1,0:T(8,128)S(1)}) custom-call(f32[96,8,128]{2,1,0:T(8,128)S(1)} %shard_map.68.refs_0_, f32[6,96,8,128]{3,2,1,0:T(8,128)S(1)} %shard_map.69.refs_1_, f32[96,8,128]{2,1,0:T(8,128)S(1)} %shard_map.70.refs_2_, f32[8,96,8,128]{3,2,1,0:T(8,128)S(1)} %copy-done.1, ...), custom_call_target="tpu_custom_call" | custom-call | flops 8388608 | tf_op jit(solution)/shard_map/pallas_call | solution.py:28
  51.2 4.2 %collective-permute-start.19 = (f32[8,96,128]{2,1,0:T(8,128)S(1)}, f32[8,96,128]{2,1,0:T(8,128)S(1)}, u32[]{:S(2)}, u32[]{:S(2)}) collective-permute-start(f32[8,96,128]{2,1,0:T(8,128)S(1)} %get-tuple-element.75.refs_8_), channel_id=1, source_target_pairs={{0,15},{1,0},{2,1},{3,2},{4,3},{5,4},{6,5},{7,6},{8,7},{9,8},{10,9... | collective-permute-start | bytes 1179656 | tf_op jit(solution)/shard_map/ppermute | solution.py:329
  55.6 4.3 %collective-permute-done.20.refs_12_ = f32[8,8,128]{2,1,0:T(8,128)S(1)} collective-permute-done((f32[8,8,128]{2,1,0:T(8,128)S(1)}, f32[8,8,128]{2,1,0:T(8,128)S(1)}, u32[]{:S(2)}, u32[]{:S(2)}) %collective-permute-start.20) | collective-permute-done | bytes 32800 | tf_op jit(solution)/shard_map/ppermute | solution.py:329
  59.9 1.5 %collective-permute-start.21 = (f32[8,8,128]{2,1,0:T(8,128)S(1)}, f32[8,8,128]{2,1,0:T(8,128)S(1)}, u32[]{:S(2)}, u32[]{:S(2)}) collective-permute-start(f32[8,8,128]{2,1,0:T(8,128)S(1)} %get-tuple-element.77), channel_id=1, source_target_pairs={{0,48},{16,0},{32,16},{48,32},{1,49},{17,1},{33,17},{49,33},{2,50}... | collective-permute-start | bytes 98312 | tf_op jit(solution)/shard_map/ppermute | solution.py:329
  61.4 3.2 %shard_map.77 = (f32[6,96,8,128]{3,2,1,0:T(8,128)S(1)}, f32[96,8,128]{2,1,0:T(8,128)S(1)}, f32[96,8,128]{2,1,0:T(8,128)S(1)}, f32[6,96,8,128]{3,2,1,0:T(8,128)S(1)}) custom-call(f32[96,8,128]{2,1,0:T(8,128)S(1)} %shard_map.73.refs_0_, f32[6,96,8,128]{3,2,1,0:T(8,128)S(1)} %shard_map.74.refs_1_, f32[96,8,128]{2,1,0:T(8,128)S(1)} %shard_map.75.refs_2_, ...), custom_call_target="tpu_custom_call" | custom-call | flops 8388608 | tf_op jit(solution)/shard_map/pallas_call | solution.py:28
  66.0 4.4 %collective-permute-start.24 = (f32[4,96,128]{2,1,0:T(8,128)S(1)}, f32[4,96,128]{2,1,0:T(8,128)S(1)}, u32[]{:S(2)}, u32[]{:S(2)}) collective-permute-start(f32[4,96,128]{2,1,0:T(8,128)S(1)} %get-tuple-element.86), channel_id=1, source_target_pairs={{0,1},{1,0},{2,3},{3,2},{4,5},{5,4},{6,7},{7,6},{8,9},{9,8},{10,11... | collective-permute-start | bytes 589832 | tf_op jit(solution)/shard_map/ppermute | solution.py:329
  71.5 15.3 %all_to_all.10.pieces = f32[8,48,128]{2,1,0:T(8,128)S(1)} all-to-all(f32[8,48,128]{2,1,0:T(8,128)S(1)} %bitcast.4), channel_id=1, replica_groups=mesh['south'=4,'east'=4,'chip'=8,'core'=2] {'chip'}, dimensions={0} | all-to-all | bytes 393216 | tf_op jit(solution)/shard_map/all_to_all | solution.py:402
  86.9 11.3 %all_to_all.11 = f32[8,48,128]{2,1,0:T(8,128)S(1)} all-to-all(f32[8,48,128]{2,1,0:T(8,128)S(1)} %shard_map.83), channel_id=1, replica_groups=mesh['south'=4,'east'=4,'chip'=8,'core'=2] {'chip'}, dimensions={0} | all-to-all | bytes 393216 | tf_op jit(solution)/shard_map/all_to_all | solution.py:404
  98.2 2.9 %collective-permute-start.25 = (f32[4,96,128]{2,1,0:T(8,128)S(1)}, f32[4,96,128]{2,1,0:T(8,128)S(1)}, u32[]{:S(2)}, u32[]{:S(2)}) collective-permute-start(f32[4,96,128]{2,1,0:T(8,128)S(1)} %get-tuple-element.87), channel_id=1, source_target_pairs={{0,1},{1,0},{2,3},{3,2},{4,5},{5,4},{6,7},{7,6},{8,9},{9,8},{10,11... | collective-permute-start | bytes 589832 | tf_op jit(solution)/shard_map/ppermute | solution.py:329
  (67 shorter events, 17.0 us)
Async XLA Ops:
  2.9 14.2 %collective-permute-start.4 = (f32[96,8,128]{2,1,0:T(8,128)S(1)}, f32[96,8,128]{2,1,0:T(8,128)S(1)}, u32[]{:S(2)}, u32[]{:S(2)}) collective-permute-start(f32[96,8,128]{2,1,0:T(8,128)S(1)} %get-tuple-element.55), channel_id=1, source_target_pairs={{0,64},{64,128},{128,192},{192,0},{1,65},{65,129},{129,193},{193,1... | collective-permute-start | bytes 1179656 | tf_op jit(solution)/shard_map/ppermute | solution.py:329
  5.2 11.9 %collective-permute-start = (f32[8,96,128]{2,1,0:T(8,128)S(1)}, f32[8,96,128]{2,1,0:T(8,128)S(1)}, u32[]{:S(2)}, u32[]{:S(2)}) collective-permute-start(f32[8,96,128]{2,1,0:T(8,128)S(1)} %get-tuple-element.49.refs_7_), channel_id=1, source_target_pairs={{0,1},{1,2},{2,3},{3,4},{4,5},{5,6},{6,7},{7,8},{8,9},{9,10},{10,1... | collective-permute-start | bytes 1179656 | tf_op jit(solution)/shard_map/ppermute | solution.py:329
  7.7 9.4 %collective-permute-start.1 = (f32[8,96,128]{2,1,0:T(8,128)S(1)}, f32[8,96,128]{2,1,0:T(8,128)S(1)}, u32[]{:S(2)}, u32[]{:S(2)}) collective-permute-start(f32[8,96,128]{2,1,0:T(8,128)S(1)} %get-tuple-element.50.refs_6_), channel_id=1, source_target_pairs={{0,15},{1,0},{2,1},{3,2},{4,3},{5,4},{6,5},{7,6},{8,7},{9,8},{10,9... | collective-permute-start | bytes 1179656 | tf_op jit(solution)/shard_map/ppermute | solution.py:329
  7.7 11.2 %collective-permute-start.5 = (f32[96,8,128]{2,1,0:T(8,128)S(1)}, f32[96,8,128]{2,1,0:T(8,128)S(1)}, u32[]{:S(2)}, u32[]{:S(2)}) collective-permute-start(f32[96,8,128]{2,1,0:T(8,128)S(1)} %get-tuple-element.58), channel_id=1, source_target_pairs={{0,192},{64,0},{128,64},{192,128},{1,193},{65,1},{129,65},{193,129... | collective-permute-start | bytes 1179656 | tf_op jit(solution)/shard_map/ppermute | solution.py:329
  9.4 4.3 %collective-permute-start.2 = (f32[8,8,128]{2,1,0:T(8,128)S(1)}, f32[8,8,128]{2,1,0:T(8,128)S(1)}, u32[]{:S(2)}, u32[]{:S(2)}) collective-permute-start(f32[8,8,128]{2,1,0:T(8,128)S(1)} %get-tuple-element.53), channel_id=1, source_target_pairs={{0,16},{16,32},{32,48},{48,0},{1,17},{17,33},{33,49},{49,1},{2,18}... | collective-permute-start | bytes 98312 | tf_op jit(solution)/shard_map/ppermute | solution.py:329
  13.6 3.5 %collective-permute-start.3 = (f32[8,8,128]{2,1,0:T(8,128)S(1)}, f32[8,8,128]{2,1,0:T(8,128)S(1)}, u32[]{:S(2)}, u32[]{:S(2)}) collective-permute-start(f32[8,8,128]{2,1,0:T(8,128)S(1)} %get-tuple-element.54), channel_id=1, source_target_pairs={{0,48},{16,0},{32,16},{48,32},{1,49},{17,1},{33,17},{49,33},{2,50}... | collective-permute-start | bytes 98312 | tf_op jit(solution)/shard_map/ppermute | solution.py:329
  17.3 15.1 %collective-permute-start.11 = (f32[96,8,128]{2,1,0:T(8,128)S(1)}, f32[96,8,128]{2,1,0:T(8,128)S(1)}, u32[]{:S(2)}, u32[]{:S(2)}) collective-permute-start(f32[96,8,128]{2,1,0:T(8,128)S(1)} %shard_map.63.refs_0_), channel_id=1, source_target_pairs={{0,192},{64,0},{128,64},{192,128},{1,193},{65,1},{129,65},{193,129... | collective-permute-start | bytes 1179656 | tf_op jit(solution)/shard_map/ppermute | solution.py:329
  19.2 13.2 %collective-permute-start.6 = (f32[8,96,128]{2,1,0:T(8,128)S(1)}, f32[8,96,128]{2,1,0:T(8,128)S(1)}, u32[]{:S(2)}, u32[]{:S(2)}) collective-permute-start(f32[8,96,128]{2,1,0:T(8,128)S(1)} %get-tuple-element.60.refs_9_), channel_id=1, source_target_pairs={{0,1},{1,2},{2,3},{3,4},{4,5},{5,6},{6,7},{7,8},{8,9},{9,10},{10,1... | collective-permute-start | bytes 1179656 | tf_op jit(solution)/shard_map/ppermute | solution.py:329
  22.7 9.7 %collective-permute-start.7 = (f32[8,96,128]{2,1,0:T(8,128)S(1)}, f32[8,96,128]{2,1,0:T(8,128)S(1)}, u32[]{:S(2)}, u32[]{:S(2)}) collective-permute-start(f32[8,96,128]{2,1,0:T(8,128)S(1)} %get-tuple-element.61.refs_8_), channel_id=1, source_target_pairs={{0,15},{1,0},{2,1},{3,2},{4,3},{5,4},{6,5},{7,6},{8,7},{9,8},{10,9... | collective-permute-start | bytes 1179656 | tf_op jit(solution)/shard_map/ppermute | solution.py:329
  24.5 8.9 %collective-permute-start.10 = (f32[96,8,128]{2,1,0:T(8,128)S(1)}, f32[96,8,128]{2,1,0:T(8,128)S(1)}, u32[]{:S(2)}, u32[]{:S(2)}) collective-permute-start(f32[96,8,128]{2,1,0:T(8,128)S(1)} %shard_map.65.refs_2_), channel_id=1, source_target_pairs={{0,64},{64,128},{128,192},{192,0},{1,65},{65,129},{129,193},{193,1... | collective-permute-start | bytes 1179656 | tf_op jit(solution)/shard_map/ppermute | solution.py:329
  24.7 4.3 %collective-permute-start.8 = (f32[8,8,128]{2,1,0:T(8,128)S(1)}, f32[8,8,128]{2,1,0:T(8,128)S(1)}, u32[]{:S(2)}, u32[]{:S(2)}) collective-permute-start(f32[8,8,128]{2,1,0:T(8,128)S(1)} %get-tuple-element.62), channel_id=1, source_target_pairs={{0,16},{16,32},{32,48},{48,0},{1,17},{17,33},{33,49},{49,1},{2,18}... | collective-permute-start | bytes 98312 | tf_op jit(solution)/shard_map/ppermute | solution.py:329
  32.6 15.9 %collective-permute-start.16 = (f32[96,8,128]{2,1,0:T(8,128)S(1)}, f32[96,8,128]{2,1,0:T(8,128)S(1)}, u32[]{:S(2)}, u32[]{:S(2)}) collective-permute-start(f32[96,8,128]{2,1,0:T(8,128)S(1)} %shard_map.70.refs_2_), channel_id=1, source_target_pairs={{0,64},{64,128},{128,192},{192,0},{1,65},{65,129},{129,193},{193,1... | collective-permute-start | bytes 1179656 | tf_op jit(solution)/shard_map/ppermute | solution.py:329
  33.7 14.7 %collective-permute-start.12 = (f32[8,96,128]{2,1,0:T(8,128)S(1)}, f32[8,96,128]{2,1,0:T(8,128)S(1)}, u32[]{:S(2)}, u32[]{:S(2)}) collective-permute-start(f32[8,96,128]{2,1,0:T(8,128)S(1)} %get-tuple-element.67.refs_9_), channel_id=1, source_target_pairs={{0,1},{1,2},{2,3},{3,4},{4,5},{5,6},{6,7},{7,8},{8,9},{9,10},{10,1... | collective-permute-start | bytes 1179656 | tf_op jit(solution)/shard_map/ppermute | solution.py:329
  37.4 11.1 %collective-permute-start.13 = (f32[8,96,128]{2,1,0:T(8,128)S(1)}, f32[8,96,128]{2,1,0:T(8,128)S(1)}, u32[]{:S(2)}, u32[]{:S(2)}) collective-permute-start(f32[8,96,128]{2,1,0:T(8,128)S(1)} %get-tuple-element.68.refs_8_), channel_id=1, source_target_pairs={{0,15},{1,0},{2,1},{3,2},{4,3},{5,4},{6,5},{7,6},{8,7},{9,8},{10,9... | collective-permute-start | bytes 1179656 | tf_op jit(solution)/shard_map/ppermute | solution.py:329
  38.1 12.2 %collective-permute-start.17 = (f32[96,8,128]{2,1,0:T(8,128)S(1)}, f32[96,8,128]{2,1,0:T(8,128)S(1)}, u32[]{:S(2)}, u32[]{:S(2)}) collective-permute-start(f32[96,8,128]{2,1,0:T(8,128)S(1)} %shard_map.68.refs_0_), channel_id=1, source_target_pairs={{0,192},{64,0},{128,64},{192,128},{1,193},{65,1},{129,65},{193,129... | collective-permute-start | bytes 1179656 | tf_op jit(solution)/shard_map/ppermute | solution.py:329
  40.8 4.3 %collective-permute-start.14 = (f32[8,8,128]{2,1,0:T(8,128)S(1)}, f32[8,8,128]{2,1,0:T(8,128)S(1)}, u32[]{:S(2)}, u32[]{:S(2)}) collective-permute-start(f32[8,8,128]{2,1,0:T(8,128)S(1)} %get-tuple-element.69), channel_id=1, source_target_pairs={{0,16},{16,32},{32,48},{48,0},{1,17},{17,33},{33,49},{49,1},{2,18}... | collective-permute-start | bytes 98312 | tf_op jit(solution)/shard_map/ppermute | solution.py:329
  48.7 15.9 %collective-permute-start.23 = (f32[96,8,128]{2,1,0:T(8,128)S(1)}, f32[96,8,128]{2,1,0:T(8,128)S(1)}, u32[]{:S(2)}, u32[]{:S(2)}) collective-permute-start(f32[96,8,128]{2,1,0:T(8,128)S(1)} %shard_map.73.refs_0_), channel_id=1, source_target_pairs={{0,192},{64,0},{128,64},{192,128},{1,193},{65,1},{129,65},{193,129... | collective-permute-start | bytes 1179656 | tf_op jit(solution)/shard_map/ppermute | solution.py:329
  50.6 14.0 %collective-permute-start.18 = (f32[8,96,128]{2,1,0:T(8,128)S(1)}, f32[8,96,128]{2,1,0:T(8,128)S(1)}, u32[]{:S(2)}, u32[]{:S(2)}) collective-permute-start(f32[8,96,128]{2,1,0:T(8,128)S(1)} %get-tuple-element.74.refs_9_), channel_id=1, source_target_pairs={{0,1},{1,2},{2,3},{3,4},{4,5},{5,6},{6,7},{7,8},{8,9},{9,10},{10,1... | collective-permute-start | bytes 1179656 | tf_op jit(solution)/shard_map/ppermute | solution.py:329
  51.2 13.4 %collective-permute-start.19 = (f32[8,96,128]{2,1,0:T(8,128)S(1)}, f32[8,96,128]{2,1,0:T(8,128)S(1)}, u32[]{:S(2)}, u32[]{:S(2)}) collective-permute-start(f32[8,96,128]{2,1,0:T(8,128)S(1)} %get-tuple-element.75.refs_8_), channel_id=1, source_target_pairs={{0,15},{1,0},{2,1},{3,2},{4,3},{5,4},{6,5},{7,6},{8,7},{9,8},{10,9... | collective-permute-start | bytes 1179656 | tf_op jit(solution)/shard_map/ppermute | solution.py:329
  55.4 9.3 %collective-permute-start.22 = (f32[96,8,128]{2,1,0:T(8,128)S(1)}, f32[96,8,128]{2,1,0:T(8,128)S(1)}, u32[]{:S(2)}, u32[]{:S(2)}) collective-permute-start(f32[96,8,128]{2,1,0:T(8,128)S(1)} %shard_map.75.refs_2_), channel_id=1, source_target_pairs={{0,64},{64,128},{128,192},{192,0},{1,65},{65,129},{129,193},{193,1... | collective-permute-start | bytes 1179656 | tf_op jit(solution)/shard_map/ppermute | solution.py:329
  55.6 4.3 %collective-permute-start.20 = (f32[8,8,128]{2,1,0:T(8,128)S(1)}, f32[8,8,128]{2,1,0:T(8,128)S(1)}, u32[]{:S(2)}, u32[]{:S(2)}) collective-permute-start(f32[8,8,128]{2,1,0:T(8,128)S(1)} %get-tuple-element.76), channel_id=1, source_target_pairs={{0,16},{16,32},{32,48},{48,0},{1,17},{17,33},{33,49},{49,1},{2,18}... | collective-permute-start | bytes 98312 | tf_op jit(solution)/shard_map/ppermute | solution.py:329
  59.9 4.7 %collective-permute-start.21 = (f32[8,8,128]{2,1,0:T(8,128)S(1)}, f32[8,8,128]{2,1,0:T(8,128)S(1)}, u32[]{:S(2)}, u32[]{:S(2)}) collective-permute-start(f32[8,8,128]{2,1,0:T(8,128)S(1)} %get-tuple-element.77), channel_id=1, source_target_pairs={{0,48},{16,0},{32,16},{48,32},{1,49},{17,1},{33,17},{49,33},{2,50}... | collective-permute-start | bytes 98312 | tf_op jit(solution)/shard_map/ppermute | solution.py:329
  66.0 5.5 %collective-permute-start.24 = (f32[4,96,128]{2,1,0:T(8,128)S(1)}, f32[4,96,128]{2,1,0:T(8,128)S(1)}, u32[]{:S(2)}, u32[]{:S(2)}) collective-permute-start(f32[4,96,128]{2,1,0:T(8,128)S(1)} %get-tuple-element.86), channel_id=1, source_target_pairs={{0,1},{1,0},{2,3},{3,2},{4,5},{5,4},{6,7},{7,6},{8,9},{9,8},{10,11... | collective-permute-start | bytes 589832 | tf_op jit(solution)/shard_map/ppermute | solution.py:329
  98.2 5.8 %collective-permute-start.25 = (f32[4,96,128]{2,1,0:T(8,128)S(1)}, f32[4,96,128]{2,1,0:T(8,128)S(1)}, u32[]{:S(2)}, u32[]{:S(2)}) collective-permute-start(f32[4,96,128]{2,1,0:T(8,128)S(1)} %get-tuple-element.87), channel_id=1, source_target_pairs={{0,1},{1,0},{2,3},{3,2},{4,5},{5,4},{6,7},{7,6},{8,9},{9,8},{10,11... | collective-permute-start | bytes 589832 | tf_op jit(solution)/shard_map/ppermute | solution.py:329
  (6 other events, 43.3 us)
